TPU v7x, 32 devices: a whole 2x2x4 slice. The times are simulated.
32 devices in a mesh: freq: 8 (over z, y), cell: 4 (over x, core).
Axes of the slice: x: 2, y: 2, z: 4, core: 2. Of those that a mesh axis runs over, the one named last changes fastest.
Arguments:
- columns: float32 [2, 16, 64, 600], P(None, 'freq'), may hold values from -6 to 6
- freq_blocks: float32 [2, 16, 600, 1024], P(None, 'freq', None, 'cell'), may hold values from -0.1875 to 0.1875
- causal_cutoffs: int32 [64], replicated, may hold values from 3 to 15
- band_index: int32 [1024], P('cell'), may hold values from 0 to 7
- band_rates: float32 [8], replicated, may hold values from 0.05 to 0.45
Outputs:
- hessian_columns: float32 [2, 16, 64, 600], P(None, 'freq', 'cell')
All inputs are finite; a program needn't handle non-finite values.
Results may differ from a plain program's by a relative error of at most 0.00007.
Values sent between devices are 32-bit elements; how exact they have to be, the bound alone decides.
No kernel may reach another device: no remote copies, remote signals or barrier semaphores. Data moves between devices by JAX's collectives and lax.ppermute only.
A program may use at most 64 MiB of HBM per device.

v0:
```python
import functools
import math

import jax
import jax.numpy as jnp
import numpy as np
from jax import lax
from jax.experimental import pallas as pl
from jax.experimental.pallas import tpu as pltpu
from jax.sharding import PartitionSpec as P


SWEEPS = 4
BANDS = 8
ROWS = 8
LANES = 128
UNROLLED_FREQS = 32
GROUPS = LANES // SWEEPS


VMEM_SPEC = pl.BlockSpec(memory_space=pltpu.VMEM)
SMEM_SPEC = pl.BlockSpec(memory_space=pltpu.SMEM)
HBM_SPEC = pl.BlockSpec(memory_space=pltpu.HBM)


def grant(mib):
    return pltpu.CompilerParams(vmem_limit_bytes=mib * 2**20)


def in_hbm(x):
    return pltpu.with_memory_space_constraint(x, pltpu.HBM)


def split(x):
    high = x.astype(jnp.bfloat16)
    return high, (x - high.astype(jnp.float32)).astype(jnp.bfloat16)


def product(a, b, contract):
    return lax.dot_general(a, b, (contract, ((), ())), preferred_element_type=jnp.float32)


def inverse_table(steps, freqs):
    cycle = 2 * steps
    turns = np.outer(np.arange(steps), np.arange(freqs)) % cycle
    angle = turns * (2.0 * math.pi / cycle)
    weight = np.where((np.arange(freqs) == 0) | (np.arange(freqs) == freqs - 1), 1.0, 2.0) / cycle
    return weight * np.cos(angle), -weight * np.sin(angle)


def forward_table(steps, freqs):
    cycle = 2 * steps
    turns = np.outer(np.arange(freqs), np.arange(steps)) % cycle
    angle = turns * (2.0 * math.pi / cycle)
    return np.cos(angle), -np.sin(angle)


def rates_of(band_ref, rates_ref):
    band = band_ref[...]
    rates = jnp.zeros(band.shape, jnp.float32)
    for b in range(BANDS):
        rates = jnp.where(band == b, rates_ref[b], rates)
    return rates


def adjoint_kernel(
    v_hbm, f_hbm, band_hbm, rates_hbm, cut_hbm, out_hbm, inner_ref, outer_ref, cutoff_ref,
    v_ref, f_ref, band_ref, rates_ref, cut_ref, out_ref, v_sem, f_sem, out_sem, small_sem,
):
    shards, _, held, rows, cells = out_hbm.shape
    cols, sensors = v_ref.shape[2:]
    v_copies, f_copies, out_copies = [], [], []
    for k in range(held):
        v_copies.append(pltpu.make_async_copy(v_hbm.at[:, k], v_ref.at[:, k], v_sem.at[k]))
        v_copies[k].start()
        for c in range(2):
            copy = pltpu.make_async_copy(f_hbm.at[c, k], f_ref.at[c, k], f_sem.at[2 * k + c])
            f_copies.append(copy)
            copy.start()
    small = []
    for at, (source, target) in enumerate(((band_hbm, band_ref), (rates_hbm, rates_ref), (cut_hbm, cut_ref))):
        small.append(pltpu.make_async_copy(source, target, small_sem.at[at]))
        small[at].start()
    odd = lax.axis_index("cell") % 2
    last = cells - LANES
    inner_at, inner_shift = pl.multiple_of((1 - odd) * last, LANES), (1 - odd) * SWEEPS
    outer_at, outer_shift = pl.multiple_of(odd * last, LANES), odd * SWEEPS
    lane_group = lax.broadcasted_iota(jnp.int32, (ROWS, LANES), 1) // SWEEPS

    def edge(at, block):
        for ref, lanes, shift in ((inner_ref, inner_at, inner_shift), (outer_ref, outer_at, outer_shift)):
            for first in range(0, sensors, ROWS * GROUPS):
                packed = jnp.zeros((ROWS, LANES), jnp.float32)
                for group in range(min(GROUPS, (sensors - first) // ROWS)):
                    rows_at = first + group * ROWS
                    cells_there = block[rows_at : rows_at + ROWS, pl.ds(lanes, LANES)]
                    moved = pltpu.roll(cells_there, group * SWEEPS + shift, 1)
                    packed = jnp.where(lane_group == group, moved, packed)
                ref[at, first // GROUPS : first // GROUPS + ROWS] = packed

    for k in range(held):
        for copy in (v_copies[k], f_copies[2 * k], f_copies[2 * k + 1]):
            copy.wait()
        high, low = split(v_ref[:, k].reshape(2 * cols, sensors))
        parts = jnp.concatenate([high, low], axis=0)
        sums = []
        for c in range(2):
            f_high, f_low = split(f_ref[c, k])
            both = product(parts, f_high, ((1,), (0,)))
            both = both[: 2 * cols] + both[2 * cols :] + product(high, f_low, ((1,), (0,)))
            sums.append(both)
        re = sums[0][:cols] + sums[1][cols:]
        im = sums[0][cols:] - sums[1][:cols]
        out_ref[:, 0, k] = re.reshape(shards, rows, cells)
        out_ref[:, 1, k] = im.reshape(shards, rows, cells)
        copy = pltpu.make_async_copy(out_ref.at[:, :, k], out_hbm.at[:, :, k], out_sem.at[k])
        out_copies.append(copy)
        copy.start()
        for c in range(2):
            edge(c * held + k, f_ref.at[c, k])
    for copy in small:
        copy.wait()
    rates = rates_of(band_ref, rates_ref)
    for ref, at in ((inner_ref, 1 - odd), (outer_ref, odd)):
        facing = jnp.where(at == 0, rates[:, :LANES], rates[:, last:])
        ref[2 * held] = jnp.broadcast_to(facing, ref.shape[1:])
    base = lax.axis_index("freq") * rows
    row = lax.broadcasted_iota(jnp.int32, (rows, LANES), 0)
    cutoff = jnp.zeros((rows, LANES), jnp.int32)
    for r in range(rows):
        cutoff = jnp.where(row == r, cut_ref[base + r], cutoff)
    cutoff_ref[...] = cutoff
    for copy in out_copies:
        copy.wait()


def adjoint(columns, blocks, band_index, band_rates, causal_cutoffs, shards):
    _, held, cols, sensors = columns.shape
    cells = blocks.shape[3]
    out = (shards, 2, held, cols // shards, cells)
    packed = -(-sensors // (ROWS * GROUPS)) * ROWS
    edge = jax.ShapeDtypeStruct((2 * held + 1, packed, LANES), jnp.float32)
    return pl.pallas_call(
        adjoint_kernel,
        in_specs=[HBM_SPEC] * 5,
        out_specs=[HBM_SPEC, VMEM_SPEC, VMEM_SPEC, VMEM_SPEC],
        out_shape=[
            pltpu.HBM(out, jnp.float32),
            edge,
            edge,
            jax.ShapeDtypeStruct((cols // shards, LANES), jnp.int32),
        ],
        scratch_shapes=[
            pltpu.VMEM(columns.shape, jnp.float32),
            pltpu.VMEM(blocks.shape, jnp.float32),
            pltpu.VMEM((1, cells), jnp.int32),
            pltpu.SMEM(band_rates.shape, jnp.float32),
            pltpu.SMEM(causal_cutoffs.shape, jnp.int32),
            pltpu.VMEM(out, jnp.float32),
            pltpu.SemaphoreType.DMA((held,)),
            pltpu.SemaphoreType.DMA((2 * held,)),
            pltpu.SemaphoreType.DMA((held,)),
            pltpu.SemaphoreType.DMA((3,)),
        ],
        compiler_params=grant(16),
        cost_estimate=pl.CostEstimate(
            flops=24 * held * cols * sensors * cells, bytes_accessed=8 * held * sensors * cells, transcendentals=0
        ),
        name="adjoint",
    )(columns, blocks, in_hbm(band_index.reshape(1, cells)), in_hbm(band_rates), in_hbm(causal_cutoffs))


def middle_kernel(x_ref, cutoff_ref, out_hbm, out_ref, out_sem):
    shards, _, held, _, cells = x_ref.shape
    freqs = shards * held
    steps = freqs - 1
    half = freqs // 2
    to_cos, to_sin = inverse_table(steps, freqs)
    from_cos, from_sin = forward_table(steps, freqs)
    cutoff = cutoff_ref[...]
    copies = []
    for lane in range(0, cells, LANES):
        at = pl.ds(lane, LANES)
        even, odd = [], []
        for k in range(half):
            a, b = divmod(k, held)
            c, d = divmod(freqs - 1 - k, held)
            re, im = x_ref[a, 0, b, :, at], x_ref[a, 1, b, :, at]
            re2, im2 = x_ref[c, 0, d, :, at], x_ref[c, 1, d, :, at]
            even += [re + re2, im - im2]
            odd += [re - re2, im + im2]
        series = []
        for t in range(steps):
            total = None
            for k in range(half):
                pair = odd if t % 2 else even
                for value, table in ((pair[2 * k], to_cos), (pair[2 * k + 1], to_sin)):
                    term = value * float(table[t, k])
                    total = term if total is None else total + term
            series.append(jnp.where(cutoff > t, total, 0.0))
        for k in range(half):
            a, b = divmod(k, held)
            c, d = divmod(freqs - 1 - k, held)
            sums = []
            for table in (from_cos, from_sin):
                for parity in (0, 1):
                    total = None
                    for t in range(parity, steps, 2):
                        term = series[t] * float(table[k, t])
                        total = term if total is None else total + term
                    sums.append(total)
            out_ref[a, 0, b, :, at] = sums[0] + sums[1]
            out_ref[c, 0, d, :, at] = sums[0] - sums[1]
            out_ref[a, 1, b, :, at] = sums[2] + sums[3]
            out_ref[c, 1, d, :, at] = sums[3] - sums[2]
        source, target = out_ref.at[:, :, :, :, at], out_hbm.at[:, :, :, :, at]
        copy = pltpu.make_async_copy(source, target, out_sem.at[lane // LANES])
        copies.append(copy)
        copy.start()
    for copy in copies:
        copy.wait()


def middle(gathered, cutoff):
    shards, _, held, rows, cells = gathered.shape
    freqs = shards * held
    steps = freqs - 1
    if freqs <= UNROLLED_FREQS and freqs % 2 == 0:
        return pl.pallas_call(
            middle_kernel,
            in_specs=[VMEM_SPEC, VMEM_SPEC],
            out_specs=HBM_SPEC,
            out_shape=pltpu.HBM(gathered.shape, jnp.float32),
            scratch_shapes=[
                pltpu.VMEM(gathered.shape, jnp.float32),
                pltpu.SemaphoreType.DMA((cells // LANES,)),
            ],
            compiler_params=grant(8),
            cost_estimate=pl.CostEstimate(
                flops=8 * freqs * steps * rows * cells, bytes_accessed=16 * freqs * rows * cells, transcendentals=0
            ),
            name="middle",
        )(gathered, cutoff)
    to_time = jnp.asarray(np.concatenate(inverse_table(steps, freqs), axis=1), jnp.float32)
    to_freq = jnp.asarray(np.concatenate(forward_table(steps, freqs), axis=0), jnp.float32)
    x = gathered.transpose(1, 0, 2, 3, 4).reshape(2 * freqs, rows * cells)
    series = jnp.dot(to_time, x, precision=lax.Precision.HIGHEST).reshape(steps, rows, cells)
    moment = lax.broadcasted_iota(jnp.int32, (steps, rows), 0)
    series = jnp.where((moment < cutoff[None, :, 0])[:, :, None], series, 0.0)
    x = jnp.dot(to_freq, series.reshape(steps, rows * cells), precision=lax.Precision.HIGHEST)
    return x.reshape(2, shards, held, rows, cells).transpose(1, 0, 2, 3, 4)


def smooth_kernel(
    f_hbm, inner_ref, outer_ref, band_ref, rates_ref, high_ref, low_ref, f_ref, a_both, a_side, sides, f_sem
):
    _, held, sensors, cells = f_hbm.shape
    width = cells + LANES
    copies = []
    for at in range(2 * held):
        c, k = divmod(at, held)
        copies.append(pltpu.make_async_copy(f_hbm.at[c, k], f_ref.at[c, k], f_sem.at[at]))
        copies[at].start()
    odd = lax.axis_index("cell") % 2
    lane = lax.broadcasted_iota(jnp.int32, (ROWS, LANES), 1)
    after_is_inner = odd == 0

    def beyond(at, group, rows):
        inner, outer = inner_ref[at, rows], outer_ref[at, rows]
        after = jnp.where(after_is_inner, inner, outer)
        before = jnp.where(after_is_inner, outer, inner)
        if group is not None:
            after = pltpu.roll(after, (LANES - group * SWEEPS) % LANES, 1)
            before = pltpu.roll(before, (LANES - (group + 1) * SWEEPS) % LANES, 1)
        cells_there = jnp.where(lane < SWEEPS, after, before)
        return jnp.where((lane < SWEEPS) | (lane >= LANES - SWEEPS), cells_there, 0.0)

    side = beyond(2 * held, None, slice(0, ROWS))[:1]
    rates = jnp.concatenate([rates_of(band_ref, rates_ref), side], axis=1)
    middle = ROWS
    diagonals = jnp.where(lax.broadcasted_iota(jnp.int32, (2 * ROWS, width), 0) == middle, 1.0, 0.0)
    for _ in range(SWEEPS):
        up = pltpu.roll(pltpu.roll(diagonals, 1, 1), 2 * ROWS - 1, 0)
        down = pltpu.roll(pltpu.roll(diagonals, width - 1, 1), 1, 0)
        diagonals = diagonals + rates * (up - 2.0 * diagonals + down)
    for lanes in range(0, width, LANES):
        column = lax.broadcasted_iota(jnp.int32, (LANES, LANES), 1)
        row = lax.broadcasted_iota(jnp.int32, (LANES, LANES), 0)
        for rows in range(0, cells, LANES):
            shift = rows - lanes
            offset = row - column + shift
            if lanes == cells:
                offset = jnp.where(column < LANES // 2, offset, offset + width)
            tile = jnp.zeros((LANES, LANES), jnp.float32)
            for o in range(-SWEEPS, SWEEPS + 1):
                entry = diagonals[middle + o : middle + o + 1, lanes : lanes + LANES]
                tile = jnp.where(offset == o, entry, tile)
            high, low = split(tile)
            if lanes < cells:
                a_both[rows : rows + LANES, lanes : lanes + LANES] = high
                a_both[cells + rows : cells + rows + LANES, lanes : lanes + LANES] = low
            else:
                a_side[rows : rows + LANES] = high
                a_side[cells + rows : cells + rows + LANES] = low
    for at in range(2 * held):
        c, k = divmod(at, held)
        for first in range(0, sensors, ROWS * GROUPS):
            for group in range(min(GROUPS, (sensors - first) // ROWS)):
                rows_at = first + group * ROWS
                packed = slice(first // GROUPS, first // GROUPS + ROWS)
                sides[rows_at : rows_at + ROWS] = beyond(at, group, packed)
        high, low = split(sides[...])
        both = product(a_side[...], high, ((1,), (1,)))
        total = both[:cells] + both[cells:] + product(a_side[:cells], low, ((1,), (1,)))
        copies[at].wait()
        high, low = split(f_ref[c, k])
        both = product(a_both[...], high, ((1,), (1,)))
        total += both[:cells] + both[cells:] + product(a_both[:cells], low, ((1,), (1,)))
        high, low = split(total)
        high_ref[c, k] = high
        low_ref[c, k] = low


def smooth(blocks, inner, outer, band_index, band_rates):
    _, held, sensors, cells = blocks.shape
    shape = jax.ShapeDtypeStruct((2, held, cells, sensors), jnp.bfloat16)
    return pl.pallas_call(
        smooth_kernel,
        in_specs=[HBM_SPEC, VMEM_SPEC, VMEM_SPEC, VMEM_SPEC, SMEM_SPEC],
        out_specs=[VMEM_SPEC] * 2,
        out_shape=[shape, shape],
        scratch_shapes=[
            pltpu.VMEM(blocks.shape, jnp.float32),
            pltpu.VMEM((2 * cells, cells), jnp.bfloat16),
            pltpu.VMEM((2 * cells, LANES), jnp.bfloat16),
            pltpu.VMEM((sensors, LANES), jnp.float32),
            pltpu.SemaphoreType.DMA((2 * held,)),
        ],
        compiler_params=grant(16),
        cost_estimate=pl.CostEstimate(
            flops=12 * held * sensors * cells * cells, bytes_accessed=16 * held * sensors * cells, transcendentals=0
        ),
        name="smooth",
    )(blocks, inner, outer, band_index.reshape(1, cells), band_rates)


def forward_kernel(steps, chips, wanted, x_ref, high_ref, low_ref, away_ref, home_ref):
    share, sensors = home_ref.shape[3:]
    per = share // ROWS
    cell = lax.axis_index("cell")
    chip, core = cell // 2, cell % 2
    cells = x_ref.shape[4]
    order = []
    for side in (1 - core, core):
        for s in steps:
            order.append((2 * lax.rem(chip + s, chips) + side) * per)
    rows = len(order) * share
    for at, k in enumerate(wanted):
        parts = []
        for c in range(2):
            for first in order:
                parts.append(x_ref[pl.ds(first, per), c, k].reshape(share, cells))
        high, low = split(jnp.concatenate(parts, axis=0))
        both = jnp.concatenate([high, low], axis=0)
        terms = []
        for c in range(2):
            wide = product(both, high_ref[c, k], ((1,), (0,)))
            terms.append(wide[: 2 * rows] + wide[2 * rows :] + product(high, low_ref[c, k], ((1,), (0,))))
        re = (terms[0][:rows] - terms[1][rows:]).reshape(2, len(steps), share, sensors)
        im = (terms[0][rows:] + terms[1][:rows]).reshape(2, len(steps), share, sensors)
        for side, ref in enumerate((away_ref, home_ref)):
            ref[:, 0, at] = re[side]
            ref[:, 1, at] = im[side]


def forward(returned, high, low, steps, chips, wanted):
    shards, _, _, rows, cells = returned.shape
    sensors = high.shape[3]
    share = shards * rows // (2 * chips)
    shape = jax.ShapeDtypeStruct((len(steps), 2, len(wanted), share, sensors), jnp.float32)
    return pl.pallas_call(
        functools.partial(forward_kernel, steps, chips, wanted),
        in_specs=[VMEM_SPEC] * 3,
        out_specs=[VMEM_SPEC] * 2,
        out_shape=[shape, shape],
        compiler_params=grant(16),
        cost_estimate=pl.CostEstimate(
            flops=48 * len(steps) * len(wanted) * share * sensors * cells,
            bytes_accessed=8 * len(wanted) * sensors * cells,
            transcendentals=0,
        ),
    )(returned, high, low)


def total_kernel(home_ref, away_ref, *refs):
    out_ref = refs[-1]
    held = out_ref.shape[1]
    for k in range(held):
        total = home_ref[0, :, k] + away_ref[0, :, k]
        for ref in refs[k:-1:held]:
            total += ref[:, 0]
        out_ref[:, k] = total


def on_device(columns, freq_blocks, causal_cutoffs, band_index, band_rates):
    shards, strips = lax.axis_size("freq"), lax.axis_size("cell")
    chips = strips // 2
    held = columns.shape[1]
    columns, blocks = in_hbm(columns), in_hbm(freq_blocks)
    spectrum, inner, outer, cutoff = adjoint(columns, blocks, band_index, band_rates, causal_cutoffs, shards)
    gathered = lax.all_to_all(spectrum, "freq", split_axis=0, concat_axis=0, tiled=True)
    inner = lax.ppermute(inner, "cell", [(i, i ^ 1) for i in range(strips)])
    pairs = [(i, i + 1) for i in range(1, strips - 1, 2)]
    outer = lax.ppermute(outer, "cell", pairs + [(j, i) for i, j in pairs])
    gathered, inner, outer = lax.optimization_barrier((gathered, inner, outer))
    spectrum = middle(gathered, cutoff)
    high, low = smooth(blocks, inner, outer, band_index, band_rates)
    returned = lax.all_to_all(spectrum, "freq", split_axis=0, concat_axis=0, tiled=True)
    swap = [(i, i ^ 1) for i in range(strips)]
    leaving = []
    if chips > 1:
        for k in range(held):
            away, home = forward(returned, high, low, range(1, chips), chips, (k,))
            leaving.append(home + lax.ppermute(away, "cell", swap))
    arrived = []
    for s in range(1, chips):
        pairs = [(i, 2 * ((i // 2 + s) % chips) + i % 2) for i in range(strips)]
        for k in range(held):
            arrived.append(lax.ppermute(leaving[k][s - 1], "cell", pairs))
    away, home = forward(returned, high, low, range(1), chips, range(held))
    away = lax.ppermute(away, "cell", swap)
    share, sensors = home.shape[3:]
    return pl.pallas_call(
        total_kernel,
        in_specs=[VMEM_SPEC] * (2 + len(arrived)),
        out_specs=VMEM_SPEC,
        out_shape=jax.ShapeDtypeStruct((2, held, share, sensors), jnp.float32),
        compiler_params=grant(16),
        name="total",
    )(home, away, *arrived)


def solution(mesh):
    placed = (P(None, "freq", None, None), P(None, "freq", None, "cell"), P(), P("cell"), P())
    return jax.shard_map(
        on_device,
        mesh=mesh,
        in_specs=placed,
        out_specs=P(None, "freq", "cell", None),
        check_vma=False,
    )
```

profile of v0, /device:TPU:0, one launch (start us, length us, event | category | flops | bytes accessed | tf_op | source)
XLA Modules:
  0.0 42.7 jit_solution(15321444599985210591)
XLA Ops:
  0.0 3.7 %adjoint.1 = (f32[8,2,2,8,256]{4,3,2,1,0:T(8,128)}, f32[5,24,128]{2,1,0:T(8,128)S(1)}, f32[5,24,128]{2,1,0:T(8,128)S(1)}, s32[8,128]{1,0:T(8,128)S(1)}) custom-call(f32[2,2,64,600]{3,2,1,0:T(8,128)} %v_hbm.1, f32[2,2,600,256]{3,2,1,0:T(8,128)} %f_hbm.3, s32[1,256]{1,0:T(1,128)} %bitcast.15, f32[8]{0:T(128)} %rates_ref.1, s32[64]{0:T(128)} %cut_hbm.1), custom_call_target="tpu_custom_call" | custom-call | flops 471859200 | bytes 2457600 | tf_op jit(solution)/shard_map/adjoint/pallas_call | solution.py:143
  3.7 0.0 copy-start
  3.7 0.0 copy-start.1
  3.7 7.3 %all-to-all-start = ((f32[8,2,2,8,256]{4,3,2,1,0:T(8,128)}), f32[8,2,2,8,256]{4,3,2,1,0:T(8,128)S(1)}, u32[]{:S(2)}, u32[]{:S(2)}) async-start(f32[8,2,2,8,256]{4,3,2,1,0:T(8,128)} %get-tuple-element.20), calls=%async_computation | async-start | bytes 524288 | tf_op jit(solution)/shard_map/all_to_all | solution.py:411
  11.0 0.0 collective-permute-start
  11.0 0.7 %collective-permute-start.1 = (f32[5,24,128]{2,1,0:T(8,128)S(1)}, f32[5,24,128]{2,1,0:T(8,128)S(1)}, u32[]{:S(2)}, u32[]{:S(2)}) collective-permute-start(f32[5,24,128]{2,1,0:T(8,128)S(1)} %get-tuple-element.22), channel_id=1, source_target_pairs={{1,2},{2,1},{5,6},{6,5},{9,10},{10,9},{13,14},{14,13},{17,18},{18,... | collective-permute-start | bytes 184328 | tf_op jit(solution)/shard_map/ppermute | solution.py:414
  11.7 0.6 %collective-permute-done.inner_ref = f32[5,24,128]{2,1,0:T(8,128)S(1)} collective-permute-done((f32[5,24,128]{2,1,0:T(8,128)S(1)}, f32[5,24,128]{2,1,0:T(8,128)S(1)}, u32[]{:S(2)}, u32[]{:S(2)}) %collective-permute-start) | collective-permute-done | bytes 61472 | tf_op jit(solution)/shard_map/ppermute | solution.py:412
  12.3 7.7 %all-to-all-done.x_ref = f32[8,2,2,8,256]{4,3,2,1,0:T(8,128)S(1)} async-done(((f32[8,2,2,8,256]{4,3,2,1,0:T(8,128)}), f32[8,2,2,8,256]{4,3,2,1,0:T(8,128)S(1)}, u32[]{:S(2)}, u32[]{:S(2)}) %all-to-all-start) | async-done | bytes 262176 | tf_op jit(solution)/shard_map/all_to_all | solution.py:411
  19.9 0.9 %middle.1 = f32[8,2,2,8,256]{4,3,2,1,0:T(8,128)} custom-call(f32[8,2,2,8,256]{4,3,2,1,0:T(8,128)S(1)} %all-to-all-done.x_ref, s32[8,128]{1,0:T(8,128)S(1)} %get-tuple-element.24.cutoff_ref), custom_call_target="tpu_custom_call" | custom-call | flops 3932160 | bytes 524288 | tf_op jit(solution)/shard_map/middle/pallas_call | solution.py:229
  20.9 3.6 %all-to-all-start.1 = ((f32[8,2,2,8,256]{4,3,2,1,0:T(8,128)}), f32[8,2,2,8,256]{4,3,2,1,0:T(8,128)S(1)}, u32[]{:S(2)}, u32[]{:S(2)}) async-start(f32[8,2,2,8,256]{4,3,2,1,0:T(8,128)} %middle.1), calls=%async_computation.1 | async-start | bytes 524288 | tf_op jit(solution)/shard_map/all_to_all | solution.py:418
  24.5 4.8 %smooth.1 = (bf16[2,2,256,600]{3,2,1,0:T(8,128)(2,1)S(1)}, bf16[2,2,256,600]{3,2,1,0:T(8,128)(2,1)S(1)}) custom-call(f32[2,2,600,256]{3,2,1,0:T(8,128)} %f_hbm.3, f32[5,24,128]{2,1,0:T(8,128)S(1)} %collective-permute-done.inner_ref, f32[5,24,128]{2,1,0:T(8,128)S(1)} %collective-permute-done.1.outer_ref, s32[1,256]{1,0:T(1,128)S(1)} %bitcast.16, f32[8]{0:T(128)S(1)} %copy-done.1), custom_call_target="tpu_custom_call" | custom-call | flops 943718400 | bytes 4915200 | tf_op jit(solution)/shard_map/smooth/pallas_call | solution.py:327
  29.3 4.1 %all-to-all-done.1.x_ref = f32[8,2,2,8,256]{4,3,2,1,0:T(8,128)S(1)} async-done(((f32[8,2,2,8,256]{4,3,2,1,0:T(8,128)}), f32[8,2,2,8,256]{4,3,2,1,0:T(8,128)S(1)}, u32[]{:S(2)}, u32[]{:S(2)}) %all-to-all-start.1) | async-done | bytes 262176 | tf_op jit(solution)/shard_map/all_to_all | solution.py:418
  33.4 0.3 shard_map.57
  33.7 0.1 collective-permute-start.5
  33.8 0.3 shard_map.56
  34.2 0.6 %collective-permute-start.3 = (f32[1,2,1,16,600]{4,3,1,2,0:T(8,128)S(1)}, f32[1,2,1,16,600]{4,3,1,2,0:T(8,128)S(1)}, u32[]{:S(2)}, u32[]{:S(2)}) collective-permute-start(f32[1,2,1,16,600]{4,3,1,2,0:T(8,128)S(1)} %bitcast.17), channel_id=1, source_target_pairs={{0,1},{1,0},{2,3},{3,2},{4,5},{5,4},{6,7},{7,6},{8,9},{9,8},{10,11... | collective-permute-start | bytes 230408 | tf_op jit(solution)/shard_map/ppermute | solution.py:424
  34.7 0.6 %shard_map.55 = (f32[1,2,2,16,600]{4,3,2,1,0:T(8,128)S(1)}, f32[1,2,2,16,600]{4,3,2,1,0:T(8,128)S(1)}) custom-call(f32[8,2,2,8,256]{4,3,2,1,0:T(8,128)S(1)} %all-to-all-done.1.x_ref, bf16[2,2,256,600]{3,2,1,0:T(8,128)(2,1)S(1)} %get-tuple-element.27.high_ref, bf16[2,2,256,600]{3,2,1,0:T(8,128)(2,1)S(1)} %get-tuple-element.28.low_ref), custom_call_target="tpu_custom_call" | custom-call | flops 235929600 | bytes 2457600 | tf_op jit(solution)/shard_map/pallas_call | solution.py:381
  35.3 0.1 collective-permute-start.2
  35.4 0.0 collective-permute-done.5
  35.4 1.2 %collective-permute-start.6 = (f32[2,1,16,600]{3,2,1,0:T(8,128)S(1)}, f32[2,1,16,600]{3,2,1,0:T(8,128)S(1)}, u32[]{:S(2)}, u32[]{:S(2)}) collective-permute-start(f32[2,1,16,600]{3,2,1,0:T(8,128)S(1)} %fusion), channel_id=1, source_target_pairs={{0,2},{1,3},{2,0},{3,1},{4,6},{5,7},{6,4},{7,5},{8,10},{9,11},{10,... | collective-permute-start | bytes 230408 | tf_op jit(solution)/shard_map/ppermute | solution.py:429
  36.6 0.9 %collective-permute-start.4 = (f32[2,1,16,600]{3,2,1,0:T(8,128)S(1)}, f32[2,1,16,600]{3,2,1,0:T(8,128)S(1)}, u32[]{:S(2)}, u32[]{:S(2)}) collective-permute-start(f32[2,1,16,600]{3,2,1,0:T(8,128)S(1)} %fusion.1), channel_id=1, source_target_pairs={{0,2},{1,3},{2,0},{3,1},{4,6},{5,7},{6,4},{7,5},{8,10},{9,11},{10,... | collective-permute-start | bytes 230408 | tf_op jit(solution)/shard_map/ppermute | solution.py:429
  37.6 3.2 %collective-permute-done.6.refs_1_ = f32[2,1,16,600]{3,2,1,0:T(8,128)S(1)} collective-permute-done((f32[2,1,16,600]{3,2,1,0:T(8,128)S(1)}, f32[2,1,16,600]{3,2,1,0:T(8,128)S(1)}, u32[]{:S(2)}, u32[]{:S(2)}) %collective-permute-start.6) | collective-permute-done | bytes 76832 | tf_op jit(solution)/shard_map/ppermute | solution.py:429
  40.8 1.3 %collective-permute-done.4.refs_0_ = f32[2,1,16,600]{3,2,1,0:T(8,128)S(1)} collective-permute-done((f32[2,1,16,600]{3,2,1,0:T(8,128)S(1)}, f32[2,1,16,600]{3,2,1,0:T(8,128)S(1)}, u32[]{:S(2)}, u32[]{:S(2)}) %collective-permute-start.4) | collective-permute-done | bytes 76832 | tf_op jit(solution)/shard_map/ppermute | solution.py:429
  42.0 0.7 %total.1 = f32[2,2,16,600]{3,2,1,0:T(8,128)} custom-call(f32[1,2,2,16,600]{4,3,2,1,0:T(8,128)S(1)} %get-tuple-element.29.home_ref, f32[1,2,2,16,600]{4,3,2,1,0:T(8,128)S(1)} %collective-permute-done.2.away_ref, f32[2,1,16,600]{3,2,1,0:T(8,128)S(1)} %collective-permute-done.4.refs_0_, f32[2,1,16,600]{3,2,1,0:T(8,128)S(1)} %collective-permute-done.6.refs_1_), custom_call_target="tpu_custom_call" | custom-call | tf_op jit(solution)/shard_map/total/pallas_call | solution.py:433
  (7 shorter events, 0.0 us)
Async XLA Ops:
  3.7 20.8 %copy-start = (s32[256]{0:T(256)S(1)}, s32[256]{0:T(256)}, u32[]{:S(2)}) copy-start(s32[256]{0:T(256)} %param.8) | copy-start | bytes 3076
  3.7 20.8 %copy-start.1 = (f32[8]{0:T(128)S(1)}, f32[8]{0:T(128)}, u32[]{:S(2)}) copy-start(f32[8]{0:T(128)} %rates_ref.1) | copy-start | bytes 100
  3.7 16.2 %all-to-all-start = ((f32[8,2,2,8,256]{4,3,2,1,0:T(8,128)}), f32[8,2,2,8,256]{4,3,2,1,0:T(8,128)S(1)}, u32[]{:S(2)}, u32[]{:S(2)}) async-start(f32[8,2,2,8,256]{4,3,2,1,0:T(8,128)} %get-tuple-element.20), calls=%async_computation | async-start | bytes 524288 | tf_op jit(solution)/shard_map/all_to_all | solution.py:411
  11.0 1.2 %collective-permute-start = (f32[5,24,128]{2,1,0:T(8,128)S(1)}, f32[5,24,128]{2,1,0:T(8,128)S(1)}, u32[]{:S(2)}, u32[]{:S(2)}) collective-permute-start(f32[5,24,128]{2,1,0:T(8,128)S(1)} %get-tuple-element.21), channel_id=1, source_target_pairs={{0,1},{1,0},{2,3},{3,2},{4,5},{5,4},{6,7},{7,6},{8,9},{9,8},{10,11... | collective-permute-start | bytes 184328 | tf_op jit(solution)/shard_map/ppermute | solution.py:412
  11.0 1.2 %collective-permute-start.1 = (f32[5,24,128]{2,1,0:T(8,128)S(1)}, f32[5,24,128]{2,1,0:T(8,128)S(1)}, u32[]{:S(2)}, u32[]{:S(2)}) collective-permute-start(f32[5,24,128]{2,1,0:T(8,128)S(1)} %get-tuple-element.22), channel_id=1, source_target_pairs={{1,2},{2,1},{5,6},{6,5},{9,10},{10,9},{13,14},{14,13},{17,18},{18,... | collective-permute-start | bytes 184328 | tf_op jit(solution)/shard_map/ppermute | solution.py:414
  20.9 12.5 %all-to-all-start.1 = ((f32[8,2,2,8,256]{4,3,2,1,0:T(8,128)}), f32[8,2,2,8,256]{4,3,2,1,0:T(8,128)S(1)}, u32[]{:S(2)}, u32[]{:S(2)}) async-start(f32[8,2,2,8,256]{4,3,2,1,0:T(8,128)} %middle.1), calls=%async_computation.1 | async-start | bytes 524288 | tf_op jit(solution)/shard_map/all_to_all | solution.py:418
  33.7 1.6 %collective-permute-start.5 = (f32[1,2,1,16,600]{4,3,1,2,0:T(8,128)S(1)}, f32[1,2,1,16,600]{4,3,1,2,0:T(8,128)S(1)}, u32[]{:S(2)}, u32[]{:S(2)}) collective-permute-start(f32[1,2,1,16,600]{4,3,1,2,0:T(8,128)S(1)} %bitcast.18), channel_id=1, source_target_pairs={{0,1},{1,0},{2,3},{3,2},{4,5},{5,4},{6,7},{7,6},{8,9},{9,8},{10,11... | collective-permute-start | bytes 230408 | tf_op jit(solution)/shard_map/ppermute | solution.py:424
  34.2 2.5 %collective-permute-start.3 = (f32[1,2,1,16,600]{4,3,1,2,0:T(8,128)S(1)}, f32[1,2,1,16,600]{4,3,1,2,0:T(8,128)S(1)}, u32[]{:S(2)}, u32[]{:S(2)}) collective-permute-start(f32[1,2,1,16,600]{4,3,1,2,0:T(8,128)S(1)} %bitcast.17), channel_id=1, source_target_pairs={{0,1},{1,0},{2,3},{3,2},{4,5},{5,4},{6,7},{7,6},{8,9},{9,8},{10,11... | collective-permute-start | bytes 230408 | tf_op jit(solution)/shard_map/ppermute | solution.py:424
  35.3 6.8 %collective-permute-start.2 = (f32[1,2,2,16,600]{4,3,2,1,0:T(8,128)S(1)}, f32[1,2,2,16,600]{4,3,2,1,0:T(8,128)S(1)}, u32[]{:S(2)}, u32[]{:S(2)}) collective-permute-start(f32[1,2,2,16,600]{4,3,2,1,0:T(8,128)S(1)} %get-tuple-element.30), channel_id=1, source_target_pairs={{0,1},{1,0},{2,3},{3,2},{4,5},{5,4},{6,7},{7,6},{8,9},{9,8},{10,11... | collective-permute-start | bytes 460808 | tf_op jit(solution)/shard_map/ppermute | solution.py:431
  35.4 5.4 %collective-permute-start.6 = (f32[2,1,16,600]{3,2,1,0:T(8,128)S(1)}, f32[2,1,16,600]{3,2,1,0:T(8,128)S(1)}, u32[]{:S(2)}, u32[]{:S(2)}) collective-permute-start(f32[2,1,16,600]{3,2,1,0:T(8,128)S(1)} %fusion), channel_id=1, source_target_pairs={{0,2},{1,3},{2,0},{3,1},{4,6},{5,7},{6,4},{7,5},{8,10},{9,11},{10,... | collective-permute-start | bytes 230408 | tf_op jit(solution)/shard_map/ppermute | solution.py:429
  36.6 5.4 %collective-permute-start.4 = (f32[2,1,16,600]{3,2,1,0:T(8,128)S(1)}, f32[2,1,16,600]{3,2,1,0:T(8,128)S(1)}, u32[]{:S(2)}, u32[]{:S(2)}) collective-permute-start(f32[2,1,16,600]{3,2,1,0:T(8,128)S(1)} %fusion.1), channel_id=1, source_target_pairs={{0,2},{1,3},{2,0},{3,1},{4,6},{5,7},{6,4},{7,5},{8,10},{9,11},{10,... | collective-permute-start | bytes 230408 | tf_op jit(solution)/shard_map/ppermute | solution.py:429
where the time goes:
time: 43.1 us; the launch traced here: 42.7 us
  waiting for transfers between devices  16.8 us (39%)
  starting transfers between devices  14.5 us (34%)
  Pallas kernels  11.3 us (26%)
    all_to_all x2, waiting for transfers between devices, on_device(): lax.all_to_all(spectrum, 'freq', split_axis=0, concat_axis=0, tiled=True)  11.8 us
    all_to_all x2, starting transfers between devices, on_device(): lax.all_to_all(spectrum, 'freq', split_axis=0, concat_axis=0, tiled=True)  10.9 us
    pallas_call x1, Pallas kernels, smooth(): pl.pallas_call(smooth_kernel, in_specs=[HBM_SPEC, VMEM_SPEC, VMEM_SPEC, V...  4.79 us
    ppermute x2, waiting for transfers between devices, on_device(): arrived.append(lax.ppermute(leaving[k][s - 1], 'cell', pairs))  4.48 us
    pallas_call x1, Pallas kernels, adjoint(): pl.pallas_call(adjoint_kernel, in_specs=[HBM_SPEC] * 5, out_specs=[HBM_SP...  3.66 us
    ppermute x2, starting transfers between devices, on_device(): arrived.append(lax.ppermute(leaving[k][s - 1], 'cell', pairs))  2.16 us
    pallas_call x3, Pallas kernels, forward(): pl.pallas_call(functools.partial(forward_kernel, steps, chips, wanted), i...  1.24 us
    pallas_call x1, Pallas kernels, middle(): pl.pallas_call(middle_kernel, in_specs=[VMEM_SPEC, VMEM_SPEC], out_specs=...  0.92 us
  transfers between devices with their start and end apart: 9, of which 5 were waited for; matrix products, arithmetic and copies ran while one was open for 0% of the time, Pallas kernels for 13%

commit v1 on v0

--- a/solution.py
+++ b/solution.py
@@ -16,6 +16,7 @@
 LANES = 128
 UNROLLED_FREQS = 32
 GROUPS = LANES // SWEEPS
+NEAR = 2 * ROWS
 
 
 VMEM_SPEC = pl.BlockSpec(memory_space=pltpu.VMEM)
@@ -64,12 +65,12 @@
 
 
 def adjoint_kernel(
-    v_hbm, f_hbm, band_hbm, rates_hbm, cut_hbm, out_hbm, inner_ref, outer_ref, cutoff_ref,
-    v_ref, f_ref, band_ref, rates_ref, cut_ref, out_ref, v_sem, f_sem, out_sem, small_sem,
+    v_hbm, f_hbm, band_hbm, rates_hbm, cut_hbm, out_ref, inner_ref, outer_ref, cutoff_ref,
+    v_ref, f_ref, band_ref, rates_ref, cut_ref, v_sem, f_sem, small_sem,
 ):
-    shards, _, held, rows, cells = out_hbm.shape
+    shards, _, held, rows, cells = out_ref.shape
     cols, sensors = v_ref.shape[2:]
-    v_copies, f_copies, out_copies = [], [], []
+    v_copies, f_copies = [], []
     for k in range(held):
         v_copies.append(pltpu.make_async_copy(v_hbm.at[:, k], v_ref.at[:, k], v_sem.at[k]))
         v_copies[k].start()
@@ -113,9 +114,6 @@
         im = sums[0][cols:] - sums[1][:cols]
         out_ref[:, 0, k] = re.reshape(shards, rows, cells)
         out_ref[:, 1, k] = im.reshape(shards, rows, cells)
-        copy = pltpu.make_async_copy(out_ref.at[:, :, k], out_hbm.at[:, :, k], out_sem.at[k])
-        out_copies.append(copy)
-        copy.start()
         for c in range(2):
             edge(c * held + k, f_ref.at[c, k])
     for copy in small:
@@ -130,8 +128,6 @@
     for r in range(rows):
         cutoff = jnp.where(row == r, cut_ref[base + r], cutoff)
     cutoff_ref[...] = cutoff
-    for copy in out_copies:
-        copy.wait()
 
 
 def adjoint(columns, blocks, band_index, band_rates, causal_cutoffs, shards):
@@ -143,9 +139,9 @@
     return pl.pallas_call(
         adjoint_kernel,
         in_specs=[HBM_SPEC] * 5,
-        out_specs=[HBM_SPEC, VMEM_SPEC, VMEM_SPEC, VMEM_SPEC],
+        out_specs=[VMEM_SPEC] * 4,
         out_shape=[
-            pltpu.HBM(out, jnp.float32),
+            jax.ShapeDtypeStruct(out, jnp.float32),
             edge,
             edge,
             jax.ShapeDtypeStruct((cols // shards, LANES), jnp.int32),
@@ -156,10 +152,8 @@
             pltpu.VMEM((1, cells), jnp.int32),
             pltpu.SMEM(band_rates.shape, jnp.float32),
             pltpu.SMEM(causal_cutoffs.shape, jnp.int32),
-            pltpu.VMEM(out, jnp.float32),
             pltpu.SemaphoreType.DMA((held,)),
             pltpu.SemaphoreType.DMA((2 * held,)),
-            pltpu.SemaphoreType.DMA((held,)),
             pltpu.SemaphoreType.DMA((3,)),
         ],
         compiler_params=grant(16),
@@ -251,89 +245,62 @@
     return x.reshape(2, shards, held, rows, cells).transpose(1, 0, 2, 3, 4)
 
 
-def smooth_kernel(
-    f_hbm, inner_ref, outer_ref, band_ref, rates_ref, high_ref, low_ref, f_ref, a_both, a_side, sides, f_sem
-):
-    _, held, sensors, cells = f_hbm.shape
-    width = cells + LANES
+def diagonals_of(rates):
+    width = rates.shape[1]
+    diagonals = jnp.where(lax.broadcasted_iota(jnp.int32, (2 * ROWS, width), 0) == ROWS, 1.0, 0.0)
+    for _ in range(SWEEPS):
+        up = pltpu.roll(pltpu.roll(diagonals, 1, 1), 2 * ROWS - 1, 0)
+        down = pltpu.roll(pltpu.roll(diagonals, width - 1, 1), 1, 0)
+        diagonals = diagonals + rates * (up - 2.0 * diagonals + down)
+    return diagonals
+
+
+def spread(diagonals, offset):
+    tile = jnp.zeros(offset.shape, jnp.float32)
+    for o in range(-SWEEPS, SWEEPS + 1):
+        tile = jnp.where(offset == o, diagonals[ROWS + o : ROWS + o + 1], tile)
+    return tile
+
+
+def smooth_kernel(f_hbm, band_ref, rates_ref, high_ref, low_ref, near_ref, f_ref, a_both, f_sem):
+    _, held, _, cells = f_hbm.shape
     copies = []
     for at in range(2 * held):
         c, k = divmod(at, held)
         copies.append(pltpu.make_async_copy(f_hbm.at[c, k], f_ref.at[c, k], f_sem.at[at]))
         copies[at].start()
-    odd = lax.axis_index("cell") % 2
-    lane = lax.broadcasted_iota(jnp.int32, (ROWS, LANES), 1)
-    after_is_inner = odd == 0
-
-    def beyond(at, group, rows):
-        inner, outer = inner_ref[at, rows], outer_ref[at, rows]
-        after = jnp.where(after_is_inner, inner, outer)
-        before = jnp.where(after_is_inner, outer, inner)
-        if group is not None:
-            after = pltpu.roll(after, (LANES - group * SWEEPS) % LANES, 1)
-            before = pltpu.roll(before, (LANES - (group + 1) * SWEEPS) % LANES, 1)
-        cells_there = jnp.where(lane < SWEEPS, after, before)
-        return jnp.where((lane < SWEEPS) | (lane >= LANES - SWEEPS), cells_there, 0.0)
-
-    side = beyond(2 * held, None, slice(0, ROWS))[:1]
-    rates = jnp.concatenate([rates_of(band_ref, rates_ref), side], axis=1)
-    middle = ROWS
-    diagonals = jnp.where(lax.broadcasted_iota(jnp.int32, (2 * ROWS, width), 0) == middle, 1.0, 0.0)
-    for _ in range(SWEEPS):
-        up = pltpu.roll(pltpu.roll(diagonals, 1, 1), 2 * ROWS - 1, 0)
-        down = pltpu.roll(pltpu.roll(diagonals, width - 1, 1), 1, 0)
-        diagonals = diagonals + rates * (up - 2.0 * diagonals + down)
-    for lanes in range(0, width, LANES):
+    diagonals = diagonals_of(jnp.concatenate([rates_of(band_ref, rates_ref), jnp.zeros((1, LANES), jnp.float32)], axis=1))
+    for lanes in range(0, cells, LANES):
         column = lax.broadcasted_iota(jnp.int32, (LANES, LANES), 1)
         row = lax.broadcasted_iota(jnp.int32, (LANES, LANES), 0)
         for rows in range(0, cells, LANES):
-            shift = rows - lanes
-            offset = row - column + shift
-            if lanes == cells:
-                offset = jnp.where(column < LANES // 2, offset, offset + width)
-            tile = jnp.zeros((LANES, LANES), jnp.float32)
-            for o in range(-SWEEPS, SWEEPS + 1):
-                entry = diagonals[middle + o : middle + o + 1, lanes : lanes + LANES]
-                tile = jnp.where(offset == o, entry, tile)
-            high, low = split(tile)
-            if lanes < cells:
-                a_both[rows : rows + LANES, lanes : lanes + LANES] = high
-                a_both[cells + rows : cells + rows + LANES, lanes : lanes + LANES] = low
-            else:
-                a_side[rows : rows + LANES] = high
-                a_side[cells + rows : cells + rows + LANES] = low
+            high, low = split(spread(diagonals[:, lanes : lanes + LANES], row - column + (rows - lanes)))
+            a_both[rows : rows + LANES, lanes : lanes + LANES] = high
+            a_both[cells + rows : cells + rows + LANES, lanes : lanes + LANES] = low
     for at in range(2 * held):
         c, k = divmod(at, held)
-        for first in range(0, sensors, ROWS * GROUPS):
-            for group in range(min(GROUPS, (sensors - first) // ROWS)):
-                rows_at = first + group * ROWS
-                packed = slice(first // GROUPS, first // GROUPS + ROWS)
-                sides[rows_at : rows_at + ROWS] = beyond(at, group, packed)
-        high, low = split(sides[...])
-        both = product(a_side[...], high, ((1,), (1,)))
-        total = both[:cells] + both[cells:] + product(a_side[:cells], low, ((1,), (1,)))
         copies[at].wait()
         high, low = split(f_ref[c, k])
         both = product(a_both[...], high, ((1,), (1,)))
-        total += both[:cells] + both[cells:] + product(a_both[:cells], low, ((1,), (1,)))
+        total = both[:cells] + both[cells:] + product(a_both[:cells], low, ((1,), (1,)))
         high, low = split(total)
         high_ref[c, k] = high
         low_ref[c, k] = low
-
-
-def smooth(blocks, inner, outer, band_index, band_rates):
+        near_ref[c, k, :NEAR] = total[:NEAR]
+        near_ref[c, k, NEAR:] = total[cells - NEAR :]
+
+
+def smooth(blocks, band_index, band_rates):
     _, held, sensors, cells = blocks.shape
     shape = jax.ShapeDtypeStruct((2, held, cells, sensors), jnp.bfloat16)
     return pl.pallas_call(
         smooth_kernel,
-        in_specs=[HBM_SPEC, VMEM_SPEC, VMEM_SPEC, VMEM_SPEC, SMEM_SPEC],
-        out_specs=[VMEM_SPEC] * 2,
-        out_shape=[shape, shape],
+        in_specs=[HBM_SPEC, VMEM_SPEC, SMEM_SPEC],
+        out_specs=[VMEM_SPEC] * 3,
+        out_shape=[shape, shape, jax.ShapeDtypeStruct((2, held, 2 * NEAR, sensors), jnp.float32)],
         scratch_shapes=[
             pltpu.VMEM(blocks.shape, jnp.float32),
             pltpu.VMEM((2 * cells, cells), jnp.bfloat16),
-            pltpu.VMEM((2 * cells, LANES), jnp.bfloat16),
-            pltpu.VMEM((sensors, LANES), jnp.float32),
             pltpu.SemaphoreType.DMA((2 * held,)),
         ],
         compiler_params=grant(16),
@@ -341,10 +308,89 @@
             flops=12 * held * sensors * cells * cells, bytes_accessed=16 * held * sensors * cells, transcendentals=0
         ),
         name="smooth",
-    )(blocks, inner, outer, band_index.reshape(1, cells), band_rates)
-
-
-def forward_kernel(steps, chips, wanted, x_ref, high_ref, low_ref, away_ref, home_ref):
+    )(blocks, band_index.reshape(1, cells), band_rates)
+
+
+def near_kernel(
+    near_ref, own_inner_ref, own_outer_ref, inner_ref, outer_ref, band_ref, rates_ref, high_ref, low_ref, sides
+):
+    held = near_ref.shape[1]
+    sensors = near_ref.shape[3]
+    cells = band_ref.shape[1]
+    even = lax.axis_index("cell") % 2 == 0
+    lane = lax.broadcasted_iota(jnp.int32, (ROWS, LANES), 1)
+    middle = LANES // 2
+    spots = (0, middle - SWEEPS, middle, LANES - SWEEPS)
+
+    def parts(at, rows):
+        own_inner, own_outer = own_inner_ref[at, rows], own_outer_ref[at, rows]
+        inner, outer = inner_ref[at, rows], outer_ref[at, rows]
+        return (
+            jnp.where(even, own_outer, own_inner),
+            jnp.where(even, own_inner, own_outer),
+            jnp.where(even, inner, outer),
+            jnp.where(even, outer, inner),
+        )
+
+    _, _, after, before = parts(2 * held, slice(0, ROWS))
+    side = jnp.where(lane < SWEEPS, after, jnp.where(lane >= LANES - SWEEPS, before, 0.0))[:1]
+    own = rates_of(band_ref, rates_ref)
+    alone = diagonals_of(jnp.concatenate([own, jnp.zeros((1, LANES), jnp.float32)], axis=1))
+    full = diagonals_of(jnp.concatenate([own, side], axis=1))
+    first = full[:, :LANES] - alone[:, :LANES]
+    last = full[:, cells - LANES : cells] - alone[:, cells - LANES : cells]
+    beyond = full[:, cells:]
+    at_lane = lax.broadcasted_iota(jnp.int32, (2 * ROWS, LANES), 1)
+    change = jnp.where(at_lane < middle // 2, first, beyond)
+    change = jnp.where((at_lane >= middle // 2) & (at_lane < middle), pltpu.roll(last, middle, 1), change)
+    change = jnp.where((at_lane >= middle) & (at_lane < middle + SWEEPS), pltpu.roll(beyond, middle, 1), change)
+    column = lax.broadcasted_iota(jnp.int32, (NEAR, LANES), 1)
+    row = lax.broadcasted_iota(jnp.int32, (NEAR, LANES), 0)
+    at_first = row - jnp.where(column < middle, column, column - LANES)
+    at_last = (row - NEAR) - (column - middle)
+    matrix = jnp.concatenate([spread(change, at_first), spread(change, at_last)], axis=0)
+    a_high, a_low = split(matrix)
+    a_both = jnp.concatenate([a_high, a_low], axis=0)
+    for at in range(2 * held):
+        c, k = divmod(at, held)
+        for begin in range(0, sensors, ROWS * GROUPS):
+            packed = slice(begin // GROUPS, begin // GROUPS + ROWS)
+            values = parts(at, packed)
+            for group in range(min(GROUPS, (sensors - begin) // ROWS)):
+                tile = jnp.zeros((ROWS, LANES), jnp.float32)
+                for value, spot in zip(values, spots):
+                    moved = pltpu.roll(value, (spot - group * SWEEPS) % LANES, 1)
+                    tile = jnp.where((lane >= spot) & (lane < spot + SWEEPS), moved, tile)
+                rows_at = begin + group * ROWS
+                sides[rows_at : rows_at + ROWS] = tile
+        high, low = split(sides[...])
+        both = product(a_both, high, ((1,), (1,)))
+        total = near_ref[c, k] + both[: 2 * NEAR] + both[2 * NEAR :] + product(a_high, low, ((1,), (1,)))
+        high, low = split(total)
+        high_ref[c, k] = high
+        low_ref[c, k] = low
+
+
+def near_edges(near, own_inner, own_outer, inner, outer, band_index, band_rates):
+    shape = jax.ShapeDtypeStruct(near.shape, jnp.bfloat16)
+    held, sensors = near.shape[1], near.shape[3]
+    return pl.pallas_call(
+        near_kernel,
+        in_specs=[VMEM_SPEC] * 6 + [SMEM_SPEC],
+        out_specs=[VMEM_SPEC] * 2,
+        out_shape=[shape, shape],
+        scratch_shapes=[pltpu.VMEM((sensors, LANES), jnp.float32)],
+        compiler_params=grant(8),
+        cost_estimate=pl.CostEstimate(
+            flops=24 * held * sensors * NEAR * LANES, bytes_accessed=8 * near.size, transcendentals=0
+        ),
+        name="near_edges",
+    )(near, own_inner, own_outer, inner, outer, band_index.reshape(1, -1), band_rates)
+
+
+def forward_kernel(
+    steps, chips, wanted, x_ref, high_ref, low_ref, near_high_ref, near_low_ref, away_ref, home_ref
+):
     share, sensors = home_ref.shape[3:]
     per = share // ROWS
     cell = lax.axis_index("cell")
@@ -355,6 +401,11 @@
         for s in steps:
             order.append((2 * lax.rem(chip + s, chips) + side) * per)
     rows = len(order) * share
+
+    def whole(ref, near, c, k):
+        inside = ref[c, k, NEAR : cells - NEAR]
+        return jnp.concatenate([near[c, k, :NEAR], inside, near[c, k, NEAR:]], axis=0)
+
     for at, k in enumerate(wanted):
         parts = []
         for c in range(2):
@@ -364,8 +415,9 @@
         both = jnp.concatenate([high, low], axis=0)
         terms = []
         for c in range(2):
-            wide = product(both, high_ref[c, k], ((1,), (0,)))
-            terms.append(wide[: 2 * rows] + wide[2 * rows :] + product(high, low_ref[c, k], ((1,), (0,))))
+            wide = product(both, whole(high_ref, near_high_ref, c, k), ((1,), (0,)))
+            small = product(high, whole(low_ref, near_low_ref, c, k), ((1,), (0,)))
+            terms.append(wide[: 2 * rows] + wide[2 * rows :] + small)
         re = (terms[0][:rows] - terms[1][rows:]).reshape(2, len(steps), share, sensors)
         im = (terms[0][rows:] + terms[1][:rows]).reshape(2, len(steps), share, sensors)
         for side, ref in enumerate((away_ref, home_ref)):
@@ -373,14 +425,14 @@
             ref[:, 1, at] = im[side]
 
 
-def forward(returned, high, low, steps, chips, wanted):
+def forward(returned, matrices, steps, chips, wanted):
     shards, _, _, rows, cells = returned.shape
-    sensors = high.shape[3]
+    sensors = matrices[0].shape[3]
     share = shards * rows // (2 * chips)
     shape = jax.ShapeDtypeStruct((len(steps), 2, len(wanted), share, sensors), jnp.float32)
     return pl.pallas_call(
         functools.partial(forward_kernel, steps, chips, wanted),
-        in_specs=[VMEM_SPEC] * 3,
+        in_specs=[VMEM_SPEC] * 5,
         out_specs=[VMEM_SPEC] * 2,
         out_shape=[shape, shape],
         compiler_params=grant(16),
@@ -389,7 +441,7 @@
             bytes_accessed=8 * len(wanted) * sensors * cells,
             transcendentals=0,
         ),
-    )(returned, high, low)
+    )(returned, *matrices)
 
 
 def total_kernel(home_ref, away_ref, *refs):
@@ -407,27 +459,34 @@
     chips = strips // 2
     held = columns.shape[1]
     columns, blocks = in_hbm(columns), in_hbm(freq_blocks)
-    spectrum, inner, outer, cutoff = adjoint(columns, blocks, band_index, band_rates, causal_cutoffs, shards)
+    spectrum, own_inner, own_outer, cutoff = adjoint(
+        columns, blocks, band_index, band_rates, causal_cutoffs, shards
+    )
     gathered = lax.all_to_all(spectrum, "freq", split_axis=0, concat_axis=0, tiled=True)
-    inner = lax.ppermute(inner, "cell", [(i, i ^ 1) for i in range(strips)])
-    pairs = [(i, i + 1) for i in range(1, strips - 1, 2)]
-    outer = lax.ppermute(outer, "cell", pairs + [(j, i) for i, j in pairs])
-    gathered, inner, outer = lax.optimization_barrier((gathered, inner, outer))
     spectrum = middle(gathered, cutoff)
-    high, low = smooth(blocks, inner, outer, band_index, band_rates)
+    spectrum, own_inner, own_outer, freq_blocks = lax.optimization_barrier(
+        (spectrum, own_inner, own_outer, freq_blocks)
+    )
+    blocks = in_hbm(freq_blocks)
     returned = lax.all_to_all(spectrum, "freq", split_axis=0, concat_axis=0, tiled=True)
     swap = [(i, i ^ 1) for i in range(strips)]
+    pairs = [(i, i + 1) for i in range(1, strips - 1, 2)]
+    outer = lax.ppermute(own_outer, "cell", pairs + [(j, i) for i, j in pairs])
+    inner = lax.ppermute(own_inner, "cell", swap)
+    high, low, near = smooth(blocks, band_index, band_rates)
+    near = near_edges(near, own_inner, own_outer, inner, outer, band_index, band_rates)
+    matrices = (high, low, *near)
     leaving = []
     if chips > 1:
         for k in range(held):
-            away, home = forward(returned, high, low, range(1, chips), chips, (k,))
+            away, home = forward(returned, matrices, range(1, chips), chips, (k,))
             leaving.append(home + lax.ppermute(away, "cell", swap))
     arrived = []
     for s in range(1, chips):
         pairs = [(i, 2 * ((i // 2 + s) % chips) + i % 2) for i in range(strips)]
         for k in range(held):
             arrived.append(lax.ppermute(leaving[k][s - 1], "cell", pairs))
-    away, home = forward(returned, high, low, range(1), chips, range(held))
+    away, home = forward(returned, matrices, range(1), chips, range(held))
     away = lax.ppermute(away, "cell", swap)
     share, sensors = home.shape[3:]
     return pl.pallas_call(

time: 43.1 us -> 42.6 us (0.988)
  blocking collectives: 0 us -> 16 us
  waiting for transfers between devices: 16.8 us -> 5.61 us
  starting transfers between devices: 14.5 us -> 8.4 us
  Pallas kernels: 11.3 us -> 12.1 us
    all_to_all x0 -> x1, blocking collectives: none -> 16 us  [on_device(): lax.all_to_all(spectrum, 'freq', split_axis=0, concat_axis=0, tiled=True)]
    all_to_all x2 -> x1, waiting for transfers between devices: 11.8 us -> 1.58 us  [on_device(): lax.all_to_all(spectrum, 'freq', split_axis=0, concat_axis=0, tiled=True)]
    all_to_all x2 -> x1, starting transfers between devices: 10.9 us -> 3.6 us  [on_device(): lax.all_to_all(spectrum, 'freq', split_axis=0, concat_axis=0, tiled=True)]
    pallas_call x2 -> x3, Pallas kernels: 8.46 us -> 9.28 us  [the longest x1 4.11 us: smooth(): pl.pallas_call(smooth_kernel, in_specs=[HBM_SPEC, VMEM_SPEC, SMEM_SPEC],...]
    ppermute x2, starting transfers between devices: 0.63 us -> 1.42 us  [on_device(): leaving.append(home + lax.ppermute(away, 'cell', swap))]
    ppermute x2, waiting for transfers between devices: 0.57 us -> 0.01 us  [the longest x1 0.01 us: on_device(): inner = lax.ppermute(own_inner, 'cell', swap)]
    ppermute x1, starting transfers between devices: 0.08 us -> 0.56 us  [on_device(): away = lax.ppermute(away, 'cell', swap)]
    ppermute x2, waiting for transfers between devices: 4.48 us -> 4.02 us  [on_device(): arrived.append(lax.ppermute(leaving[k][s - 1], 'cell', pairs))]
  transfers between devices with their start and end apart: 9 -> 8, of which waited for: 5 -> 3; matrix products, arithmetic and copies ran while one was open for 0% -> 0% of each run, Pallas kernels for 13% -> 17%
where the time goes in v1:
time: 42.6 us; the launch traced here: 42.3 us
  blocking collectives  16 us (38%)
  Pallas kernels  12.1 us (28%)
  starting transfers between devices  8.4 us (20%)
  waiting for transfers between devices  5.61 us (13%)
    all_to_all x1, blocking collectives, on_device(): lax.all_to_all(spectrum, 'freq', split_axis=0, concat_axis=0, tiled=True)  16 us
    pallas_call x1, Pallas kernels, smooth(): pl.pallas_call(smooth_kernel, in_specs=[HBM_SPEC, VMEM_SPEC, SMEM_SPEC],...  4.11 us
    ppermute x2, waiting for transfers between devices, on_device(): arrived.append(lax.ppermute(leaving[k][s - 1], 'cell', pairs))  4.02 us
    all_to_all x1, starting transfers between devices, on_device(): lax.all_to_all(spectrum, 'freq', split_axis=0, concat_axis=0, tiled=True)  3.6 us
    pallas_call x1, Pallas kernels, adjoint(): pl.pallas_call(adjoint_kernel, in_specs=[HBM_SPEC] * 5, out_specs=[VMEM_S...  3.03 us
    ppermute x2, starting transfers between devices, on_device(): arrived.append(lax.ppermute(leaving[k][s - 1], 'cell', pairs))  2.16 us
    pallas_call x1, Pallas kernels, near_edges(): pl.pallas_call(near_kernel, in_specs=[VMEM_SPEC] * 6 + [SMEM_SPEC], out_s...  2.15 us
    all_to_all x1, waiting for transfers between devices, on_device(): lax.all_to_all(spectrum, 'freq', split_axis=0, concat_axis=0, tiled=True)  1.58 us
  transfers between devices with their start and end apart: 8, of which 3 were waited for; matrix products, arithmetic and copies ran while one was open for 0% of the time, Pallas kernels for 17%

profile of v1, /device:TPU:0, one launch (start us, length us, event | category | flops | bytes accessed | tf_op | source)
XLA Modules:
  0.0 42.3 jit_solution(12303247459069713668)
XLA Ops:
  0.0 3.0 %adjoint.1 = (f32[8,2,2,8,256]{4,3,2,1,0:T(8,128)S(1)}, f32[5,24,128]{2,1,0:T(8,128)S(1)}, f32[5,24,128]{2,1,0:T(8,128)S(1)}, s32[8,128]{1,0:T(8,128)S(1)}) custom-call(f32[2,2,64,600]{3,2,1,0:T(8,128)} %v_hbm.1, f32[2,2,600,256]{3,2,1,0:T(8,128)} %f_hbm.2, s32[1,256]{1,0:T(1,128)} %bitcast.15, f32[8]{0:T(128)} %rates_ref.3, s32[64]{0:T(128)} %cut_hbm.1), custom_call_target="tpu_custom_call" | custom-call | flops 471859200 | bytes 2457600 | tf_op jit(solution)/shard_map/adjoint/pallas_call | solution.py:139
  3.0 0.0 copy-start
  3.0 0.0 copy-start.1
  3.1 16.0 %all_to_all.10.x_ref = f32[8,2,2,8,256]{4,3,2,1,0:T(8,128)S(1)} all-to-all(f32[8,2,2,8,256]{4,3,2,1,0:T(8,128)S(1)} %get-tuple-element.24), channel_id=1, replica_groups=mesh['freq'=8,'cell'=4] {'freq'}, dimensions={0} | all-to-all | bytes 524288 | tf_op jit(solution)/shard_map/all_to_all | solution.py:465
  19.1 0.9 %middle.1 = f32[8,2,2,8,256]{4,3,2,1,0:T(8,128)} custom-call(f32[8,2,2,8,256]{4,3,2,1,0:T(8,128)S(1)} %all_to_all.10.x_ref, s32[8,128]{1,0:T(8,128)S(1)} %get-tuple-element.25.cutoff_ref), custom_call_target="tpu_custom_call" | custom-call | flops 3932160 | bytes 524288 | tf_op jit(solution)/shard_map/middle/pallas_call | solution.py:223
  20.0 3.6 %all-to-all-start.1 = ((f32[8,2,2,8,256]{4,3,2,1,0:T(8,128)}), f32[8,2,2,8,256]{4,3,2,1,0:T(8,128)S(1)}, u32[]{:S(2)}, u32[]{:S(2)}) async-start(f32[8,2,2,8,256]{4,3,2,1,0:T(8,128)} %middle.1), calls=%async_computation.1 | async-start | bytes 524288 | tf_op jit(solution)/shard_map/all_to_all | solution.py:471
  23.6 0.7 %collective-permute-start.1 = (f32[5,24,128]{2,1,0:T(8,128)S(1)}, f32[5,24,128]{2,1,0:T(8,128)S(1)}, u32[]{:S(2)}, u32[]{:S(2)}) collective-permute-start(f32[5,24,128]{2,1,0:T(8,128)S(1)} %get-tuple-element.34.own_outer_ref), channel_id=1, source_target_pairs={{1,2},{2,1},{5,6},{6,5},{9,10},{10,9},{13,14},{14,13},{17,18},{18,... | collective-permute-start | bytes 184328 | tf_op jit(solution)/shard_map/ppermute | solution.py:474
  24.3 4.1 %smooth.1 = (bf16[2,2,256,600]{3,2,1,0:T(8,128)(2,1)S(1)}, bf16[2,2,256,600]{3,2,1,0:T(8,128)(2,1)S(1)}, f32[2,2,32,600]{3,2,1,0:T(8,128)S(1)}) custom-call(f32[2,2,600,256]{3,2,1,0:T(8,128)} %f_hbm.2, s32[1,256]{1,0:T(1,128)S(1)} %bitcast.16, f32[8]{0:T(128)S(1)} %copy-done.1), custom_call_target="tpu_custom_call" | custom-call | flops 943718400 | bytes 4915200 | tf_op jit(solution)/shard_map/smooth/pallas_call | solution.py:296
  28.4 0.0 collective-permute-done.inner_ref
  28.4 0.0 collective-permute-done.1.outer_ref
  28.4 2.1 %near_edges.1 = (bf16[2,2,32,600]{3,2,1,0:T(8,128)(2,1)S(1)}, bf16[2,2,32,600]{3,2,1,0:T(8,128)(2,1)S(1)}) custom-call(f32[2,2,32,600]{3,2,1,0:T(8,128)S(1)} %get-tuple-element.32.near_ref, f32[5,24,128]{2,1,0:T(8,128)S(1)} %get-tuple-element.33.own_inner_ref, f32[5,24,128]{2,1,0:T(8,128)S(1)} %get-tuple-element.34.own_outer_ref, ...), custom_call_target="tpu_custom_call" | custom-call | flops 58982400 | bytes 614400 | tf_op jit(solution)/shard_map/near_edges/pallas_call | solution.py:377
  30.6 1.6 %all-to-all-done.1.x_ref = f32[8,2,2,8,256]{4,3,2,1,0:T(8,128)S(1)} async-done(((f32[8,2,2,8,256]{4,3,2,1,0:T(8,128)}), f32[8,2,2,8,256]{4,3,2,1,0:T(8,128)S(1)}, u32[]{:S(2)}, u32[]{:S(2)}) %all-to-all-start.1) | async-done | bytes 262176 | tf_op jit(solution)/shard_map/all_to_all | solution.py:471
  32.2 0.3 shard_map.57
  32.5 1.3 %collective-permute-start.5 = (f32[1,2,1,16,600]{4,3,1,2,0:T(8,128)S(1)}, f32[1,2,1,16,600]{4,3,1,2,0:T(8,128)S(1)}, u32[]{:S(2)}, u32[]{:S(2)}) collective-permute-start(f32[1,2,1,16,600]{4,3,1,2,0:T(8,128)S(1)} %bitcast.19), channel_id=1, source_target_pairs={{0,1},{1,0},{2,3},{3,2},{4,5},{5,4},{6,7},{7,6},{8,9},{9,8},{10,11... | collective-permute-start | bytes 230408 | tf_op jit(solution)/shard_map/ppermute | solution.py:483
  33.9 0.3 shard_map.56
  34.2 0.1 collective-permute-start.3
  34.3 0.6 %shard_map.55 = (f32[1,2,2,16,600]{4,3,2,1,0:T(8,128)S(1)}, f32[1,2,2,16,600]{4,3,2,1,0:T(8,128)S(1)}) custom-call(f32[8,2,2,8,256]{4,3,2,1,0:T(8,128)S(1)} %all-to-all-done.1.x_ref, bf16[2,2,256,600]{3,2,1,0:T(8,128)(2,1)S(1)} %get-tuple-element.30.high_ref, bf16[2,2,256,600]{3,2,1,0:T(8,128)(2,1)S(1)} %get-tuple-element.31.low_ref, ...), custom_call_target="tpu_custom_call" | custom-call | flops 235929600 | bytes 2457600 | tf_op jit(solution)/shard_map/pallas_call | solution.py:433
  34.8 0.6 %collective-permute-start.2 = (f32[1,2,2,16,600]{4,3,2,1,0:T(8,128)S(1)}, f32[1,2,2,16,600]{4,3,2,1,0:T(8,128)S(1)}, u32[]{:S(2)}, u32[]{:S(2)}) collective-permute-start(f32[1,2,2,16,600]{4,3,2,1,0:T(8,128)S(1)} %get-tuple-element.38), channel_id=1, source_target_pairs={{0,1},{1,0},{2,3},{3,2},{4,5},{5,4},{6,7},{7,6},{8,9},{9,8},{10,11... | collective-permute-start | bytes 460808 | tf_op jit(solution)/shard_map/ppermute | solution.py:490
  35.4 0.0 collective-permute-done.5
  35.4 0.6 %collective-permute-start.6 = (f32[2,1,16,600]{3,2,1,0:T(8,128)S(1)}, f32[2,1,16,600]{3,2,1,0:T(8,128)S(1)}, u32[]{:S(2)}, u32[]{:S(2)}) collective-permute-start(f32[2,1,16,600]{3,2,1,0:T(8,128)S(1)} %fusion), channel_id=1, source_target_pairs={{0,2},{1,3},{2,0},{3,1},{4,6},{5,7},{6,4},{7,5},{8,10},{9,11},{10,... | collective-permute-start | bytes 230408 | tf_op jit(solution)/shard_map/ppermute | solution.py:488
  36.0 1.6 %collective-permute-start.4 = (f32[2,1,16,600]{3,2,1,0:T(8,128)S(1)}, f32[2,1,16,600]{3,2,1,0:T(8,128)S(1)}, u32[]{:S(2)}, u32[]{:S(2)}) collective-permute-start(f32[2,1,16,600]{3,2,1,0:T(8,128)S(1)} %fusion.1), channel_id=1, source_target_pairs={{0,2},{1,3},{2,0},{3,1},{4,6},{5,7},{6,4},{7,5},{8,10},{9,11},{10,... | collective-permute-start | bytes 230408 | tf_op jit(solution)/shard_map/ppermute | solution.py:488
  37.6 3.1 %collective-permute-done.6.refs_1_ = f32[2,1,16,600]{3,2,1,0:T(8,128)S(1)} collective-permute-done((f32[2,1,16,600]{3,2,1,0:T(8,128)S(1)}, f32[2,1,16,600]{3,2,1,0:T(8,128)S(1)}, u32[]{:S(2)}, u32[]{:S(2)}) %collective-permute-start.6) | collective-permute-done | bytes 76832 | tf_op jit(solution)/shard_map/ppermute | solution.py:488
  40.7 0.9 %collective-permute-done.4.refs_0_ = f32[2,1,16,600]{3,2,1,0:T(8,128)S(1)} collective-permute-done((f32[2,1,16,600]{3,2,1,0:T(8,128)S(1)}, f32[2,1,16,600]{3,2,1,0:T(8,128)S(1)}, u32[]{:S(2)}, u32[]{:S(2)}) %collective-permute-start.4) | collective-permute-done | bytes 76832 | tf_op jit(solution)/shard_map/ppermute | solution.py:488
  41.6 0.7 %total.1 = f32[2,2,16,600]{3,2,1,0:T(8,128)} custom-call(f32[1,2,2,16,600]{4,3,2,1,0:T(8,128)S(1)} %get-tuple-element.37.home_ref, f32[1,2,2,16,600]{4,3,2,1,0:T(8,128)S(1)} %collective-permute-done.2.away_ref, f32[2,1,16,600]{3,2,1,0:T(8,128)S(1)} %collective-permute-done.4.refs_0_, f32[2,1,16,600]{3,2,1,0:T(8,128)S(1)} %collective-permute-done.6.refs_1_), custom_call_target="tpu_custom_call" | custom-call | tf_op jit(solution)/shard_map/total/pallas_call | solution.py:492
  (7 shorter events, 0.0 us)
Async XLA Ops:
  3.0 21.2 %copy-start = (s32[256]{0:T(256)S(1)}, s32[256]{0:T(256)}, u32[]{:S(2)}) copy-start(s32[256]{0:T(256)} %param.8) | copy-start | bytes 3076
  3.0 21.2 %copy-start.1 = (f32[8]{0:T(128)S(1)}, f32[8]{0:T(128)}, u32[]{:S(2)}) copy-start(f32[8]{0:T(128)} %rates_ref.3) | copy-start | bytes 100
  20.0 12.2 %all-to-all-start.1 = ((f32[8,2,2,8,256]{4,3,2,1,0:T(8,128)}), f32[8,2,2,8,256]{4,3,2,1,0:T(8,128)S(1)}, u32[]{:S(2)}, u32[]{:S(2)}) async-start(f32[8,2,2,8,256]{4,3,2,1,0:T(8,128)} %middle.1), calls=%async_computation.1 | async-start | bytes 524288 | tf_op jit(solution)/shard_map/all_to_all | solution.py:471
  23.6 4.8 %collective-permute-start = (f32[5,24,128]{2,1,0:T(8,128)S(1)}, f32[5,24,128]{2,1,0:T(8,128)S(1)}, u32[]{:S(2)}, u32[]{:S(2)}) collective-permute-start(f32[5,24,128]{2,1,0:T(8,128)S(1)} %get-tuple-element.33.own_inner_ref), channel_id=1, source_target_pairs={{0,1},{1,0},{2,3},{3,2},{4,5},{5,4},{6,7},{7,6},{8,9},{9,8},{10,11... | collective-permute-start | bytes 184328 | tf_op jit(solution)/shard_map/ppermute | solution.py:475
  23.6 4.8 %collective-permute-start.1 = (f32[5,24,128]{2,1,0:T(8,128)S(1)}, f32[5,24,128]{2,1,0:T(8,128)S(1)}, u32[]{:S(2)}, u32[]{:S(2)}) collective-permute-start(f32[5,24,128]{2,1,0:T(8,128)S(1)} %get-tuple-element.34.own_outer_ref), channel_id=1, source_target_pairs={{1,2},{2,1},{5,6},{6,5},{9,10},{10,9},{13,14},{14,13},{17,18},{18,... | collective-permute-start | bytes 184328 | tf_op jit(solution)/shard_map/ppermute | solution.py:474
  32.5 2.9 %collective-permute-start.5 = (f32[1,2,1,16,600]{4,3,1,2,0:T(8,128)S(1)}, f32[1,2,1,16,600]{4,3,1,2,0:T(8,128)S(1)}, u32[]{:S(2)}, u32[]{:S(2)}) collective-permute-start(f32[1,2,1,16,600]{4,3,1,2,0:T(8,128)S(1)} %bitcast.19), channel_id=1, source_target_pairs={{0,1},{1,0},{2,3},{3,2},{4,5},{5,4},{6,7},{7,6},{8,9},{9,8},{10,11... | collective-permute-start | bytes 230408 | tf_op jit(solution)/shard_map/ppermute | solution.py:483
  34.2 1.8 %collective-permute-start.3 = (f32[1,2,1,16,600]{4,3,1,2,0:T(8,128)S(1)}, f32[1,2,1,16,600]{4,3,1,2,0:T(8,128)S(1)}, u32[]{:S(2)}, u32[]{:S(2)}) collective-permute-start(f32[1,2,1,16,600]{4,3,1,2,0:T(8,128)S(1)} %bitcast.18), channel_id=1, source_target_pairs={{0,1},{1,0},{2,3},{3,2},{4,5},{5,4},{6,7},{7,6},{8,9},{9,8},{10,11... | collective-permute-start | bytes 230408 | tf_op jit(solution)/shard_map/ppermute | solution.py:483
  34.8 6.8 %collective-permute-start.2 = (f32[1,2,2,16,600]{4,3,2,1,0:T(8,128)S(1)}, f32[1,2,2,16,600]{4,3,2,1,0:T(8,128)S(1)}, u32[]{:S(2)}, u32[]{:S(2)}) collective-permute-start(f32[1,2,2,16,600]{4,3,2,1,0:T(8,128)S(1)} %get-tuple-element.38), channel_id=1, source_target_pairs={{0,1},{1,0},{2,3},{3,2},{4,5},{5,4},{6,7},{7,6},{8,9},{9,8},{10,11... | collective-permute-start | bytes 460808 | tf_op jit(solution)/shard_map/ppermute | solution.py:490
  35.4 5.3 %collective-permute-start.6 = (f32[2,1,16,600]{3,2,1,0:T(8,128)S(1)}, f32[2,1,16,600]{3,2,1,0:T(8,128)S(1)}, u32[]{:S(2)}, u32[]{:S(2)}) collective-permute-start(f32[2,1,16,600]{3,2,1,0:T(8,128)S(1)} %fusion), channel_id=1, source_target_pairs={{0,2},{1,3},{2,0},{3,1},{4,6},{5,7},{6,4},{7,5},{8,10},{9,11},{10,... | collective-permute-start | bytes 230408 | tf_op jit(solution)/shard_map/ppermute | solution.py:488
  36.0 5.6 %collective-permute-start.4 = (f32[2,1,16,600]{3,2,1,0:T(8,128)S(1)}, f32[2,1,16,600]{3,2,1,0:T(8,128)S(1)}, u32[]{:S(2)}, u32[]{:S(2)}) collective-permute-start(f32[2,1,16,600]{3,2,1,0:T(8,128)S(1)} %fusion.1), channel_id=1, source_target_pairs={{0,2},{1,3},{2,0},{3,1},{4,6},{5,7},{6,4},{7,5},{8,10},{9,11},{10,... | collective-permute-start | bytes 230408 | tf_op jit(solution)/shard_map/ppermute | solution.py:488

commit v2 on v1

--- a/solution.py
+++ b/solution.py
@@ -318,9 +318,9 @@
     sensors = near_ref.shape[3]
     cells = band_ref.shape[1]
     even = lax.axis_index("cell") % 2 == 0
-    lane = lax.broadcasted_iota(jnp.int32, (ROWS, LANES), 1)
-    middle = LANES // 2
-    spots = (0, middle - SWEEPS, middle, LANES - SWEEPS)
+    kinds = 4
+    per = kinds * SWEEPS
+    pairs = LANES // (2 * per)
 
     def parts(at, rows):
         own_inner, own_outer = own_inner_ref[at, rows], own_outer_ref[at, rows]
@@ -332,6 +332,7 @@
             jnp.where(even, outer, inner),
         )
 
+    lane = lax.broadcasted_iota(jnp.int32, (ROWS, LANES), 1)
     _, _, after, before = parts(2 * held, slice(0, ROWS))
     side = jnp.where(lane < SWEEPS, after, jnp.where(lane >= LANES - SWEEPS, before, 0.0))[:1]
     own = rates_of(band_ref, rates_ref)
@@ -340,35 +341,51 @@
     first = full[:, :LANES] - alone[:, :LANES]
     last = full[:, cells - LANES : cells] - alone[:, cells - LANES : cells]
     beyond = full[:, cells:]
-    at_lane = lax.broadcasted_iota(jnp.int32, (2 * ROWS, LANES), 1)
-    change = jnp.where(at_lane < middle // 2, first, beyond)
-    change = jnp.where((at_lane >= middle // 2) & (at_lane < middle), pltpu.roll(last, middle, 1), change)
-    change = jnp.where((at_lane >= middle) & (at_lane < middle + SWEEPS), pltpu.roll(beyond, middle, 1), change)
-    column = lax.broadcasted_iota(jnp.int32, (NEAR, LANES), 1)
-    row = lax.broadcasted_iota(jnp.int32, (NEAR, LANES), 0)
-    at_first = row - jnp.where(column < middle, column, column - LANES)
-    at_last = (row - NEAR) - (column - middle)
-    matrix = jnp.concatenate([spread(change, at_first), spread(change, at_last)], axis=0)
+    kind = lax.broadcasted_iota(jnp.int32, (2 * ROWS, LANES), 1) // SWEEPS
+    change = jnp.where(kind == 0, first, 0.0)
+    change = jnp.where(kind == 1, pltpu.roll(last, 2 * SWEEPS, 1), change)
+    change = jnp.where(kind == 2, pltpu.roll(beyond, 2 * SWEEPS, 1), change)
+    change = jnp.where(kind == 3, pltpu.roll(beyond, 4 * SWEEPS, 1), change)
+    for shift in (per, 2 * per, 4 * per):
+        change = change + pltpu.roll(change, shift, 1)
+    row = lax.broadcasted_iota(jnp.int32, (2 * NEAR, LANES), 0)
+    column = lax.broadcasted_iota(jnp.int32, (2 * NEAR, LANES), 1)
+    kind, i = (column // SWEEPS) % kinds, column % SWEEPS
+    at_first = jnp.where(kind == 0, row - i, jnp.where(kind == 3, row + SWEEPS - i, LANES))
+    end = row - 2 * NEAR
+    at_last = jnp.where(kind == 1, end + SWEEPS - i, jnp.where(kind == 2, end - i, LANES))
+    matrix = spread(change, jnp.where(row < NEAR, at_first, at_last))
     a_high, a_low = split(matrix)
-    a_both = jnp.concatenate([a_high, a_low], axis=0)
-    for at in range(2 * held):
-        c, k = divmod(at, held)
+    owner = column // per
+    cell_of = lane // SWEEPS
+    for begin_at in range(0, 2 * held, pairs):
+        ats = range(begin_at, min(2 * held, begin_at + pairs))
         for begin in range(0, sensors, ROWS * GROUPS):
             packed = slice(begin // GROUPS, begin // GROUPS + ROWS)
-            values = parts(at, packed)
+            values = [value for at in ats for value in parts(at, packed)]
+            values = [pltpu.roll(value, n * SWEEPS, 1) if n else value for n, value in enumerate(values)]
             for group in range(min(GROUPS, (sensors - begin) // ROWS)):
                 tile = jnp.zeros((ROWS, LANES), jnp.float32)
-                for value, spot in zip(values, spots):
-                    moved = pltpu.roll(value, (spot - group * SWEEPS) % LANES, 1)
-                    tile = jnp.where((lane >= spot) & (lane < spot + SWEEPS), moved, tile)
+                for n, value in enumerate(values):
+                    tile = jnp.where(cell_of == (group + n) % GROUPS, value, tile)
+                tile = pltpu.roll(tile, (LANES - group * SWEEPS) % LANES, 1)
                 rows_at = begin + group * ROWS
-                sides[rows_at : rows_at + ROWS] = tile
+                sides[rows_at : rows_at + ROWS] = tile + pltpu.roll(tile, LANES // 2, 1)
         high, low = split(sides[...])
-        both = product(a_both, high, ((1,), (1,)))
-        total = near_ref[c, k] + both[: 2 * NEAR] + both[2 * NEAR :] + product(a_high, low, ((1,), (1,)))
-        high, low = split(total)
-        high_ref[c, k] = high
-        low_ref[c, k] = low
+        low_lane = lax.broadcasted_iota(jnp.int32, (sensors, LANES), 1) >= LANES // 2
+        operand = jnp.where(low_lane, low.astype(jnp.float32), high.astype(jnp.float32)).astype(jnp.bfloat16)
+        left = []
+        for p in range(len(ats)):
+            left.append(jnp.where(owner % pairs == p, a_high.astype(jnp.float32), 0.0))
+            left.append(jnp.where(owner == p, a_low.astype(jnp.float32), 0.0))
+        left = jnp.concatenate(left, axis=0).astype(jnp.bfloat16)
+        terms = product(left, operand, ((1,), (1,)))
+        for p, at in enumerate(ats):
+            c, k = divmod(at, held)
+            mine = terms[4 * NEAR * p : 4 * NEAR * (p + 1)]
+            high, low = split(near_ref[c, k] + mine[: 2 * NEAR] + mine[2 * NEAR :])
+            high_ref[c, k] = high
+            low_ref[c, k] = low
 
 
 def near_edges(near, own_inner, own_outer, inner, outer, band_index, band_rates):

time: 42.6 us -> 42 us (0.986)
  waiting for transfers between devices: 5.61 us -> 6.35 us
  starting transfers between devices: 8.4 us -> 7.72 us
  Pallas kernels: 12.1 us -> 11.5 us
    all_to_all x1, waiting for transfers between devices: 1.58 us -> 2.25 us  [on_device(): lax.all_to_all(spectrum, 'freq', split_axis=0, concat_axis=0, tiled=True)]
    ppermute x2, starting transfers between devices: 1.42 us -> 0.74 us  [on_device(): leaving.append(home + lax.ppermute(away, 'cell', swap))]
    pallas_call x1, Pallas kernels: 2.15 us -> 1.47 us  [near_edges(): pl.pallas_call(near_kernel, in_specs=[VMEM_SPEC] * 6 + [SMEM_SPEC], out_s...]
  transfers between devices with their start and end apart: 8 -> 8, of which waited for: 3 -> 3; matrix products, arithmetic and copies ran while one was open for 0% -> 0% of each run, Pallas kernels for 17% -> 16%
where the time goes in v2:
time: 42 us; the launch traced here: 41.7 us
  blocking collectives  16 us (38%)
  Pallas kernels  11.5 us (27%)
  starting transfers between devices  7.72 us (18%)
  waiting for transfers between devices  6.35 us (15%)
    all_to_all x1, blocking collectives, on_device(): lax.all_to_all(spectrum, 'freq', split_axis=0, concat_axis=0, tiled=True)  16 us
    pallas_call x1, Pallas kernels, smooth(): pl.pallas_call(smooth_kernel, in_specs=[HBM_SPEC, VMEM_SPEC, SMEM_SPEC],...  4.11 us
    ppermute x2, waiting for transfers between devices, on_device(): arrived.append(lax.ppermute(leaving[k][s - 1], 'cell', pairs))  4.09 us
    all_to_all x1, starting transfers between devices, on_device(): lax.all_to_all(spectrum, 'freq', split_axis=0, concat_axis=0, tiled=True)  3.6 us
    pallas_call x1, Pallas kernels, adjoint(): pl.pallas_call(adjoint_kernel, in_specs=[HBM_SPEC] * 5, out_specs=[VMEM_S...  3.03 us
    all_to_all x1, waiting for transfers between devices, on_device(): lax.all_to_all(spectrum, 'freq', split_axis=0, concat_axis=0, tiled=True)  2.25 us
    ppermute x2, starting transfers between devices, on_device(): arrived.append(lax.ppermute(leaving[k][s - 1], 'cell', pairs))  2.16 us
    pallas_call x1, Pallas kernels, near_edges(): pl.pallas_call(near_kernel, in_specs=[VMEM_SPEC] * 6 + [SMEM_SPEC], out_s...  1.47 us
  transfers between devices with their start and end apart: 8, of which 3 were waited for; matrix products, arithmetic and copies ran while one was open for 0% of the time, Pallas kernels for 16%

profile of v2, /device:TPU:0, one launch (start us, length us, event | category | flops | bytes accessed | tf_op | source)
XLA Modules:
  0.0 41.7 jit_solution(189064722686033639)
XLA Ops:
  0.0 3.0 %adjoint.1 = (f32[8,2,2,8,256]{4,3,2,1,0:T(8,128)S(1)}, f32[5,24,128]{2,1,0:T(8,128)S(1)}, f32[5,24,128]{2,1,0:T(8,128)S(1)}, s32[8,128]{1,0:T(8,128)S(1)}) custom-call(f32[2,2,64,600]{3,2,1,0:T(8,128)} %v_hbm.1, f32[2,2,600,256]{3,2,1,0:T(8,128)} %f_hbm.2, s32[1,256]{1,0:T(1,128)} %bitcast.15, f32[8]{0:T(128)} %rates_ref.3, s32[64]{0:T(128)} %cut_hbm.1), custom_call_target="tpu_custom_call" | custom-call | flops 471859200 | bytes 2457600 | tf_op jit(solution)/shard_map/adjoint/pallas_call | solution.py:139
  3.0 0.0 copy-start
  3.0 0.0 copy-start.1
  3.1 16.0 %all_to_all.10.x_ref = f32[8,2,2,8,256]{4,3,2,1,0:T(8,128)S(1)} all-to-all(f32[8,2,2,8,256]{4,3,2,1,0:T(8,128)S(1)} %get-tuple-element.24), channel_id=1, replica_groups=mesh['freq'=8,'cell'=4] {'freq'}, dimensions={0} | all-to-all | bytes 524288 | tf_op jit(solution)/shard_map/all_to_all | solution.py:482
  19.1 0.9 %middle.1 = f32[8,2,2,8,256]{4,3,2,1,0:T(8,128)} custom-call(f32[8,2,2,8,256]{4,3,2,1,0:T(8,128)S(1)} %all_to_all.10.x_ref, s32[8,128]{1,0:T(8,128)S(1)} %get-tuple-element.25.cutoff_ref), custom_call_target="tpu_custom_call" | custom-call | flops 3932160 | bytes 524288 | tf_op jit(solution)/shard_map/middle/pallas_call | solution.py:223
  20.0 3.6 %all-to-all-start.1 = ((f32[8,2,2,8,256]{4,3,2,1,0:T(8,128)}), f32[8,2,2,8,256]{4,3,2,1,0:T(8,128)S(1)}, u32[]{:S(2)}, u32[]{:S(2)}) async-start(f32[8,2,2,8,256]{4,3,2,1,0:T(8,128)} %middle.1), calls=%async_computation.1 | async-start | bytes 524288 | tf_op jit(solution)/shard_map/all_to_all | solution.py:488
  23.6 0.7 %collective-permute-start.1 = (f32[5,24,128]{2,1,0:T(8,128)S(1)}, f32[5,24,128]{2,1,0:T(8,128)S(1)}, u32[]{:S(2)}, u32[]{:S(2)}) collective-permute-start(f32[5,24,128]{2,1,0:T(8,128)S(1)} %get-tuple-element.34.own_outer_ref), channel_id=1, source_target_pairs={{1,2},{2,1},{5,6},{6,5},{9,10},{10,9},{13,14},{14,13},{17,18},{18,... | collective-permute-start | bytes 184328 | tf_op jit(solution)/shard_map/ppermute | solution.py:491
  24.3 4.1 %smooth.1 = (bf16[2,2,256,600]{3,2,1,0:T(8,128)(2,1)S(1)}, bf16[2,2,256,600]{3,2,1,0:T(8,128)(2,1)S(1)}, f32[2,2,32,600]{3,2,1,0:T(8,128)S(1)}) custom-call(f32[2,2,600,256]{3,2,1,0:T(8,128)} %f_hbm.2, s32[1,256]{1,0:T(1,128)S(1)} %bitcast.16, f32[8]{0:T(128)S(1)} %copy-done.1), custom_call_target="tpu_custom_call" | custom-call | flops 943718400 | bytes 4915200 | tf_op jit(solution)/shard_map/smooth/pallas_call | solution.py:296
  28.4 0.0 collective-permute-done.inner_ref
  28.4 0.0 collective-permute-done.1.outer_ref
  28.4 1.5 %near_edges.1 = (bf16[2,2,32,600]{3,2,1,0:T(8,128)(2,1)S(1)}, bf16[2,2,32,600]{3,2,1,0:T(8,128)(2,1)S(1)}) custom-call(f32[2,2,32,600]{3,2,1,0:T(8,128)S(1)} %get-tuple-element.32.near_ref, f32[5,24,128]{2,1,0:T(8,128)S(1)} %get-tuple-element.33.own_inner_ref, f32[5,24,128]{2,1,0:T(8,128)S(1)} %get-tuple-element.34.own_outer_ref, ...), custom_call_target="tpu_custom_call" | custom-call | flops 58982400 | bytes 614400 | tf_op jit(solution)/shard_map/near_edges/pallas_call | solution.py:394
  29.9 2.3 %all-to-all-done.1.x_ref = f32[8,2,2,8,256]{4,3,2,1,0:T(8,128)S(1)} async-done(((f32[8,2,2,8,256]{4,3,2,1,0:T(8,128)}), f32[8,2,2,8,256]{4,3,2,1,0:T(8,128)S(1)}, u32[]{:S(2)}, u32[]{:S(2)}) %all-to-all-start.1) | async-done | bytes 262176 | tf_op jit(solution)/shard_map/all_to_all | solution.py:488
  32.2 0.3 shard_map.57
  32.5 0.7 %collective-permute-start.5 = (f32[1,2,1,16,600]{4,3,1,2,0:T(8,128)S(1)}, f32[1,2,1,16,600]{4,3,1,2,0:T(8,128)S(1)}, u32[]{:S(2)}, u32[]{:S(2)}) collective-permute-start(f32[1,2,1,16,600]{4,3,1,2,0:T(8,128)S(1)} %bitcast.19), channel_id=1, source_target_pairs={{0,1},{1,0},{2,3},{3,2},{4,5},{5,4},{6,7},{7,6},{8,9},{9,8},{10,11... | collective-permute-start | bytes 230408 | tf_op jit(solution)/shard_map/ppermute | solution.py:500
  33.2 0.3 shard_map.56
  33.5 0.1 collective-permute-start.3
  33.6 0.6 %shard_map.55 = (f32[1,2,2,16,600]{4,3,2,1,0:T(8,128)S(1)}, f32[1,2,2,16,600]{4,3,2,1,0:T(8,128)S(1)}) custom-call(f32[8,2,2,8,256]{4,3,2,1,0:T(8,128)S(1)} %all-to-all-done.1.x_ref, bf16[2,2,256,600]{3,2,1,0:T(8,128)(2,1)S(1)} %get-tuple-element.30.high_ref, bf16[2,2,256,600]{3,2,1,0:T(8,128)(2,1)S(1)} %get-tuple-element.31.low_ref, ...), custom_call_target="tpu_custom_call" | custom-call | flops 235929600 | bytes 2457600 | tf_op jit(solution)/shard_map/pallas_call | solution.py:450
  34.2 0.6 %collective-permute-start.2 = (f32[1,2,2,16,600]{4,3,2,1,0:T(8,128)S(1)}, f32[1,2,2,16,600]{4,3,2,1,0:T(8,128)S(1)}, u32[]{:S(2)}, u32[]{:S(2)}) collective-permute-start(f32[1,2,2,16,600]{4,3,2,1,0:T(8,128)S(1)} %get-tuple-element.38), channel_id=1, source_target_pairs={{0,1},{1,0},{2,3},{3,2},{4,5},{5,4},{6,7},{7,6},{8,9},{9,8},{10,11... | collective-permute-start | bytes 460808 | tf_op jit(solution)/shard_map/ppermute | solution.py:507
  34.7 1.0 %collective-permute-start.6 = (f32[2,1,16,600]{3,2,1,0:T(8,128)S(1)}, f32[2,1,16,600]{3,2,1,0:T(8,128)S(1)}, u32[]{:S(2)}, u32[]{:S(2)}) collective-permute-start(f32[2,1,16,600]{3,2,1,0:T(8,128)S(1)} %fusion), channel_id=1, source_target_pairs={{0,2},{1,3},{2,0},{3,1},{4,6},{5,7},{6,4},{7,5},{8,10},{9,11},{10,... | collective-permute-start | bytes 230408 | tf_op jit(solution)/shard_map/ppermute | solution.py:505
  35.7 0.0 collective-permute-done.3
  35.8 1.2 %collective-permute-start.4 = (f32[2,1,16,600]{3,2,1,0:T(8,128)S(1)}, f32[2,1,16,600]{3,2,1,0:T(8,128)S(1)}, u32[]{:S(2)}, u32[]{:S(2)}) collective-permute-start(f32[2,1,16,600]{3,2,1,0:T(8,128)S(1)} %fusion.1), channel_id=1, source_target_pairs={{0,2},{1,3},{2,0},{3,1},{4,6},{5,7},{6,4},{7,5},{8,10},{9,11},{10,... | collective-permute-start | bytes 230408 | tf_op jit(solution)/shard_map/ppermute | solution.py:505
  36.9 3.0 %collective-permute-done.6.refs_1_ = f32[2,1,16,600]{3,2,1,0:T(8,128)S(1)} collective-permute-done((f32[2,1,16,600]{3,2,1,0:T(8,128)S(1)}, f32[2,1,16,600]{3,2,1,0:T(8,128)S(1)}, u32[]{:S(2)}, u32[]{:S(2)}) %collective-permute-start.6) | collective-permute-done | bytes 76832 | tf_op jit(solution)/shard_map/ppermute | solution.py:505
  39.9 1.1 %collective-permute-done.4.refs_0_ = f32[2,1,16,600]{3,2,1,0:T(8,128)S(1)} collective-permute-done((f32[2,1,16,600]{3,2,1,0:T(8,128)S(1)}, f32[2,1,16,600]{3,2,1,0:T(8,128)S(1)}, u32[]{:S(2)}, u32[]{:S(2)}) %collective-permute-start.4) | collective-permute-done | bytes 76832 | tf_op jit(solution)/shard_map/ppermute | solution.py:505
  41.0 0.7 %total.1 = f32[2,2,16,600]{3,2,1,0:T(8,128)} custom-call(f32[1,2,2,16,600]{4,3,2,1,0:T(8,128)S(1)} %get-tuple-element.37.home_ref, f32[1,2,2,16,600]{4,3,2,1,0:T(8,128)S(1)} %collective-permute-done.2.away_ref, f32[2,1,16,600]{3,2,1,0:T(8,128)S(1)} %collective-permute-done.4.refs_0_, f32[2,1,16,600]{3,2,1,0:T(8,128)S(1)} %collective-permute-done.6.refs_1_), custom_call_target="tpu_custom_call" | custom-call | tf_op jit(solution)/shard_map/total/pallas_call | solution.py:509
  (7 shorter events, 0.0 us)
Async XLA Ops:
  3.0 21.2 %copy-start = (s32[256]{0:T(256)S(1)}, s32[256]{0:T(256)}, u32[]{:S(2)}) copy-start(s32[256]{0:T(256)} %param.8) | copy-start | bytes 3076
  3.0 21.2 %copy-start.1 = (f32[8]{0:T(128)S(1)}, f32[8]{0:T(128)}, u32[]{:S(2)}) copy-start(f32[8]{0:T(128)} %rates_ref.3) | copy-start | bytes 100
  20.0 12.2 %all-to-all-start.1 = ((f32[8,2,2,8,256]{4,3,2,1,0:T(8,128)}), f32[8,2,2,8,256]{4,3,2,1,0:T(8,128)S(1)}, u32[]{:S(2)}, u32[]{:S(2)}) async-start(f32[8,2,2,8,256]{4,3,2,1,0:T(8,128)} %middle.1), calls=%async_computation.1 | async-start | bytes 524288 | tf_op jit(solution)/shard_map/all_to_all | solution.py:488
  23.6 4.8 %collective-permute-start = (f32[5,24,128]{2,1,0:T(8,128)S(1)}, f32[5,24,128]{2,1,0:T(8,128)S(1)}, u32[]{:S(2)}, u32[]{:S(2)}) collective-permute-start(f32[5,24,128]{2,1,0:T(8,128)S(1)} %get-tuple-element.33.own_inner_ref), channel_id=1, source_target_pairs={{0,1},{1,0},{2,3},{3,2},{4,5},{5,4},{6,7},{7,6},{8,9},{9,8},{10,11... | collective-permute-start | bytes 184328 | tf_op jit(solution)/shard_map/ppermute | solution.py:492
  23.6 4.8 %collective-permute-start.1 = (f32[5,24,128]{2,1,0:T(8,128)S(1)}, f32[5,24,128]{2,1,0:T(8,128)S(1)}, u32[]{:S(2)}, u32[]{:S(2)}) collective-permute-start(f32[5,24,128]{2,1,0:T(8,128)S(1)} %get-tuple-element.34.own_outer_ref), channel_id=1, source_target_pairs={{1,2},{2,1},{5,6},{6,5},{9,10},{10,9},{13,14},{14,13},{17,18},{18,... | collective-permute-start | bytes 184328 | tf_op jit(solution)/shard_map/ppermute | solution.py:491
  32.5 2.2 %collective-permute-start.5 = (f32[1,2,1,16,600]{4,3,1,2,0:T(8,128)S(1)}, f32[1,2,1,16,600]{4,3,1,2,0:T(8,128)S(1)}, u32[]{:S(2)}, u32[]{:S(2)}) collective-permute-start(f32[1,2,1,16,600]{4,3,1,2,0:T(8,128)S(1)} %bitcast.19), channel_id=1, source_target_pairs={{0,1},{1,0},{2,3},{3,2},{4,5},{5,4},{6,7},{7,6},{8,9},{9,8},{10,11... | collective-permute-start | bytes 230408 | tf_op jit(solution)/shard_map/ppermute | solution.py:500
  33.5 2.2 %collective-permute-start.3 = (f32[1,2,1,16,600]{4,3,1,2,0:T(8,128)S(1)}, f32[1,2,1,16,600]{4,3,1,2,0:T(8,128)S(1)}, u32[]{:S(2)}, u32[]{:S(2)}) collective-permute-start(f32[1,2,1,16,600]{4,3,1,2,0:T(8,128)S(1)} %bitcast.18), channel_id=1, source_target_pairs={{0,1},{1,0},{2,3},{3,2},{4,5},{5,4},{6,7},{7,6},{8,9},{9,8},{10,11... | collective-permute-start | bytes 230408 | tf_op jit(solution)/shard_map/ppermute | solution.py:500
  34.2 6.8 %collective-permute-start.2 = (f32[1,2,2,16,600]{4,3,2,1,0:T(8,128)S(1)}, f32[1,2,2,16,600]{4,3,2,1,0:T(8,128)S(1)}, u32[]{:S(2)}, u32[]{:S(2)}) collective-permute-start(f32[1,2,2,16,600]{4,3,2,1,0:T(8,128)S(1)} %get-tuple-element.38), channel_id=1, source_target_pairs={{0,1},{1,0},{2,3},{3,2},{4,5},{5,4},{6,7},{7,6},{8,9},{9,8},{10,11... | collective-permute-start | bytes 460808 | tf_op jit(solution)/shard_map/ppermute | solution.py:507
  34.7 5.1 %collective-permute-start.6 = (f32[2,1,16,600]{3,2,1,0:T(8,128)S(1)}, f32[2,1,16,600]{3,2,1,0:T(8,128)S(1)}, u32[]{:S(2)}, u32[]{:S(2)}) collective-permute-start(f32[2,1,16,600]{3,2,1,0:T(8,128)S(1)} %fusion), channel_id=1, source_target_pairs={{0,2},{1,3},{2,0},{3,1},{4,6},{5,7},{6,4},{7,5},{8,10},{9,11},{10,... | collective-permute-start | bytes 230408 | tf_op jit(solution)/shard_map/ppermute | solution.py:505
  35.8 5.3 %collective-permute-start.4 = (f32[2,1,16,600]{3,2,1,0:T(8,128)S(1)}, f32[2,1,16,600]{3,2,1,0:T(8,128)S(1)}, u32[]{:S(2)}, u32[]{:S(2)}) collective-permute-start(f32[2,1,16,600]{3,2,1,0:T(8,128)S(1)} %fusion.1), channel_id=1, source_target_pairs={{0,2},{1,3},{2,0},{3,1},{4,6},{5,7},{6,4},{7,5},{8,10},{9,11},{10,... | collective-permute-start | bytes 230408 | tf_op jit(solution)/shard_map/ppermute | solution.py:505

commit v3 on v2

--- a/solution.py
+++ b/solution.py
@@ -20,7 +20,6 @@
 
 
 VMEM_SPEC = pl.BlockSpec(memory_space=pltpu.VMEM)
-SMEM_SPEC = pl.BlockSpec(memory_space=pltpu.SMEM)
 HBM_SPEC = pl.BlockSpec(memory_space=pltpu.HBM)
 
 
@@ -65,7 +64,7 @@
 
 
 def adjoint_kernel(
-    v_hbm, f_hbm, band_hbm, rates_hbm, cut_hbm, out_ref, inner_ref, outer_ref, cutoff_ref,
+    v_hbm, f_hbm, band_hbm, rates_hbm, cut_hbm, out_ref, inner_ref, outer_ref, cutoff_ref, spread_ref,
     v_ref, f_ref, band_ref, rates_ref, cut_ref, v_sem, f_sem, small_sem,
 ):
     shards, _, held, rows, cells = out_ref.shape
@@ -119,6 +118,7 @@
     for copy in small:
         copy.wait()
     rates = rates_of(band_ref, rates_ref)
+    spread_ref[...] = jnp.broadcast_to(rates, spread_ref.shape)
     for ref, at in ((inner_ref, 1 - odd), (outer_ref, odd)):
         facing = jnp.where(at == 0, rates[:, :LANES], rates[:, last:])
         ref[2 * held] = jnp.broadcast_to(facing, ref.shape[1:])
@@ -139,12 +139,13 @@
     return pl.pallas_call(
         adjoint_kernel,
         in_specs=[HBM_SPEC] * 5,
-        out_specs=[VMEM_SPEC] * 4,
+        out_specs=[VMEM_SPEC] * 5,
         out_shape=[
             jax.ShapeDtypeStruct(out, jnp.float32),
             edge,
             edge,
             jax.ShapeDtypeStruct((cols // shards, LANES), jnp.int32),
+            jax.ShapeDtypeStruct((ROWS, cells), jnp.float32),
         ],
         scratch_shapes=[
             pltpu.VMEM(columns.shape, jnp.float32),
@@ -262,14 +263,14 @@
     return tile
 
 
-def smooth_kernel(f_hbm, band_ref, rates_ref, high_ref, low_ref, near_ref, f_ref, a_both, f_sem):
+def smooth_kernel(f_hbm, rates_ref, high_ref, low_ref, near_ref, f_ref, a_both, f_sem):
     _, held, _, cells = f_hbm.shape
     copies = []
     for at in range(2 * held):
         c, k = divmod(at, held)
         copies.append(pltpu.make_async_copy(f_hbm.at[c, k], f_ref.at[c, k], f_sem.at[at]))
         copies[at].start()
-    diagonals = diagonals_of(jnp.concatenate([rates_of(band_ref, rates_ref), jnp.zeros((1, LANES), jnp.float32)], axis=1))
+    diagonals = diagonals_of(jnp.concatenate([rates_ref[:1], jnp.zeros((1, LANES), jnp.float32)], axis=1))
     for lanes in range(0, cells, LANES):
         column = lax.broadcasted_iota(jnp.int32, (LANES, LANES), 1)
         row = lax.broadcasted_iota(jnp.int32, (LANES, LANES), 0)
@@ -290,12 +291,12 @@
         near_ref[c, k, NEAR:] = total[cells - NEAR :]
 
 
-def smooth(blocks, band_index, band_rates):
+def smooth(blocks, rates):
     _, held, sensors, cells = blocks.shape
     shape = jax.ShapeDtypeStruct((2, held, cells, sensors), jnp.bfloat16)
     return pl.pallas_call(
         smooth_kernel,
-        in_specs=[HBM_SPEC, VMEM_SPEC, SMEM_SPEC],
+        in_specs=[HBM_SPEC, VMEM_SPEC],
         out_specs=[VMEM_SPEC] * 3,
         out_shape=[shape, shape, jax.ShapeDtypeStruct((2, held, 2 * NEAR, sensors), jnp.float32)],
         scratch_shapes=[
@@ -308,15 +309,15 @@
             flops=12 * held * sensors * cells * cells, bytes_accessed=16 * held * sensors * cells, transcendentals=0
         ),
         name="smooth",
-    )(blocks, band_index.reshape(1, cells), band_rates)
+    )(blocks, rates)
 
 
 def near_kernel(
-    near_ref, own_inner_ref, own_outer_ref, inner_ref, outer_ref, band_ref, rates_ref, high_ref, low_ref, sides
+    near_ref, own_inner_ref, own_outer_ref, inner_ref, outer_ref, rates_ref, high_ref, low_ref, sides
 ):
     held = near_ref.shape[1]
     sensors = near_ref.shape[3]
-    cells = band_ref.shape[1]
+    cells = rates_ref.shape[1]
     even = lax.axis_index("cell") % 2 == 0
     kinds = 4
     per = kinds * SWEEPS
@@ -335,7 +336,7 @@
     lane = lax.broadcasted_iota(jnp.int32, (ROWS, LANES), 1)
     _, _, after, before = parts(2 * held, slice(0, ROWS))
     side = jnp.where(lane < SWEEPS, after, jnp.where(lane >= LANES - SWEEPS, before, 0.0))[:1]
-    own = rates_of(band_ref, rates_ref)
+    own = rates_ref[:1]
     alone = diagonals_of(jnp.concatenate([own, jnp.zeros((1, LANES), jnp.float32)], axis=1))
     full = diagonals_of(jnp.concatenate([own, side], axis=1))
     first = full[:, :LANES] - alone[:, :LANES]
@@ -388,12 +389,12 @@
             low_ref[c, k] = low
 
 
-def near_edges(near, own_inner, own_outer, inner, outer, band_index, band_rates):
+def near_edges(near, own_inner, own_outer, inner, outer, rates):
     shape = jax.ShapeDtypeStruct(near.shape, jnp.bfloat16)
     held, sensors = near.shape[1], near.shape[3]
     return pl.pallas_call(
         near_kernel,
-        in_specs=[VMEM_SPEC] * 6 + [SMEM_SPEC],
+        in_specs=[VMEM_SPEC] * 6,
         out_specs=[VMEM_SPEC] * 2,
         out_shape=[shape, shape],
         scratch_shapes=[pltpu.VMEM((sensors, LANES), jnp.float32)],
@@ -402,7 +403,7 @@
             flops=24 * held * sensors * NEAR * LANES, bytes_accessed=8 * near.size, transcendentals=0
         ),
         name="near_edges",
-    )(near, own_inner, own_outer, inner, outer, band_index.reshape(1, -1), band_rates)
+    )(near, own_inner, own_outer, inner, outer, rates)
 
 
 def forward_kernel(
@@ -476,7 +477,7 @@
     chips = strips // 2
     held = columns.shape[1]
     columns, blocks = in_hbm(columns), in_hbm(freq_blocks)
-    spectrum, own_inner, own_outer, cutoff = adjoint(
+    spectrum, own_inner, own_outer, cutoff, rates = adjoint(
         columns, blocks, band_index, band_rates, causal_cutoffs, shards
     )
     gathered = lax.all_to_all(spectrum, "freq", split_axis=0, concat_axis=0, tiled=True)
@@ -490,8 +491,8 @@
     pairs = [(i, i + 1) for i in range(1, strips - 1, 2)]
     outer = lax.ppermute(own_outer, "cell", pairs + [(j, i) for i, j in pairs])
     inner = lax.ppermute(own_inner, "cell", swap)
-    high, low, near = smooth(blocks, band_index, band_rates)
-    near = near_edges(near, own_inner, own_outer, inner, outer, band_index, band_rates)
+    high, low, near = smooth(blocks, rates)
+    near = near_edges(near, own_inner, own_outer, inner, outer, rates)
     matrices = (high, low, *near)
     leaving = []
     if chips > 1:

time: 42 us -> 41.8 us (level)
  waiting for transfers between devices: 6.35 us -> 7.85 us
  Pallas kernels: 11.5 us -> 10.4 us
  starting transfers between devices: 7.72 us -> 7.13 us
    all_to_all x1, waiting for transfers between devices: 2.25 us -> 3.36 us  [on_device(): lax.all_to_all(spectrum, 'freq', split_axis=0, concat_axis=0, tiled=True)]
    pallas_call x2, Pallas kernels: 5.58 us -> 4.49 us  [the longest x1 3.56 us: smooth(): pl.pallas_call(smooth_kernel, in_specs=[HBM_SPEC, VMEM_SPEC], out_specs=[...]
    ppermute x1, starting transfers between devices: 0.56 us -> 0.08 us  [on_device(): away = lax.ppermute(away, 'cell', swap)]
  transfers between devices with their start and end apart: 8 -> 8, of which waited for: 3 -> 3; matrix products, arithmetic and copies ran while one was open for 0% -> 0% of each run, Pallas kernels for 16% -> 13%
where the time goes in v3:
time: 41.8 us; the launch traced here: 41.5 us
  blocking collectives  16 us (38%)
  Pallas kernels  10.4 us (25%)
  waiting for transfers between devices  7.85 us (19%)
  starting transfers between devices  7.13 us (17%)
    all_to_all x1, blocking collectives, on_device(): lax.all_to_all(spectrum, 'freq', split_axis=0, concat_axis=0, tiled=True)  16 us
    ppermute x2, waiting for transfers between devices, on_device(): arrived.append(lax.ppermute(leaving[k][s - 1], 'cell', pairs))  4.48 us
    all_to_all x1, starting transfers between devices, on_device(): lax.all_to_all(spectrum, 'freq', split_axis=0, concat_axis=0, tiled=True)  3.6 us
    pallas_call x1, Pallas kernels, smooth(): pl.pallas_call(smooth_kernel, in_specs=[HBM_SPEC, VMEM_SPEC], out_specs=[...  3.56 us
    all_to_all x1, waiting for transfers between devices, on_device(): lax.all_to_all(spectrum, 'freq', split_axis=0, concat_axis=0, tiled=True)  3.36 us
    pallas_call x1, Pallas kernels, adjoint(): pl.pallas_call(adjoint_kernel, in_specs=[HBM_SPEC] * 5, out_specs=[VMEM_S...  3.03 us
    ppermute x2, starting transfers between devices, on_device(): arrived.append(lax.ppermute(leaving[k][s - 1], 'cell', pairs))  2.16 us
    pallas_call x3, Pallas kernels, forward(): pl.pallas_call(functools.partial(forward_kernel, steps, chips, wanted), i...  1.24 us
  transfers between devices with their start and end apart: 8, of which 3 were waited for; matrix products, arithmetic and copies ran while one was open for 0% of the time, Pallas kernels for 13%

profile of v3, /device:TPU:0, one launch (start us, length us, event | category | flops | bytes accessed | tf_op | source)
XLA Modules:
  0.0 41.5 jit_solution(13787148861991800202)
XLA Ops:
  0.0 3.0 %adjoint.1 = (f32[8,2,2,8,256]{4,3,2,1,0:T(8,128)S(1)}, f32[5,24,128]{2,1,0:T(8,128)S(1)}, f32[5,24,128]{2,1,0:T(8,128)S(1)}, s32[8,128]{1,0:T(8,128)S(1)}, f32[8,256]{1,0:T(8,128)S(1)}) custom-call(f32[2,2,64,600]{3,2,1,0:T(8,128)} %v_hbm.1, f32[2,2,600,256]{3,2,1,0:T(8,128)} %f_hbm.2, s32[1,256]{1,0:T(1,128)} %bitcast.17, f32[8]{0:T(128)} %rates_hbm.1, ...), custom_call_target="tpu_custom_call" | custom-call | flops 471859200 | bytes 2457600 | tf_op jit(solution)/shard_map/adjoint/pallas_call | solution.py:139
  3.0 16.0 %all_to_all.10.x_ref = f32[8,2,2,8,256]{4,3,2,1,0:T(8,128)S(1)} all-to-all(f32[8,2,2,8,256]{4,3,2,1,0:T(8,128)S(1)} %get-tuple-element.25), channel_id=1, replica_groups=mesh['freq'=8,'cell'=4] {'freq'}, dimensions={0} | all-to-all | bytes 524288 | tf_op jit(solution)/shard_map/all_to_all | solution.py:483
  19.1 0.9 %middle.1 = f32[8,2,2,8,256]{4,3,2,1,0:T(8,128)} custom-call(f32[8,2,2,8,256]{4,3,2,1,0:T(8,128)S(1)} %all_to_all.10.x_ref, s32[8,128]{1,0:T(8,128)S(1)} %get-tuple-element.26.cutoff_ref), custom_call_target="tpu_custom_call" | custom-call | flops 3932160 | bytes 524288 | tf_op jit(solution)/shard_map/middle/pallas_call | solution.py:224
  20.0 3.6 %all-to-all-start.1 = ((f32[8,2,2,8,256]{4,3,2,1,0:T(8,128)}), f32[8,2,2,8,256]{4,3,2,1,0:T(8,128)S(1)}, u32[]{:S(2)}, u32[]{:S(2)}) async-start(f32[8,2,2,8,256]{4,3,2,1,0:T(8,128)} %middle.1), calls=%async_computation.1 | async-start | bytes 524288 | tf_op jit(solution)/shard_map/all_to_all | solution.py:489
  23.6 0.0 collective-permute-start
  23.6 0.7 %collective-permute-start.1 = (f32[5,24,128]{2,1,0:T(8,128)S(1)}, f32[5,24,128]{2,1,0:T(8,128)S(1)}, u32[]{:S(2)}, u32[]{:S(2)}) collective-permute-start(f32[5,24,128]{2,1,0:T(8,128)S(1)} %get-tuple-element.36.own_outer_ref), channel_id=1, source_target_pairs={{1,2},{2,1},{5,6},{6,5},{9,10},{10,9},{13,14},{14,13},{17,18},{18,... | collective-permute-start | bytes 184328 | tf_op jit(solution)/shard_map/ppermute | solution.py:492
  24.3 3.6 %smooth.1 = (bf16[2,2,256,600]{3,2,1,0:T(8,128)(2,1)S(1)}, bf16[2,2,256,600]{3,2,1,0:T(8,128)(2,1)S(1)}, f32[2,2,32,600]{3,2,1,0:T(8,128)S(1)}) custom-call(f32[2,2,600,256]{3,2,1,0:T(8,128)} %f_hbm.2, f32[8,256]{1,0:T(8,128)S(1)} %get-tuple-element.31.rates_ref), custom_call_target="tpu_custom_call" | custom-call | flops 943718400 | bytes 4915200 | tf_op jit(solution)/shard_map/smooth/pallas_call | solution.py:297
  27.8 0.0 collective-permute-done.inner_ref
  27.8 0.0 collective-permute-done.1.outer_ref
  27.9 0.9 %near_edges.1 = (bf16[2,2,32,600]{3,2,1,0:T(8,128)(2,1)S(1)}, bf16[2,2,32,600]{3,2,1,0:T(8,128)(2,1)S(1)}) custom-call(f32[2,2,32,600]{3,2,1,0:T(8,128)S(1)} %get-tuple-element.34.near_ref, f32[5,24,128]{2,1,0:T(8,128)S(1)} %get-tuple-element.35.own_inner_ref, f32[5,24,128]{2,1,0:T(8,128)S(1)} %get-tuple-element.36.own_outer_ref, ...), custom_call_target="tpu_custom_call" | custom-call | flops 58982400 | bytes 614400 | tf_op jit(solution)/shard_map/near_edges/pallas_call | solution.py:395
  28.8 3.4 %all-to-all-done.1.x_ref = f32[8,2,2,8,256]{4,3,2,1,0:T(8,128)S(1)} async-done(((f32[8,2,2,8,256]{4,3,2,1,0:T(8,128)}), f32[8,2,2,8,256]{4,3,2,1,0:T(8,128)S(1)}, u32[]{:S(2)}, u32[]{:S(2)}) %all-to-all-start.1) | async-done | bytes 262176 | tf_op jit(solution)/shard_map/all_to_all | solution.py:489
  32.1 0.3 shard_map.57
  32.5 0.1 collective-permute-start.5
  32.6 0.3 shard_map.56
  32.9 0.6 %collective-permute-start.3 = (f32[1,2,1,16,600]{4,3,1,2,0:T(8,128)S(1)}, f32[1,2,1,16,600]{4,3,1,2,0:T(8,128)S(1)}, u32[]{:S(2)}, u32[]{:S(2)}) collective-permute-start(f32[1,2,1,16,600]{4,3,1,2,0:T(8,128)S(1)} %bitcast.15), channel_id=1, source_target_pairs={{0,1},{1,0},{2,3},{3,2},{4,5},{5,4},{6,7},{7,6},{8,9},{9,8},{10,11... | collective-permute-start | bytes 230408 | tf_op jit(solution)/shard_map/ppermute | solution.py:501
  33.5 0.6 %shard_map.55 = (f32[1,2,2,16,600]{4,3,2,1,0:T(8,128)S(1)}, f32[1,2,2,16,600]{4,3,2,1,0:T(8,128)S(1)}) custom-call(f32[8,2,2,8,256]{4,3,2,1,0:T(8,128)S(1)} %all-to-all-done.1.x_ref, bf16[2,2,256,600]{3,2,1,0:T(8,128)(2,1)S(1)} %get-tuple-element.32.high_ref, bf16[2,2,256,600]{3,2,1,0:T(8,128)(2,1)S(1)} %get-tuple-element.33.low_ref, ...), custom_call_target="tpu_custom_call" | custom-call | flops 235929600 | bytes 2457600 | tf_op jit(solution)/shard_map/pallas_call | solution.py:451
  34.0 0.1 collective-permute-start.2
  34.2 1.6 %collective-permute-start.6 = (f32[2,1,16,600]{3,2,1,0:T(8,128)S(1)}, f32[2,1,16,600]{3,2,1,0:T(8,128)S(1)}, u32[]{:S(2)}, u32[]{:S(2)}) collective-permute-start(f32[2,1,16,600]{3,2,1,0:T(8,128)S(1)} %fusion), channel_id=1, source_target_pairs={{0,2},{1,3},{2,0},{3,1},{4,6},{5,7},{6,4},{7,5},{8,10},{9,11},{10,... | collective-permute-start | bytes 230408 | tf_op jit(solution)/shard_map/ppermute | solution.py:506
  35.7 0.0 collective-permute-done.3
  35.7 0.6 %collective-permute-start.4 = (f32[2,1,16,600]{3,2,1,0:T(8,128)S(1)}, f32[2,1,16,600]{3,2,1,0:T(8,128)S(1)}, u32[]{:S(2)}, u32[]{:S(2)}) collective-permute-start(f32[2,1,16,600]{3,2,1,0:T(8,128)S(1)} %fusion.1), channel_id=1, source_target_pairs={{0,2},{1,3},{2,0},{3,1},{4,6},{5,7},{6,4},{7,5},{8,10},{9,11},{10,... | collective-permute-start | bytes 230408 | tf_op jit(solution)/shard_map/ppermute | solution.py:506
  36.3 3.2 %collective-permute-done.6.refs_1_ = f32[2,1,16,600]{3,2,1,0:T(8,128)S(1)} collective-permute-done((f32[2,1,16,600]{3,2,1,0:T(8,128)S(1)}, f32[2,1,16,600]{3,2,1,0:T(8,128)S(1)}, u32[]{:S(2)}, u32[]{:S(2)}) %collective-permute-start.6) | collective-permute-done | bytes 76832 | tf_op jit(solution)/shard_map/ppermute | solution.py:506
  39.5 1.3 %collective-permute-done.4.refs_0_ = f32[2,1,16,600]{3,2,1,0:T(8,128)S(1)} collective-permute-done((f32[2,1,16,600]{3,2,1,0:T(8,128)S(1)}, f32[2,1,16,600]{3,2,1,0:T(8,128)S(1)}, u32[]{:S(2)}, u32[]{:S(2)}) %collective-permute-start.4) | collective-permute-done | bytes 76832 | tf_op jit(solution)/shard_map/ppermute | solution.py:506
  40.8 0.0 collective-permute-done.2.away_ref
  40.8 0.7 %total.1 = f32[2,2,16,600]{3,2,1,0:T(8,128)} custom-call(f32[1,2,2,16,600]{4,3,2,1,0:T(8,128)S(1)} %get-tuple-element.39.home_ref, f32[1,2,2,16,600]{4,3,2,1,0:T(8,128)S(1)} %collective-permute-done.2.away_ref, f32[2,1,16,600]{3,2,1,0:T(8,128)S(1)} %collective-permute-done.4.refs_0_, f32[2,1,16,600]{3,2,1,0:T(8,128)S(1)} %collective-permute-done.6.refs_1_), custom_call_target="tpu_custom_call" | custom-call | tf_op jit(solution)/shard_map/total/pallas_call | solution.py:510
  (3 shorter events, 0.0 us)
Async XLA Ops:
  20.0 12.2 %all-to-all-start.1 = ((f32[8,2,2,8,256]{4,3,2,1,0:T(8,128)}), f32[8,2,2,8,256]{4,3,2,1,0:T(8,128)S(1)}, u32[]{:S(2)}, u32[]{:S(2)}) async-start(f32[8,2,2,8,256]{4,3,2,1,0:T(8,128)} %middle.1), calls=%async_computation.1 | async-start | bytes 524288 | tf_op jit(solution)/shard_map/all_to_all | solution.py:489
  23.6 4.3 %collective-permute-start = (f32[5,24,128]{2,1,0:T(8,128)S(1)}, f32[5,24,128]{2,1,0:T(8,128)S(1)}, u32[]{:S(2)}, u32[]{:S(2)}) collective-permute-start(f32[5,24,128]{2,1,0:T(8,128)S(1)} %get-tuple-element.35.own_inner_ref), channel_id=1, source_target_pairs={{0,1},{1,0},{2,3},{3,2},{4,5},{5,4},{6,7},{7,6},{8,9},{9,8},{10,11... | collective-permute-start | bytes 184328 | tf_op jit(solution)/shard_map/ppermute | solution.py:493
  23.6 4.3 %collective-permute-start.1 = (f32[5,24,128]{2,1,0:T(8,128)S(1)}, f32[5,24,128]{2,1,0:T(8,128)S(1)}, u32[]{:S(2)}, u32[]{:S(2)}) collective-permute-start(f32[5,24,128]{2,1,0:T(8,128)S(1)} %get-tuple-element.36.own_outer_ref), channel_id=1, source_target_pairs={{1,2},{2,1},{5,6},{6,5},{9,10},{10,9},{13,14},{14,13},{17,18},{18,... | collective-permute-start | bytes 184328 | tf_op jit(solution)/shard_map/ppermute | solution.py:492
  32.5 1.6 %collective-permute-start.5 = (f32[1,2,1,16,600]{4,3,1,2,0:T(8,128)S(1)}, f32[1,2,1,16,600]{4,3,1,2,0:T(8,128)S(1)}, u32[]{:S(2)}, u32[]{:S(2)}) collective-permute-start(f32[1,2,1,16,600]{4,3,1,2,0:T(8,128)S(1)} %bitcast.16), channel_id=1, source_target_pairs={{0,1},{1,0},{2,3},{3,2},{4,5},{5,4},{6,7},{7,6},{8,9},{9,8},{10,11... | collective-permute-start | bytes 230408 | tf_op jit(solution)/shard_map/ppermute | solution.py:501
  32.9 2.8 %collective-permute-start.3 = (f32[1,2,1,16,600]{4,3,1,2,0:T(8,128)S(1)}, f32[1,2,1,16,600]{4,3,1,2,0:T(8,128)S(1)}, u32[]{:S(2)}, u32[]{:S(2)}) collective-permute-start(f32[1,2,1,16,600]{4,3,1,2,0:T(8,128)S(1)} %bitcast.15), channel_id=1, source_target_pairs={{0,1},{1,0},{2,3},{3,2},{4,5},{5,4},{6,7},{7,6},{8,9},{9,8},{10,11... | collective-permute-start | bytes 230408 | tf_op jit(solution)/shard_map/ppermute | solution.py:501
  34.0 6.8 %collective-permute-start.2 = (f32[1,2,2,16,600]{4,3,2,1,0:T(8,128)S(1)}, f32[1,2,2,16,600]{4,3,2,1,0:T(8,128)S(1)}, u32[]{:S(2)}, u32[]{:S(2)}) collective-permute-start(f32[1,2,2,16,600]{4,3,2,1,0:T(8,128)S(1)} %get-tuple-element.40), channel_id=1, source_target_pairs={{0,1},{1,0},{2,3},{3,2},{4,5},{5,4},{6,7},{7,6},{8,9},{9,8},{10,11... | collective-permute-start | bytes 460808 | tf_op jit(solution)/shard_map/ppermute | solution.py:508
  34.2 5.4 %collective-permute-start.6 = (f32[2,1,16,600]{3,2,1,0:T(8,128)S(1)}, f32[2,1,16,600]{3,2,1,0:T(8,128)S(1)}, u32[]{:S(2)}, u32[]{:S(2)}) collective-permute-start(f32[2,1,16,600]{3,2,1,0:T(8,128)S(1)} %fusion), channel_id=1, source_target_pairs={{0,2},{1,3},{2,0},{3,1},{4,6},{5,7},{6,4},{7,5},{8,10},{9,11},{10,... | collective-permute-start | bytes 230408 | tf_op jit(solution)/shard_map/ppermute | solution.py:506
  35.7 5.1 %collective-permute-start.4 = (f32[2,1,16,600]{3,2,1,0:T(8,128)S(1)}, f32[2,1,16,600]{3,2,1,0:T(8,128)S(1)}, u32[]{:S(2)}, u32[]{:S(2)}) collective-permute-start(f32[2,1,16,600]{3,2,1,0:T(8,128)S(1)} %fusion.1), channel_id=1, source_target_pairs={{0,2},{1,3},{2,0},{3,1},{4,6},{5,7},{6,4},{7,5},{8,10},{9,11},{10,... | collective-permute-start | bytes 230408 | tf_op jit(solution)/shard_map/ppermute | solution.py:506

commit v4 on v3

--- a/solution.py
+++ b/solution.py
@@ -61,6 +61,10 @@
     for b in range(BANDS):
         rates = jnp.where(band == b, rates_ref[b], rates)
     return rates
+
+
+def packed_of(sensors):
+    return -(-sensors // (ROWS * GROUPS)) * ROWS
 
 
 def adjoint_kernel(
@@ -86,6 +90,7 @@
     inner_at, inner_shift = pl.multiple_of((1 - odd) * last, LANES), (1 - odd) * SWEEPS
     outer_at, outer_shift = pl.multiple_of(odd * last, LANES), odd * SWEEPS
     lane_group = lax.broadcasted_iota(jnp.int32, (ROWS, LANES), 1) // SWEEPS
+    packed_rows = packed_of(sensors)
 
     def edge(at, block):
         for ref, lanes, shift in ((inner_ref, inner_at, inner_shift), (outer_ref, outer_at, outer_shift)):
@@ -96,11 +101,12 @@
                     cells_there = block[rows_at : rows_at + ROWS, pl.ds(lanes, LANES)]
                     moved = pltpu.roll(cells_there, group * SWEEPS + shift, 1)
                     packed = jnp.where(lane_group == group, moved, packed)
-                ref[at, first // GROUPS : first // GROUPS + ROWS] = packed
-
+                place = at * packed_rows + first // GROUPS
+                ref[place : place + ROWS] = packed
+
+    for copy in v_copies + f_copies:
+        copy.wait()
     for k in range(held):
-        for copy in (v_copies[k], f_copies[2 * k], f_copies[2 * k + 1]):
-            copy.wait()
         high, low = split(v_ref[:, k].reshape(2 * cols, sensors))
         parts = jnp.concatenate([high, low], axis=0)
         sums = []
@@ -121,7 +127,7 @@
     spread_ref[...] = jnp.broadcast_to(rates, spread_ref.shape)
     for ref, at in ((inner_ref, 1 - odd), (outer_ref, odd)):
         facing = jnp.where(at == 0, rates[:, :LANES], rates[:, last:])
-        ref[2 * held] = jnp.broadcast_to(facing, ref.shape[1:])
+        ref[2 * held * packed_rows :] = jnp.broadcast_to(facing, (ROWS, LANES))
     base = lax.axis_index("freq") * rows
     row = lax.broadcasted_iota(jnp.int32, (rows, LANES), 0)
     cutoff = jnp.zeros((rows, LANES), jnp.int32)
@@ -134,8 +140,7 @@
     _, held, cols, sensors = columns.shape
     cells = blocks.shape[3]
     out = (shards, 2, held, cols // shards, cells)
-    packed = -(-sensors // (ROWS * GROUPS)) * ROWS
-    edge = jax.ShapeDtypeStruct((2 * held + 1, packed, LANES), jnp.float32)
+    edge = jax.ShapeDtypeStruct((2 * held * packed_of(sensors) + ROWS, LANES), jnp.float32)
     return pl.pallas_call(
         adjoint_kernel,
         in_specs=[HBM_SPEC] * 5,
@@ -323,9 +328,10 @@
     per = kinds * SWEEPS
     pairs = LANES // (2 * per)
 
-    def parts(at, rows):
-        own_inner, own_outer = own_inner_ref[at, rows], own_outer_ref[at, rows]
-        inner, outer = inner_ref[at, rows], outer_ref[at, rows]
+    def parts(first):
+        rows = slice(first, first + ROWS)
+        own_inner, own_outer = own_inner_ref[rows], own_outer_ref[rows]
+        inner, outer = inner_ref[rows], outer_ref[rows]
         return (
             jnp.where(even, own_outer, own_inner),
             jnp.where(even, own_inner, own_outer),
@@ -334,7 +340,8 @@
         )
 
     lane = lax.broadcasted_iota(jnp.int32, (ROWS, LANES), 1)
-    _, _, after, before = parts(2 * held, slice(0, ROWS))
+    packed_rows = packed_of(sensors)
+    _, _, after, before = parts(2 * held * packed_rows)
     side = jnp.where(lane < SWEEPS, after, jnp.where(lane >= LANES - SWEEPS, before, 0.0))[:1]
     own = rates_ref[:1]
     alone = diagonals_of(jnp.concatenate([own, jnp.zeros((1, LANES), jnp.float32)], axis=1))
@@ -362,8 +369,7 @@
     for begin_at in range(0, 2 * held, pairs):
         ats = range(begin_at, min(2 * held, begin_at + pairs))
         for begin in range(0, sensors, ROWS * GROUPS):
-            packed = slice(begin // GROUPS, begin // GROUPS + ROWS)
-            values = [value for at in ats for value in parts(at, packed)]
+            values = [value for at in ats for value in parts(at * packed_rows + begin // GROUPS)]
             values = [pltpu.roll(value, n * SWEEPS, 1) if n else value for n, value in enumerate(values)]
             for group in range(min(GROUPS, (sensors - begin) // ROWS)):
                 tile = jnp.zeros((ROWS, LANES), jnp.float32)

time: 41.8 us -> 41.6 us (level)
  no operation moved by 1% of the time
where the time goes in v4:
time: 41.6 us; the launch traced here: 41.3 us
  blocking collectives  16 us (38%)
  Pallas kernels  10.2 us (25%)
  waiting for transfers between devices  7.87 us (19%)
  starting transfers between devices  7.13 us (17%)
    all_to_all x1, blocking collectives, on_device(): lax.all_to_all(spectrum, 'freq', split_axis=0, concat_axis=0, tiled=True)  16 us
    ppermute x2, waiting for transfers between devices, on_device(): arrived.append(lax.ppermute(leaving[k][s - 1], 'cell', pairs))  4.48 us
    all_to_all x1, starting transfers between devices, on_device(): lax.all_to_all(spectrum, 'freq', split_axis=0, concat_axis=0, tiled=True)  3.6 us
    pallas_call x1, Pallas kernels, smooth(): pl.pallas_call(smooth_kernel, in_specs=[HBM_SPEC, VMEM_SPEC], out_specs=[...  3.55 us
    all_to_all x1, waiting for transfers between devices, on_device(): lax.all_to_all(spectrum, 'freq', split_axis=0, concat_axis=0, tiled=True)  3.38 us
    pallas_call x1, Pallas kernels, adjoint(): pl.pallas_call(adjoint_kernel, in_specs=[HBM_SPEC] * 5, out_specs=[VMEM_S...  2.85 us
    ppermute x2, starting transfers between devices, on_device(): arrived.append(lax.ppermute(leaving[k][s - 1], 'cell', pairs))  2.16 us
    pallas_call x3, Pallas kernels, forward(): pl.pallas_call(functools.partial(forward_kernel, steps, chips, wanted), i...  1.24 us
  transfers between devices with their start and end apart: 8, of which 3 were waited for; matrix products, arithmetic and copies ran while one was open for 0% of the time, Pallas kernels for 13%

profile of v4, /device:TPU:0, one launch (start us, length us, event | category | flops | bytes accessed | tf_op | source)
XLA Modules:
  0.0 41.3 jit_solution(5110596979965195444)
XLA Ops:
  0.0 2.8 %adjoint.1 = (f32[8,2,2,8,256]{4,3,2,1,0:T(8,128)S(1)}, f32[104,128]{1,0:T(8,128)S(1)}, f32[104,128]{1,0:T(8,128)S(1)}, s32[8,128]{1,0:T(8,128)S(1)}, f32[8,256]{1,0:T(8,128)S(1)}) custom-call(f32[2,2,64,600]{3,2,1,0:T(8,128)} %v_hbm.1, f32[2,2,600,256]{3,2,1,0:T(8,128)} %f_hbm.2, s32[1,256]{1,0:T(1,128)} %bitcast.17, f32[8]{0:T(128)} %rates_hbm.1, s32[64]{0:T(128)} %cut_hbm.1), custom_call_target="tpu_custom_call" | custom-call | flops 471859200 | bytes 2457600 | tf_op jit(solution)/shard_map/adjoint/pallas_call | solution.py:144
  2.9 16.0 %all_to_all.10.x_ref = f32[8,2,2,8,256]{4,3,2,1,0:T(8,128)S(1)} all-to-all(f32[8,2,2,8,256]{4,3,2,1,0:T(8,128)S(1)} %get-tuple-element.25), channel_id=1, replica_groups=mesh['freq'=8,'cell'=4] {'freq'}, dimensions={0} | all-to-all | bytes 524288 | tf_op jit(solution)/shard_map/all_to_all | solution.py:489
  18.9 0.9 %middle.1 = f32[8,2,2,8,256]{4,3,2,1,0:T(8,128)} custom-call(f32[8,2,2,8,256]{4,3,2,1,0:T(8,128)S(1)} %all_to_all.10.x_ref, s32[8,128]{1,0:T(8,128)S(1)} %get-tuple-element.26.cutoff_ref), custom_call_target="tpu_custom_call" | custom-call | flops 3932160 | bytes 524288 | tf_op jit(solution)/shard_map/middle/pallas_call | solution.py:229
  19.8 3.6 %all-to-all-start.1 = ((f32[8,2,2,8,256]{4,3,2,1,0:T(8,128)}), f32[8,2,2,8,256]{4,3,2,1,0:T(8,128)S(1)}, u32[]{:S(2)}, u32[]{:S(2)}) async-start(f32[8,2,2,8,256]{4,3,2,1,0:T(8,128)} %middle.1), calls=%async_computation.1 | async-start | bytes 524288 | tf_op jit(solution)/shard_map/all_to_all | solution.py:495
  23.4 0.0 collective-permute-start
  23.4 0.7 %collective-permute-start.1 = (f32[104,128]{1,0:T(8,128)S(1)}, f32[104,128]{1,0:T(8,128)S(1)}, u32[]{:S(2)}, u32[]{:S(2)}) collective-permute-start(f32[104,128]{1,0:T(8,128)S(1)} %get-tuple-element.36.own_outer_ref), channel_id=1, source_target_pairs={{1,2},{2,1},{5,6},{6,5},{9,10},{10,9},{13,14},{14,13},{17,18},{18,... | collective-permute-start | bytes 159752 | tf_op jit(solution)/shard_map/ppermute | solution.py:498
  24.1 3.6 %smooth.1 = (bf16[2,2,256,600]{3,2,1,0:T(8,128)(2,1)S(1)}, bf16[2,2,256,600]{3,2,1,0:T(8,128)(2,1)S(1)}, f32[2,2,32,600]{3,2,1,0:T(8,128)S(1)}) custom-call(f32[2,2,600,256]{3,2,1,0:T(8,128)} %f_hbm.2, f32[8,256]{1,0:T(8,128)S(1)} %get-tuple-element.31.rates_ref), custom_call_target="tpu_custom_call" | custom-call | flops 943718400 | bytes 4915200 | tf_op jit(solution)/shard_map/smooth/pallas_call | solution.py:302
  27.6 0.0 collective-permute-done.inner_ref
  27.6 0.9 %near_edges.1 = (bf16[2,2,32,600]{3,2,1,0:T(8,128)(2,1)S(1)}, bf16[2,2,32,600]{3,2,1,0:T(8,128)(2,1)S(1)}) custom-call(f32[2,2,32,600]{3,2,1,0:T(8,128)S(1)} %get-tuple-element.34.near_ref, f32[104,128]{1,0:T(8,128)S(1)} %get-tuple-element.35.own_inner_ref, f32[104,128]{1,0:T(8,128)S(1)} %get-tuple-element.36.own_outer_ref, ...), custom_call_target="tpu_custom_call" | custom-call | flops 58982400 | bytes 614400 | tf_op jit(solution)/shard_map/near_edges/pallas_call | solution.py:401
  28.6 3.4 %all-to-all-done.1.x_ref = f32[8,2,2,8,256]{4,3,2,1,0:T(8,128)S(1)} async-done(((f32[8,2,2,8,256]{4,3,2,1,0:T(8,128)}), f32[8,2,2,8,256]{4,3,2,1,0:T(8,128)S(1)}, u32[]{:S(2)}, u32[]{:S(2)}) %all-to-all-start.1) | async-done | bytes 262176 | tf_op jit(solution)/shard_map/all_to_all | solution.py:495
  32.0 0.3 shard_map.57
  32.3 0.1 collective-permute-start.5
  32.4 0.3 shard_map.56
  32.7 0.6 %collective-permute-start.3 = (f32[1,2,1,16,600]{4,3,1,2,0:T(8,128)S(1)}, f32[1,2,1,16,600]{4,3,1,2,0:T(8,128)S(1)}, u32[]{:S(2)}, u32[]{:S(2)}) collective-permute-start(f32[1,2,1,16,600]{4,3,1,2,0:T(8,128)S(1)} %bitcast.15), channel_id=1, source_target_pairs={{0,1},{1,0},{2,3},{3,2},{4,5},{5,4},{6,7},{7,6},{8,9},{9,8},{10,11... | collective-permute-start | bytes 230408 | tf_op jit(solution)/shard_map/ppermute | solution.py:507
  33.3 0.6 %shard_map.55 = (f32[1,2,2,16,600]{4,3,2,1,0:T(8,128)S(1)}, f32[1,2,2,16,600]{4,3,2,1,0:T(8,128)S(1)}) custom-call(f32[8,2,2,8,256]{4,3,2,1,0:T(8,128)S(1)} %all-to-all-done.1.x_ref, bf16[2,2,256,600]{3,2,1,0:T(8,128)(2,1)S(1)} %get-tuple-element.32.high_ref, bf16[2,2,256,600]{3,2,1,0:T(8,128)(2,1)S(1)} %get-tuple-element.33.low_ref, ...), custom_call_target="tpu_custom_call" | custom-call | flops 235929600 | bytes 2457600 | tf_op jit(solution)/shard_map/pallas_call | solution.py:457
  33.9 0.1 collective-permute-start.2
  33.9 0.0 collective-permute-done.5
  34.0 1.6 %collective-permute-start.6 = (f32[2,1,16,600]{3,2,1,0:T(8,128)S(1)}, f32[2,1,16,600]{3,2,1,0:T(8,128)S(1)}, u32[]{:S(2)}, u32[]{:S(2)}) collective-permute-start(f32[2,1,16,600]{3,2,1,0:T(8,128)S(1)} %fusion), channel_id=1, source_target_pairs={{0,2},{1,3},{2,0},{3,1},{4,6},{5,7},{6,4},{7,5},{8,10},{9,11},{10,... | collective-permute-start | bytes 230408 | tf_op jit(solution)/shard_map/ppermute | solution.py:512
  35.5 0.0 collective-permute-done.3
  35.5 0.6 %collective-permute-start.4 = (f32[2,1,16,600]{3,2,1,0:T(8,128)S(1)}, f32[2,1,16,600]{3,2,1,0:T(8,128)S(1)}, u32[]{:S(2)}, u32[]{:S(2)}) collective-permute-start(f32[2,1,16,600]{3,2,1,0:T(8,128)S(1)} %fusion.1), channel_id=1, source_target_pairs={{0,2},{1,3},{2,0},{3,1},{4,6},{5,7},{6,4},{7,5},{8,10},{9,11},{10,... | collective-permute-start | bytes 230408 | tf_op jit(solution)/shard_map/ppermute | solution.py:512
  36.1 3.2 %collective-permute-done.6.refs_1_ = f32[2,1,16,600]{3,2,1,0:T(8,128)S(1)} collective-permute-done((f32[2,1,16,600]{3,2,1,0:T(8,128)S(1)}, f32[2,1,16,600]{3,2,1,0:T(8,128)S(1)}, u32[]{:S(2)}, u32[]{:S(2)}) %collective-permute-start.6) | collective-permute-done | bytes 76832 | tf_op jit(solution)/shard_map/ppermute | solution.py:512
  39.3 1.3 %collective-permute-done.4.refs_0_ = f32[2,1,16,600]{3,2,1,0:T(8,128)S(1)} collective-permute-done((f32[2,1,16,600]{3,2,1,0:T(8,128)S(1)}, f32[2,1,16,600]{3,2,1,0:T(8,128)S(1)}, u32[]{:S(2)}, u32[]{:S(2)}) %collective-permute-start.4) | collective-permute-done | bytes 76832 | tf_op jit(solution)/shard_map/ppermute | solution.py:512
  40.6 0.0 collective-permute-done.2.away_ref
  40.6 0.7 %total.1 = f32[2,2,16,600]{3,2,1,0:T(8,128)} custom-call(f32[1,2,2,16,600]{4,3,2,1,0:T(8,128)S(1)} %get-tuple-element.39.home_ref, f32[1,2,2,16,600]{4,3,2,1,0:T(8,128)S(1)} %collective-permute-done.2.away_ref, f32[2,1,16,600]{3,2,1,0:T(8,128)S(1)} %collective-permute-done.4.refs_0_, f32[2,1,16,600]{3,2,1,0:T(8,128)S(1)} %collective-permute-done.6.refs_1_), custom_call_target="tpu_custom_call" | custom-call | tf_op jit(solution)/shard_map/total/pallas_call | solution.py:516
  (3 shorter events, 0.0 us)
Async XLA Ops:
  19.8 12.2 %all-to-all-start.1 = ((f32[8,2,2,8,256]{4,3,2,1,0:T(8,128)}), f32[8,2,2,8,256]{4,3,2,1,0:T(8,128)S(1)}, u32[]{:S(2)}, u32[]{:S(2)}) async-start(f32[8,2,2,8,256]{4,3,2,1,0:T(8,128)} %middle.1), calls=%async_computation.1 | async-start | bytes 524288 | tf_op jit(solution)/shard_map/all_to_all | solution.py:495
  23.4 4.2 %collective-permute-start = (f32[104,128]{1,0:T(8,128)S(1)}, f32[104,128]{1,0:T(8,128)S(1)}, u32[]{:S(2)}, u32[]{:S(2)}) collective-permute-start(f32[104,128]{1,0:T(8,128)S(1)} %get-tuple-element.35.own_inner_ref), channel_id=1, source_target_pairs={{0,1},{1,0},{2,3},{3,2},{4,5},{5,4},{6,7},{7,6},{8,9},{9,8},{10,11... | collective-permute-start | bytes 159752 | tf_op jit(solution)/shard_map/ppermute | solution.py:499
  23.4 4.2 %collective-permute-start.1 = (f32[104,128]{1,0:T(8,128)S(1)}, f32[104,128]{1,0:T(8,128)S(1)}, u32[]{:S(2)}, u32[]{:S(2)}) collective-permute-start(f32[104,128]{1,0:T(8,128)S(1)} %get-tuple-element.36.own_outer_ref), channel_id=1, source_target_pairs={{1,2},{2,1},{5,6},{6,5},{9,10},{10,9},{13,14},{14,13},{17,18},{18,... | collective-permute-start | bytes 159752 | tf_op jit(solution)/shard_map/ppermute | solution.py:498
  32.3 1.6 %collective-permute-start.5 = (f32[1,2,1,16,600]{4,3,1,2,0:T(8,128)S(1)}, f32[1,2,1,16,600]{4,3,1,2,0:T(8,128)S(1)}, u32[]{:S(2)}, u32[]{:S(2)}) collective-permute-start(f32[1,2,1,16,600]{4,3,1,2,0:T(8,128)S(1)} %bitcast.16), channel_id=1, source_target_pairs={{0,1},{1,0},{2,3},{3,2},{4,5},{5,4},{6,7},{7,6},{8,9},{9,8},{10,11... | collective-permute-start | bytes 230408 | tf_op jit(solution)/shard_map/ppermute | solution.py:507
  32.7 2.8 %collective-permute-start.3 = (f32[1,2,1,16,600]{4,3,1,2,0:T(8,128)S(1)}, f32[1,2,1,16,600]{4,3,1,2,0:T(8,128)S(1)}, u32[]{:S(2)}, u32[]{:S(2)}) collective-permute-start(f32[1,2,1,16,600]{4,3,1,2,0:T(8,128)S(1)} %bitcast.15), channel_id=1, source_target_pairs={{0,1},{1,0},{2,3},{3,2},{4,5},{5,4},{6,7},{7,6},{8,9},{9,8},{10,11... | collective-permute-start | bytes 230408 | tf_op jit(solution)/shard_map/ppermute | solution.py:507
  33.9 6.8 %collective-permute-start.2 = (f32[1,2,2,16,600]{4,3,2,1,0:T(8,128)S(1)}, f32[1,2,2,16,600]{4,3,2,1,0:T(8,128)S(1)}, u32[]{:S(2)}, u32[]{:S(2)}) collective-permute-start(f32[1,2,2,16,600]{4,3,2,1,0:T(8,128)S(1)} %get-tuple-element.40), channel_id=1, source_target_pairs={{0,1},{1,0},{2,3},{3,2},{4,5},{5,4},{6,7},{7,6},{8,9},{9,8},{10,11... | collective-permute-start | bytes 460808 | tf_op jit(solution)/shard_map/ppermute | solution.py:514
  34.0 5.3 %collective-permute-start.6 = (f32[2,1,16,600]{3,2,1,0:T(8,128)S(1)}, f32[2,1,16,600]{3,2,1,0:T(8,128)S(1)}, u32[]{:S(2)}, u32[]{:S(2)}) collective-permute-start(f32[2,1,16,600]{3,2,1,0:T(8,128)S(1)} %fusion), channel_id=1, source_target_pairs={{0,2},{1,3},{2,0},{3,1},{4,6},{5,7},{6,4},{7,5},{8,10},{9,11},{10,... | collective-permute-start | bytes 230408 | tf_op jit(solution)/shard_map/ppermute | solution.py:512
  35.5 5.1 %collective-permute-start.4 = (f32[2,1,16,600]{3,2,1,0:T(8,128)S(1)}, f32[2,1,16,600]{3,2,1,0:T(8,128)S(1)}, u32[]{:S(2)}, u32[]{:S(2)}) collective-permute-start(f32[2,1,16,600]{3,2,1,0:T(8,128)S(1)} %fusion.1), channel_id=1, source_target_pairs={{0,2},{1,3},{2,0},{3,1},{4,6},{5,7},{6,4},{7,5},{8,10},{9,11},{10,... | collective-permute-start | bytes 230408 | tf_op jit(solution)/shard_map/ppermute | solution.py:512

commit v5 on v4

--- a/solution.py
+++ b/solution.py
@@ -69,18 +69,13 @@
 
 def adjoint_kernel(
     v_hbm, f_hbm, band_hbm, rates_hbm, cut_hbm, out_ref, inner_ref, outer_ref, cutoff_ref, spread_ref,
-    v_ref, f_ref, band_ref, rates_ref, cut_ref, v_sem, f_sem, small_sem,
+    v_ref, f_ref, band_ref, rates_ref, cut_ref, tail_v, tail_f, v_sem, f_sem, small_sem,
 ):
     shards, _, held, rows, cells = out_ref.shape
     cols, sensors = v_ref.shape[2:]
-    v_copies, f_copies = [], []
-    for k in range(held):
-        v_copies.append(pltpu.make_async_copy(v_hbm.at[:, k], v_ref.at[:, k], v_sem.at[k]))
-        v_copies[k].start()
-        for c in range(2):
-            copy = pltpu.make_async_copy(f_hbm.at[c, k], f_ref.at[c, k], f_sem.at[2 * k + c])
-            f_copies.append(copy)
-            copy.start()
+    copies = [pltpu.make_async_copy(f_hbm, f_ref, f_sem), pltpu.make_async_copy(v_hbm, v_ref, v_sem)]
+    for copy in copies:
+        copy.start()
     small = []
     for at, (source, target) in enumerate(((band_hbm, band_ref), (rates_hbm, rates_ref), (cut_hbm, cut_ref))):
         small.append(pltpu.make_async_copy(source, target, small_sem.at[at]))
@@ -104,16 +99,25 @@
                 place = at * packed_rows + first // GROUPS
                 ref[place : place + ROWS] = packed
 
-    for copy in v_copies + f_copies:
+    tail_v[...] = jnp.zeros_like(tail_v)
+    tail_f[...] = jnp.zeros_like(tail_f)
+    for copy in copies:
         copy.wait()
     for k in range(held):
         high, low = split(v_ref[:, k].reshape(2 * cols, sensors))
         parts = jnp.concatenate([high, low], axis=0)
+        body = sensors // (2 * LANES) * (2 * LANES)
+        rest = sensors - body
+        tail_v[: 4 * cols, :rest] = parts[:, body:]
+        tail_v[: 2 * cols, LANES : LANES + rest] = high[:, body:]
         sums = []
         for c in range(2):
             f_high, f_low = split(f_ref[c, k])
-            both = product(parts, f_high, ((1,), (0,)))
-            both = both[: 2 * cols] + both[2 * cols :] + product(high, f_low, ((1,), (0,)))
+            tail_f[c, :rest] = f_high[body:]
+            tail_f[c, LANES : LANES + rest] = f_low[body:]
+            both = product(parts[:, :body], f_high[:body], ((1,), (0,)))
+            both += product(tail_v[...], tail_f[c], ((1,), (0,)))
+            both = both[: 2 * cols] + both[2 * cols :] + product(high[:, :body], f_low[:body], ((1,), (0,)))
             sums.append(both)
         re = sums[0][:cols] + sums[1][cols:]
         im = sums[0][cols:] - sums[1][:cols]
@@ -158,8 +162,10 @@
             pltpu.VMEM((1, cells), jnp.int32),
             pltpu.SMEM(band_rates.shape, jnp.float32),
             pltpu.SMEM(causal_cutoffs.shape, jnp.int32),
-            pltpu.SemaphoreType.DMA((held,)),
-            pltpu.SemaphoreType.DMA((2 * held,)),
+            pltpu.VMEM((4 * cols, 2 * LANES), jnp.bfloat16),
+            pltpu.VMEM((2, 2 * LANES, cells), jnp.bfloat16),
+            pltpu.SemaphoreType.DMA,
+            pltpu.SemaphoreType.DMA,
             pltpu.SemaphoreType.DMA((3,)),
         ],
         compiler_params=grant(16),

time: 41.6 us -> 41.6 us (level)
  no operation moved by 1% of the time
where the time goes in v5:
time: 41.6 us; the launch traced here: 41.3 us
  blocking collectives  16 us (38%)
  Pallas kernels  10.1 us (24%)
  waiting for transfers between devices  7.86 us (19%)
  starting transfers between devices  7.13 us (17%)
    all_to_all x1, blocking collectives, on_device(): lax.all_to_all(spectrum, 'freq', split_axis=0, concat_axis=0, tiled=True)  16 us
    ppermute x2, waiting for transfers between devices, on_device(): arrived.append(lax.ppermute(leaving[k][s - 1], 'cell', pairs))  4.48 us
    all_to_all x1, starting transfers between devices, on_device(): lax.all_to_all(spectrum, 'freq', split_axis=0, concat_axis=0, tiled=True)  3.6 us
    pallas_call x1, Pallas kernels, smooth(): pl.pallas_call(smooth_kernel, in_specs=[HBM_SPEC, VMEM_SPEC], out_specs=[...  3.56 us
    all_to_all x1, waiting for transfers between devices, on_device(): lax.all_to_all(spectrum, 'freq', split_axis=0, concat_axis=0, tiled=True)  3.37 us
    pallas_call x1, Pallas kernels, adjoint(): pl.pallas_call(adjoint_kernel, in_specs=[HBM_SPEC] * 5, out_specs=[VMEM_S...  2.78 us
    ppermute x2, starting transfers between devices, on_device(): arrived.append(lax.ppermute(leaving[k][s - 1], 'cell', pairs))  2.16 us
    pallas_call x3, Pallas kernels, forward(): pl.pallas_call(functools.partial(forward_kernel, steps, chips, wanted), i...  1.24 us
  transfers between devices with their start and end apart: 8, of which 3 were waited for; matrix products, arithmetic and copies ran while one was open for 0% of the time, Pallas kernels for 13%

profile of v5, /device:TPU:0, one launch (start us, length us, event | category | flops | bytes accessed | tf_op | source)
XLA Modules:
  0.0 41.3 jit_solution(1480831751404596343)
XLA Ops:
  0.0 2.8 %adjoint.1 = (f32[8,2,2,8,256]{4,3,2,1,0:T(8,128)S(1)}, f32[104,128]{1,0:T(8,128)S(1)}, f32[104,128]{1,0:T(8,128)S(1)}, s32[8,128]{1,0:T(8,128)S(1)}, f32[8,256]{1,0:T(8,128)S(1)}) custom-call(f32[2,2,64,600]{3,2,1,0:T(8,128)} %v_hbm.1, f32[2,2,600,256]{3,2,1,0:T(8,128)} %f_hbm.2, s32[1,256]{1,0:T(1,128)} %bitcast.17, f32[8]{0:T(128)} %rates_hbm.1, s32[64]{0:T(128)} %cut_hbm.1), custom_call_target="tpu_custom_call" | custom-call | flops 471859200 | bytes 2457600 | tf_op jit(solution)/shard_map/adjoint/pallas_call | solution.py:148
  2.8 16.0 %all_to_all.10.x_ref = f32[8,2,2,8,256]{4,3,2,1,0:T(8,128)S(1)} all-to-all(f32[8,2,2,8,256]{4,3,2,1,0:T(8,128)S(1)} %get-tuple-element.25), channel_id=1, replica_groups=mesh['freq'=8,'cell'=4] {'freq'}, dimensions={0} | all-to-all | bytes 524288 | tf_op jit(solution)/shard_map/all_to_all | solution.py:495
  18.8 0.9 %middle.1 = f32[8,2,2,8,256]{4,3,2,1,0:T(8,128)} custom-call(f32[8,2,2,8,256]{4,3,2,1,0:T(8,128)S(1)} %all_to_all.10.x_ref, s32[8,128]{1,0:T(8,128)S(1)} %get-tuple-element.26.cutoff_ref), custom_call_target="tpu_custom_call" | custom-call | flops 3932160 | bytes 524288 | tf_op jit(solution)/shard_map/middle/pallas_call | solution.py:235
  19.8 3.6 %all-to-all-start.1 = ((f32[8,2,2,8,256]{4,3,2,1,0:T(8,128)}), f32[8,2,2,8,256]{4,3,2,1,0:T(8,128)S(1)}, u32[]{:S(2)}, u32[]{:S(2)}) async-start(f32[8,2,2,8,256]{4,3,2,1,0:T(8,128)} %middle.1), calls=%async_computation.1 | async-start | bytes 524288 | tf_op jit(solution)/shard_map/all_to_all | solution.py:501
  23.4 0.0 collective-permute-start
  23.4 0.7 %collective-permute-start.1 = (f32[104,128]{1,0:T(8,128)S(1)}, f32[104,128]{1,0:T(8,128)S(1)}, u32[]{:S(2)}, u32[]{:S(2)}) collective-permute-start(f32[104,128]{1,0:T(8,128)S(1)} %get-tuple-element.36.own_outer_ref), channel_id=1, source_target_pairs={{1,2},{2,1},{5,6},{6,5},{9,10},{10,9},{13,14},{14,13},{17,18},{18,... | collective-permute-start | bytes 159752 | tf_op jit(solution)/shard_map/ppermute | solution.py:504
  24.0 3.6 %smooth.1 = (bf16[2,2,256,600]{3,2,1,0:T(8,128)(2,1)S(1)}, bf16[2,2,256,600]{3,2,1,0:T(8,128)(2,1)S(1)}, f32[2,2,32,600]{3,2,1,0:T(8,128)S(1)}) custom-call(f32[2,2,600,256]{3,2,1,0:T(8,128)} %f_hbm.2, f32[8,256]{1,0:T(8,128)S(1)} %get-tuple-element.31.rates_ref), custom_call_target="tpu_custom_call" | custom-call | flops 943718400 | bytes 4915200 | tf_op jit(solution)/shard_map/smooth/pallas_call | solution.py:308
  27.6 0.0 collective-permute-done.inner_ref
  27.6 0.0 collective-permute-done.1.outer_ref
  27.6 0.9 %near_edges.1 = (bf16[2,2,32,600]{3,2,1,0:T(8,128)(2,1)S(1)}, bf16[2,2,32,600]{3,2,1,0:T(8,128)(2,1)S(1)}) custom-call(f32[2,2,32,600]{3,2,1,0:T(8,128)S(1)} %get-tuple-element.34.near_ref, f32[104,128]{1,0:T(8,128)S(1)} %get-tuple-element.35.own_inner_ref, f32[104,128]{1,0:T(8,128)S(1)} %get-tuple-element.36.own_outer_ref, ...), custom_call_target="tpu_custom_call" | custom-call | flops 58982400 | bytes 614400 | tf_op jit(solution)/shard_map/near_edges/pallas_call | solution.py:407
  28.6 3.4 %all-to-all-done.1.x_ref = f32[8,2,2,8,256]{4,3,2,1,0:T(8,128)S(1)} async-done(((f32[8,2,2,8,256]{4,3,2,1,0:T(8,128)}), f32[8,2,2,8,256]{4,3,2,1,0:T(8,128)S(1)}, u32[]{:S(2)}, u32[]{:S(2)}) %all-to-all-start.1) | async-done | bytes 262176 | tf_op jit(solution)/shard_map/all_to_all | solution.py:501
  31.9 0.3 shard_map.57
  32.3 0.1 collective-permute-start.5
  32.3 0.3 shard_map.56
  32.7 0.6 %collective-permute-start.3 = (f32[1,2,1,16,600]{4,3,1,2,0:T(8,128)S(1)}, f32[1,2,1,16,600]{4,3,1,2,0:T(8,128)S(1)}, u32[]{:S(2)}, u32[]{:S(2)}) collective-permute-start(f32[1,2,1,16,600]{4,3,1,2,0:T(8,128)S(1)} %bitcast.15), channel_id=1, source_target_pairs={{0,1},{1,0},{2,3},{3,2},{4,5},{5,4},{6,7},{7,6},{8,9},{9,8},{10,11... | collective-permute-start | bytes 230408 | tf_op jit(solution)/shard_map/ppermute | solution.py:513
  33.3 0.6 %shard_map.55 = (f32[1,2,2,16,600]{4,3,2,1,0:T(8,128)S(1)}, f32[1,2,2,16,600]{4,3,2,1,0:T(8,128)S(1)}) custom-call(f32[8,2,2,8,256]{4,3,2,1,0:T(8,128)S(1)} %all-to-all-done.1.x_ref, bf16[2,2,256,600]{3,2,1,0:T(8,128)(2,1)S(1)} %get-tuple-element.32.high_ref, bf16[2,2,256,600]{3,2,1,0:T(8,128)(2,1)S(1)} %get-tuple-element.33.low_ref, ...), custom_call_target="tpu_custom_call" | custom-call | flops 235929600 | bytes 2457600 | tf_op jit(solution)/shard_map/pallas_call | solution.py:463
  33.8 0.1 collective-permute-start.2
  33.9 0.0 collective-permute-done.5
  33.9 1.6 %collective-permute-start.6 = (f32[2,1,16,600]{3,2,1,0:T(8,128)S(1)}, f32[2,1,16,600]{3,2,1,0:T(8,128)S(1)}, u32[]{:S(2)}, u32[]{:S(2)}) collective-permute-start(f32[2,1,16,600]{3,2,1,0:T(8,128)S(1)} %fusion), channel_id=1, source_target_pairs={{0,2},{1,3},{2,0},{3,1},{4,6},{5,7},{6,4},{7,5},{8,10},{9,11},{10,... | collective-permute-start | bytes 230408 | tf_op jit(solution)/shard_map/ppermute | solution.py:518
  35.5 0.0 collective-permute-done.3
  35.5 0.6 %collective-permute-start.4 = (f32[2,1,16,600]{3,2,1,0:T(8,128)S(1)}, f32[2,1,16,600]{3,2,1,0:T(8,128)S(1)}, u32[]{:S(2)}, u32[]{:S(2)}) collective-permute-start(f32[2,1,16,600]{3,2,1,0:T(8,128)S(1)} %fusion.1), channel_id=1, source_target_pairs={{0,2},{1,3},{2,0},{3,1},{4,6},{5,7},{6,4},{7,5},{8,10},{9,11},{10,... | collective-permute-start | bytes 230408 | tf_op jit(solution)/shard_map/ppermute | solution.py:518
  36.1 3.2 %collective-permute-done.6.refs_1_ = f32[2,1,16,600]{3,2,1,0:T(8,128)S(1)} collective-permute-done((f32[2,1,16,600]{3,2,1,0:T(8,128)S(1)}, f32[2,1,16,600]{3,2,1,0:T(8,128)S(1)}, u32[]{:S(2)}, u32[]{:S(2)}) %collective-permute-start.6) | collective-permute-done | bytes 76832 | tf_op jit(solution)/shard_map/ppermute | solution.py:518
  39.3 1.3 %collective-permute-done.4.refs_0_ = f32[2,1,16,600]{3,2,1,0:T(8,128)S(1)} collective-permute-done((f32[2,1,16,600]{3,2,1,0:T(8,128)S(1)}, f32[2,1,16,600]{3,2,1,0:T(8,128)S(1)}, u32[]{:S(2)}, u32[]{:S(2)}) %collective-permute-start.4) | collective-permute-done | bytes 76832 | tf_op jit(solution)/shard_map/ppermute | solution.py:518
  40.6 0.7 %total.1 = f32[2,2,16,600]{3,2,1,0:T(8,128)} custom-call(f32[1,2,2,16,600]{4,3,2,1,0:T(8,128)S(1)} %get-tuple-element.39.home_ref, f32[1,2,2,16,600]{4,3,2,1,0:T(8,128)S(1)} %collective-permute-done.2.away_ref, f32[2,1,16,600]{3,2,1,0:T(8,128)S(1)} %collective-permute-done.4.refs_0_, f32[2,1,16,600]{3,2,1,0:T(8,128)S(1)} %collective-permute-done.6.refs_1_), custom_call_target="tpu_custom_call" | custom-call | tf_op jit(solution)/shard_map/total/pallas_call | solution.py:522
  (3 shorter events, 0.0 us)
Async XLA Ops:
  19.8 12.2 %all-to-all-start.1 = ((f32[8,2,2,8,256]{4,3,2,1,0:T(8,128)}), f32[8,2,2,8,256]{4,3,2,1,0:T(8,128)S(1)}, u32[]{:S(2)}, u32[]{:S(2)}) async-start(f32[8,2,2,8,256]{4,3,2,1,0:T(8,128)} %middle.1), calls=%async_computation.1 | async-start | bytes 524288 | tf_op jit(solution)/shard_map/all_to_all | solution.py:501
  23.4 4.2 %collective-permute-start = (f32[104,128]{1,0:T(8,128)S(1)}, f32[104,128]{1,0:T(8,128)S(1)}, u32[]{:S(2)}, u32[]{:S(2)}) collective-permute-start(f32[104,128]{1,0:T(8,128)S(1)} %get-tuple-element.35.own_inner_ref), channel_id=1, source_target_pairs={{0,1},{1,0},{2,3},{3,2},{4,5},{5,4},{6,7},{7,6},{8,9},{9,8},{10,11... | collective-permute-start | bytes 159752 | tf_op jit(solution)/shard_map/ppermute | solution.py:505
  23.4 4.3 %collective-permute-start.1 = (f32[104,128]{1,0:T(8,128)S(1)}, f32[104,128]{1,0:T(8,128)S(1)}, u32[]{:S(2)}, u32[]{:S(2)}) collective-permute-start(f32[104,128]{1,0:T(8,128)S(1)} %get-tuple-element.36.own_outer_ref), channel_id=1, source_target_pairs={{1,2},{2,1},{5,6},{6,5},{9,10},{10,9},{13,14},{14,13},{17,18},{18,... | collective-permute-start | bytes 159752 | tf_op jit(solution)/shard_map/ppermute | solution.py:504
  32.3 1.6 %collective-permute-start.5 = (f32[1,2,1,16,600]{4,3,1,2,0:T(8,128)S(1)}, f32[1,2,1,16,600]{4,3,1,2,0:T(8,128)S(1)}, u32[]{:S(2)}, u32[]{:S(2)}) collective-permute-start(f32[1,2,1,16,600]{4,3,1,2,0:T(8,128)S(1)} %bitcast.16), channel_id=1, source_target_pairs={{0,1},{1,0},{2,3},{3,2},{4,5},{5,4},{6,7},{7,6},{8,9},{9,8},{10,11... | collective-permute-start | bytes 230408 | tf_op jit(solution)/shard_map/ppermute | solution.py:513
  32.7 2.8 %collective-permute-start.3 = (f32[1,2,1,16,600]{4,3,1,2,0:T(8,128)S(1)}, f32[1,2,1,16,600]{4,3,1,2,0:T(8,128)S(1)}, u32[]{:S(2)}, u32[]{:S(2)}) collective-permute-start(f32[1,2,1,16,600]{4,3,1,2,0:T(8,128)S(1)} %bitcast.15), channel_id=1, source_target_pairs={{0,1},{1,0},{2,3},{3,2},{4,5},{5,4},{6,7},{7,6},{8,9},{9,8},{10,11... | collective-permute-start | bytes 230408 | tf_op jit(solution)/shard_map/ppermute | solution.py:513
  33.8 6.8 %collective-permute-start.2 = (f32[1,2,2,16,600]{4,3,2,1,0:T(8,128)S(1)}, f32[1,2,2,16,600]{4,3,2,1,0:T(8,128)S(1)}, u32[]{:S(2)}, u32[]{:S(2)}) collective-permute-start(f32[1,2,2,16,600]{4,3,2,1,0:T(8,128)S(1)} %get-tuple-element.40), channel_id=1, source_target_pairs={{0,1},{1,0},{2,3},{3,2},{4,5},{5,4},{6,7},{7,6},{8,9},{9,8},{10,11... | collective-permute-start | bytes 460808 | tf_op jit(solution)/shard_map/ppermute | solution.py:520
  33.9 5.4 %collective-permute-start.6 = (f32[2,1,16,600]{3,2,1,0:T(8,128)S(1)}, f32[2,1,16,600]{3,2,1,0:T(8,128)S(1)}, u32[]{:S(2)}, u32[]{:S(2)}) collective-permute-start(f32[2,1,16,600]{3,2,1,0:T(8,128)S(1)} %fusion), channel_id=1, source_target_pairs={{0,2},{1,3},{2,0},{3,1},{4,6},{5,7},{6,4},{7,5},{8,10},{9,11},{10,... | collective-permute-start | bytes 230408 | tf_op jit(solution)/shard_map/ppermute | solution.py:518
  35.5 5.1 %collective-permute-start.4 = (f32[2,1,16,600]{3,2,1,0:T(8,128)S(1)}, f32[2,1,16,600]{3,2,1,0:T(8,128)S(1)}, u32[]{:S(2)}, u32[]{:S(2)}) collective-permute-start(f32[2,1,16,600]{3,2,1,0:T(8,128)S(1)} %fusion.1), channel_id=1, source_target_pairs={{0,2},{1,3},{2,0},{3,1},{4,6},{5,7},{6,4},{7,5},{8,10},{9,11},{10,... | collective-permute-start | bytes 230408 | tf_op jit(solution)/shard_map/ppermute | solution.py:518

commit v6 on v5

--- a/solution.py
+++ b/solution.py
@@ -418,10 +418,41 @@
     )(near, own_inner, own_outer, inner, outer, rates)
 
 
+def pack(ref, s, values, pad_ref):
+    rows, sensors = values[0].shape
+    tiles, rest = divmod(sensors, LANES)
+    for p, value in enumerate(values):
+        for t in range(tiles):
+            place = (p * tiles + t) * rows
+            ref[s, place : place + rows] = value[:, t * LANES : (t + 1) * LANES]
+        pad_ref[p, :, :rest] = value[:, tiles * LANES :]
+    lane = lax.broadcasted_iota(jnp.int32, (rows, LANES), 1)
+    second = pltpu.roll(pad_ref[1], rest, 1)
+    place = 2 * tiles * rows
+    ref[s, place : place + rows] = jnp.where(lane < rest, pad_ref[0], second)
+    half = rows // 2
+    moved = pltpu.roll(second, LANES // 2, 1)
+    ref[s, place + rows :] = jnp.where(lane[:half] < LANES // 2, second[:half], moved[half:])
+
+
+def unpack(ref, rows, sensors):
+    tiles, rest = divmod(sensors, LANES)
+    parts = []
+    place = 2 * tiles * rows
+    lane = lax.broadcasted_iota(jnp.int32, (rows, LANES), 1)
+    first, last = ref[place : place + rows], ref[place + rows :]
+    second = jnp.concatenate([last, pltpu.roll(last, LANES // 2, 1)], axis=0)
+    second = pltpu.roll(jnp.where(lane < rest, second, first), LANES - rest, 1)
+    for p, tail in enumerate((first, second)):
+        tile = [ref[(p * tiles + t) * rows : (p * tiles + t + 1) * rows] for t in range(tiles)]
+        parts.append(jnp.concatenate(tile + [tail], axis=1)[:, :sensors])
+    return parts
+
+
 def forward_kernel(
-    steps, chips, wanted, x_ref, high_ref, low_ref, near_high_ref, near_low_ref, away_ref, home_ref
+    steps, chips, wanted, share, x_ref, high_ref, low_ref, near_high_ref, near_low_ref, away_ref, home_ref, pad_ref
 ):
-    share, sensors = home_ref.shape[3:]
+    sensors = high_ref.shape[3]
     per = share // ROWS
     cell = lax.axis_index("cell")
     chip, core = cell // 2, cell % 2
@@ -451,20 +482,29 @@
         re = (terms[0][:rows] - terms[1][rows:]).reshape(2, len(steps), share, sensors)
         im = (terms[0][rows:] + terms[1][:rows]).reshape(2, len(steps), share, sensors)
         for side, ref in enumerate((away_ref, home_ref)):
-            ref[:, 0, at] = re[side]
-            ref[:, 1, at] = im[side]
-
-
-def forward(returned, matrices, steps, chips, wanted):
+            if len(ref.shape) == 3:
+                for s in range(len(steps)):
+                    pack(ref, s, (re[side, s], im[side, s]), pad_ref)
+            else:
+                ref[:, 0, at] = re[side]
+                ref[:, 1, at] = im[side]
+
+
+def forward(returned, matrices, steps, chips, wanted, packed):
     shards, _, _, rows, cells = returned.shape
     sensors = matrices[0].shape[3]
     share = shards * rows // (2 * chips)
-    shape = jax.ShapeDtypeStruct((len(steps), 2, len(wanted), share, sensors), jnp.float32)
+    if packed:
+        rows = 2 * (sensors // LANES) * share + share + share // 2
+        shape = jax.ShapeDtypeStruct((len(steps), rows, LANES), jnp.float32)
+    else:
+        shape = jax.ShapeDtypeStruct((len(steps), 2, len(wanted), share, sensors), jnp.float32)
     return pl.pallas_call(
-        functools.partial(forward_kernel, steps, chips, wanted),
+        functools.partial(forward_kernel, steps, chips, wanted, share),
         in_specs=[VMEM_SPEC] * 5,
         out_specs=[VMEM_SPEC] * 2,
         out_shape=[shape, shape],
+        scratch_shapes=[pltpu.VMEM((2, share, LANES), jnp.float32)],
         compiler_params=grant(16),
         cost_estimate=pl.CostEstimate(
             flops=48 * len(steps) * len(wanted) * share * sensors * cells,
@@ -478,10 +518,12 @@
     out_ref = refs[-1]
     held = out_ref.shape[1]
     for k in range(held):
-        total = home_ref[0, :, k] + away_ref[0, :, k]
-        for ref in refs[k:-1:held]:
-            total += ref[:, 0]
-        out_ref[:, k] = total
+        arrived = [unpack(ref, *out_ref.shape[2:]) for ref in refs[k:-1:held]]
+        for c in range(2):
+            total = home_ref[0, c, k] + away_ref[0, c, k]
+            for parts in arrived:
+                total += parts[c]
+            out_ref[c, k] = total
 
 
 def on_device(columns, freq_blocks, causal_cutoffs, band_index, band_rates):
@@ -509,14 +551,14 @@
     leaving = []
     if chips > 1:
         for k in range(held):
-            away, home = forward(returned, matrices, range(1, chips), chips, (k,))
+            away, home = forward(returned, matrices, range(1, chips), chips, (k,), True)
             leaving.append(home + lax.ppermute(away, "cell", swap))
     arrived = []
     for s in range(1, chips):
         pairs = [(i, 2 * ((i // 2 + s) % chips) + i % 2) for i in range(strips)]
         for k in range(held):
             arrived.append(lax.ppermute(leaving[k][s - 1], "cell", pairs))
-    away, home = forward(returned, matrices, range(1), chips, range(held))
+    away, home = forward(returned, matrices, range(1), chips, range(held), False)
     away = lax.ppermute(away, "cell", swap)
     share, sensors = home.shape[3:]
     return pl.pallas_call(

time: 41.6 us -> 41.7 us (level)
  no operation moved by 1% of the time
where the time goes in v6:
time: 41.7 us; the launch traced here: 41.4 us
  blocking collectives  16 us (38%)
  Pallas kernels  10.5 us (25%)
  waiting for transfers between devices  7.68 us (18%)
  starting transfers between devices  7.01 us (17%)
    all_to_all x1, blocking collectives, on_device(): lax.all_to_all(spectrum, 'freq', split_axis=0, concat_axis=0, tiled=True)  16 us
    ppermute x2, waiting for transfers between devices, on_device(): arrived.append(lax.ppermute(leaving[k][s - 1], 'cell', pairs))  4.3 us
    all_to_all x1, starting transfers between devices, on_device(): lax.all_to_all(spectrum, 'freq', split_axis=0, concat_axis=0, tiled=True)  3.6 us
    pallas_call x1, Pallas kernels, smooth(): pl.pallas_call(smooth_kernel, in_specs=[HBM_SPEC, VMEM_SPEC], out_specs=[...  3.56 us
    all_to_all x1, waiting for transfers between devices, on_device(): lax.all_to_all(spectrum, 'freq', split_axis=0, concat_axis=0, tiled=True)  3.37 us
    pallas_call x1, Pallas kernels, adjoint(): pl.pallas_call(adjoint_kernel, in_specs=[HBM_SPEC] * 5, out_specs=[VMEM_S...  2.78 us
    ppermute x2, starting transfers between devices, on_device(): arrived.append(lax.ppermute(leaving[k][s - 1], 'cell', pairs))  2.16 us
    pallas_call x3, Pallas kernels, forward(): pl.pallas_call(functools.partial(forward_kernel, steps, chips, wanted, sh...  1.52 us
  transfers between devices with their start and end apart: 8, of which 3 were waited for; matrix products, arithmetic and copies ran while one was open for 0% of the time, Pallas kernels for 13%

profile of v6, /device:TPU:0, one launch (start us, length us, event | category | flops | bytes accessed | tf_op | source)
XLA Modules:
  0.0 41.4 jit_solution(16352729522062689270)
XLA Ops:
  0.0 2.8 %adjoint.1 = (f32[8,2,2,8,256]{4,3,2,1,0:T(8,128)S(1)}, f32[104,128]{1,0:T(8,128)S(1)}, f32[104,128]{1,0:T(8,128)S(1)}, s32[8,128]{1,0:T(8,128)S(1)}, f32[8,256]{1,0:T(8,128)S(1)}) custom-call(f32[2,2,64,600]{3,2,1,0:T(8,128)} %v_hbm.1, f32[2,2,600,256]{3,2,1,0:T(8,128)} %f_hbm.2, s32[1,256]{1,0:T(1,128)} %bitcast.5, f32[8]{0:T(128)} %rates_hbm.1, s32[64]{0:T(128)} %cut_hbm.1), custom_call_target="tpu_custom_call" | custom-call | flops 471859200 | bytes 2457600 | tf_op jit(solution)/shard_map/adjoint/pallas_call | solution.py:148
  2.8 16.0 %all_to_all.10.x_ref = f32[8,2,2,8,256]{4,3,2,1,0:T(8,128)S(1)} all-to-all(f32[8,2,2,8,256]{4,3,2,1,0:T(8,128)S(1)} %get-tuple-element.25), channel_id=1, replica_groups=mesh['freq'=8,'cell'=4] {'freq'}, dimensions={0} | all-to-all | bytes 524288 | tf_op jit(solution)/shard_map/all_to_all | solution.py:537
  18.8 0.9 %middle.1 = f32[8,2,2,8,256]{4,3,2,1,0:T(8,128)} custom-call(f32[8,2,2,8,256]{4,3,2,1,0:T(8,128)S(1)} %all_to_all.10.x_ref, s32[8,128]{1,0:T(8,128)S(1)} %get-tuple-element.26.cutoff_ref), custom_call_target="tpu_custom_call" | custom-call | flops 3932160 | bytes 524288 | tf_op jit(solution)/shard_map/middle/pallas_call | solution.py:235
  19.8 3.6 %all-to-all-start.1 = ((f32[8,2,2,8,256]{4,3,2,1,0:T(8,128)}), f32[8,2,2,8,256]{4,3,2,1,0:T(8,128)S(1)}, u32[]{:S(2)}, u32[]{:S(2)}) async-start(f32[8,2,2,8,256]{4,3,2,1,0:T(8,128)} %middle.1), calls=%async_computation.1 | async-start | bytes 524288 | tf_op jit(solution)/shard_map/all_to_all | solution.py:543
  23.4 0.0 collective-permute-start
  23.4 0.7 %collective-permute-start.1 = (f32[104,128]{1,0:T(8,128)S(1)}, f32[104,128]{1,0:T(8,128)S(1)}, u32[]{:S(2)}, u32[]{:S(2)}) collective-permute-start(f32[104,128]{1,0:T(8,128)S(1)} %get-tuple-element.36.own_outer_ref), channel_id=1, source_target_pairs={{1,2},{2,1},{5,6},{6,5},{9,10},{10,9},{13,14},{14,13},{17,18},{18,... | collective-permute-start | bytes 159752 | tf_op jit(solution)/shard_map/ppermute | solution.py:546
  24.0 3.6 %smooth.1 = (bf16[2,2,256,600]{3,2,1,0:T(8,128)(2,1)S(1)}, bf16[2,2,256,600]{3,2,1,0:T(8,128)(2,1)S(1)}, f32[2,2,32,600]{3,2,1,0:T(8,128)S(1)}) custom-call(f32[2,2,600,256]{3,2,1,0:T(8,128)} %f_hbm.2, f32[8,256]{1,0:T(8,128)S(1)} %get-tuple-element.31.rates_ref), custom_call_target="tpu_custom_call" | custom-call | flops 943718400 | bytes 4915200 | tf_op jit(solution)/shard_map/smooth/pallas_call | solution.py:308
  27.6 0.0 collective-permute-done.inner_ref
  27.6 0.0 collective-permute-done.1.outer_ref
  27.6 0.9 %near_edges.1 = (bf16[2,2,32,600]{3,2,1,0:T(8,128)(2,1)S(1)}, bf16[2,2,32,600]{3,2,1,0:T(8,128)(2,1)S(1)}) custom-call(f32[2,2,32,600]{3,2,1,0:T(8,128)S(1)} %get-tuple-element.34.near_ref, f32[104,128]{1,0:T(8,128)S(1)} %get-tuple-element.35.own_inner_ref, f32[104,128]{1,0:T(8,128)S(1)} %get-tuple-element.36.own_outer_ref, ...), custom_call_target="tpu_custom_call" | custom-call | flops 58982400 | bytes 614400 | tf_op jit(solution)/shard_map/near_edges/pallas_call | solution.py:407
  28.6 3.4 %all-to-all-done.1.x_ref = f32[8,2,2,8,256]{4,3,2,1,0:T(8,128)S(1)} async-done(((f32[8,2,2,8,256]{4,3,2,1,0:T(8,128)}), f32[8,2,2,8,256]{4,3,2,1,0:T(8,128)S(1)}, u32[]{:S(2)}, u32[]{:S(2)}) %all-to-all-start.1) | async-done | bytes 262176 | tf_op jit(solution)/shard_map/all_to_all | solution.py:543
  31.9 0.5 %shard_map.57 = (f32[1,152,128]{2,1,0:T(8,128)S(1)}, f32[1,152,128]{2,1,0:T(8,128)S(1)}) custom-call(f32[8,2,2,8,256]{4,3,2,1,0:T(8,128)S(1)} %all-to-all-done.1.x_ref, bf16[2,2,256,600]{3,2,1,0:T(8,128)(2,1)S(1)} %get-tuple-element.32.high_ref, bf16[2,2,256,600]{3,2,1,0:T(8,128)(2,1)S(1)} %get-tuple-element.33.low_ref, ...), custom_call_target="tpu_custom_call" | custom-call | flops 117964800 | bytes 1228800 | tf_op jit(solution)/shard_map/pallas_call | solution.py:502
  32.4 0.5 %shard_map.56 = (f32[1,152,128]{2,1,0:T(8,128)S(1)}, f32[1,152,128]{2,1,0:T(8,128)S(1)}) custom-call(f32[8,2,2,8,256]{4,3,2,1,0:T(8,128)S(1)} %all-to-all-done.1.x_ref, bf16[2,2,256,600]{3,2,1,0:T(8,128)(2,1)S(1)} %get-tuple-element.32.high_ref, bf16[2,2,256,600]{3,2,1,0:T(8,128)(2,1)S(1)} %get-tuple-element.33.low_ref, ...), custom_call_target="tpu_custom_call" | custom-call | flops 117964800 | bytes 1228800 | tf_op jit(solution)/shard_map/pallas_call | solution.py:502
  32.9 0.5 %collective-permute-start.3 = (f32[1,152,128]{2,1,0:T(8,128)S(1)}, f32[1,152,128]{2,1,0:T(8,128)S(1)}, u32[]{:S(2)}, u32[]{:S(2)}) collective-permute-start(f32[1,152,128]{2,1,0:T(8,128)S(1)} %get-tuple-element.42), channel_id=1, source_target_pairs={{0,1},{1,0},{2,3},{3,2},{4,5},{5,4},{6,7},{7,6},{8,9},{9,8},{10,11... | collective-permute-start | bytes 233480 | tf_op jit(solution)/shard_map/ppermute | solution.py:555
  33.4 0.6 %shard_map.55 = (f32[1,2,2,16,600]{4,3,2,1,0:T(8,128)S(1)}, f32[1,2,2,16,600]{4,3,2,1,0:T(8,128)S(1)}) custom-call(f32[8,2,2,8,256]{4,3,2,1,0:T(8,128)S(1)} %all-to-all-done.1.x_ref, bf16[2,2,256,600]{3,2,1,0:T(8,128)(2,1)S(1)} %get-tuple-element.32.high_ref, bf16[2,2,256,600]{3,2,1,0:T(8,128)(2,1)S(1)} %get-tuple-element.33.low_ref, ...), custom_call_target="tpu_custom_call" | custom-call | flops 235929600 | bytes 2457600 | tf_op jit(solution)/shard_map/pallas_call | solution.py:502
  34.0 0.1 collective-permute-start.2
  34.0 0.0 collective-permute-done.5
  34.1 1.6 %collective-permute-start.6 = (f32[152,128]{1,0:T(8,128)S(1)}, f32[152,128]{1,0:T(8,128)S(1)}, u32[]{:S(2)}, u32[]{:S(2)}) collective-permute-start(f32[152,128]{1,0:T(8,128)S(1)} %add_bitcast_fusion), channel_id=1, source_target_pairs={{0,2},{1,3},{2,0},{3,1},{4,6},{5,7},{6,4},{7,5},{8,10},{9,11},{10,... | collective-permute-start | bytes 233480 | tf_op jit(solution)/shard_map/ppermute | solution.py:560
  35.6 0.0 collective-permute-done.3
  35.6 0.6 %collective-permute-start.4 = (f32[152,128]{1,0:T(8,128)S(1)}, f32[152,128]{1,0:T(8,128)S(1)}, u32[]{:S(2)}, u32[]{:S(2)}) collective-permute-start(f32[152,128]{1,0:T(8,128)S(1)} %add_bitcast_fusion.1), channel_id=1, source_target_pairs={{0,2},{1,3},{2,0},{3,1},{4,6},{5,7},{6,4},{7,5},{8,10},{9,11},{10,... | collective-permute-start | bytes 233480 | tf_op jit(solution)/shard_map/ppermute | solution.py:560
  36.2 0.0 collective-permute-done.2.away_ref
  36.2 3.0 %collective-permute-done.6.refs_1_ = f32[152,128]{1,0:T(8,128)S(1)} collective-permute-done((f32[152,128]{1,0:T(8,128)S(1)}, f32[152,128]{1,0:T(8,128)S(1)}, u32[]{:S(2)}, u32[]{:S(2)}) %collective-permute-start.6) | collective-permute-done | bytes 77856 | tf_op jit(solution)/shard_map/ppermute | solution.py:560
  39.3 1.3 %collective-permute-done.4.refs_0_ = f32[152,128]{1,0:T(8,128)S(1)} collective-permute-done((f32[152,128]{1,0:T(8,128)S(1)}, f32[152,128]{1,0:T(8,128)S(1)}, u32[]{:S(2)}, u32[]{:S(2)}) %collective-permute-start.4) | collective-permute-done | bytes 77856 | tf_op jit(solution)/shard_map/ppermute | solution.py:560
  40.5 0.8 %total.1 = f32[2,2,16,600]{3,2,1,0:T(8,128)} custom-call(f32[1,2,2,16,600]{4,3,2,1,0:T(8,128)S(1)} %get-tuple-element.39.home_ref, f32[1,2,2,16,600]{4,3,2,1,0:T(8,128)S(1)} %collective-permute-done.2.away_ref, f32[152,128]{1,0:T(8,128)S(1)} %collective-permute-done.4.refs_0_, f32[152,128]{1,0:T(8,128)S(1)} %collective-permute-done.6.refs_1_), custom_call_target="tpu_custom_call" | custom-call | tf_op jit(solution)/shard_map/total/pallas_call | solution.py:564
  (3 shorter events, 0.0 us)
Async XLA Ops:
  19.8 12.2 %all-to-all-start.1 = ((f32[8,2,2,8,256]{4,3,2,1,0:T(8,128)}), f32[8,2,2,8,256]{4,3,2,1,0:T(8,128)S(1)}, u32[]{:S(2)}, u32[]{:S(2)}) async-start(f32[8,2,2,8,256]{4,3,2,1,0:T(8,128)} %middle.1), calls=%async_computation.1 | async-start | bytes 524288 | tf_op jit(solution)/shard_map/all_to_all | solution.py:543
  23.4 4.2 %collective-permute-start = (f32[104,128]{1,0:T(8,128)S(1)}, f32[104,128]{1,0:T(8,128)S(1)}, u32[]{:S(2)}, u32[]{:S(2)}) collective-permute-start(f32[104,128]{1,0:T(8,128)S(1)} %get-tuple-element.35.own_inner_ref), channel_id=1, source_target_pairs={{0,1},{1,0},{2,3},{3,2},{4,5},{5,4},{6,7},{7,6},{8,9},{9,8},{10,11... | collective-permute-start | bytes 159752 | tf_op jit(solution)/shard_map/ppermute | solution.py:547
  23.4 4.3 %collective-permute-start.1 = (f32[104,128]{1,0:T(8,128)S(1)}, f32[104,128]{1,0:T(8,128)S(1)}, u32[]{:S(2)}, u32[]{:S(2)}) collective-permute-start(f32[104,128]{1,0:T(8,128)S(1)} %get-tuple-element.36.own_outer_ref), channel_id=1, source_target_pairs={{1,2},{2,1},{5,6},{6,5},{9,10},{10,9},{13,14},{14,13},{17,18},{18,... | collective-permute-start | bytes 159752 | tf_op jit(solution)/shard_map/ppermute | solution.py:546
  32.4 1.6 %collective-permute-start.5 = (f32[1,152,128]{2,1,0:T(8,128)S(1)}, f32[1,152,128]{2,1,0:T(8,128)S(1)}, u32[]{:S(2)}, u32[]{:S(2)}) collective-permute-start(f32[1,152,128]{2,1,0:T(8,128)S(1)} %get-tuple-element.44), channel_id=1, source_target_pairs={{0,1},{1,0},{2,3},{3,2},{4,5},{5,4},{6,7},{7,6},{8,9},{9,8},{10,11... | collective-permute-start | bytes 233480 | tf_op jit(solution)/shard_map/ppermute | solution.py:555
  32.9 2.7 %collective-permute-start.3 = (f32[1,152,128]{2,1,0:T(8,128)S(1)}, f32[1,152,128]{2,1,0:T(8,128)S(1)}, u32[]{:S(2)}, u32[]{:S(2)}) collective-permute-start(f32[1,152,128]{2,1,0:T(8,128)S(1)} %get-tuple-element.42), channel_id=1, source_target_pairs={{0,1},{1,0},{2,3},{3,2},{4,5},{5,4},{6,7},{7,6},{8,9},{9,8},{10,11... | collective-permute-start | bytes 233480 | tf_op jit(solution)/shard_map/ppermute | solution.py:555
  34.0 2.3 %collective-permute-start.2 = (f32[1,2,2,16,600]{4,3,2,1,0:T(8,128)S(1)}, f32[1,2,2,16,600]{4,3,2,1,0:T(8,128)S(1)}, u32[]{:S(2)}, u32[]{:S(2)}) collective-permute-start(f32[1,2,2,16,600]{4,3,2,1,0:T(8,128)S(1)} %get-tuple-element.40), channel_id=1, source_target_pairs={{0,1},{1,0},{2,3},{3,2},{4,5},{5,4},{6,7},{7,6},{8,9},{9,8},{10,11... | collective-permute-start | bytes 460808 | tf_op jit(solution)/shard_map/ppermute | solution.py:562
  34.1 5.2 %collective-permute-start.6 = (f32[152,128]{1,0:T(8,128)S(1)}, f32[152,128]{1,0:T(8,128)S(1)}, u32[]{:S(2)}, u32[]{:S(2)}) collective-permute-start(f32[152,128]{1,0:T(8,128)S(1)} %add_bitcast_fusion), channel_id=1, source_target_pairs={{0,2},{1,3},{2,0},{3,1},{4,6},{5,7},{6,4},{7,5},{8,10},{9,11},{10,... | collective-permute-start | bytes 233480 | tf_op jit(solution)/shard_map/ppermute | solution.py:560
  35.6 4.9 %collective-permute-start.4 = (f32[152,128]{1,0:T(8,128)S(1)}, f32[152,128]{1,0:T(8,128)S(1)}, u32[]{:S(2)}, u32[]{:S(2)}) collective-permute-start(f32[152,128]{1,0:T(8,128)S(1)} %add_bitcast_fusion.1), channel_id=1, source_target_pairs={{0,2},{1,3},{2,0},{3,1},{4,6},{5,7},{6,4},{7,5},{8,10},{9,11},{10,... | collective-permute-start | bytes 233480 | tf_op jit(solution)/shard_map/ppermute | solution.py:560

commit v7 on v4

--- a/solution.py
+++ b/solution.py
@@ -468,11 +468,11 @@
     )(returned, *matrices)
 
 
-def total_kernel(home_ref, away_ref, *refs):
+def total_kernel(stay_ref, *refs):
     out_ref = refs[-1]
     held = out_ref.shape[1]
     for k in range(held):
-        total = home_ref[0, :, k] + away_ref[0, :, k]
+        total = stay_ref[0, :, k]
         for ref in refs[k:-1:held]:
             total += ref[:, 0]
         out_ref[:, k] = total
@@ -515,12 +515,12 @@
     share, sensors = home.shape[3:]
     return pl.pallas_call(
         total_kernel,
-        in_specs=[VMEM_SPEC] * (2 + len(arrived)),
+        in_specs=[VMEM_SPEC] * (1 + len(arrived)),
         out_specs=VMEM_SPEC,
         out_shape=jax.ShapeDtypeStruct((2, held, share, sensors), jnp.float32),
         compiler_params=grant(16),
         name="total",
-    )(home, away, *arrived)
+    )(home + away, *arrived)
 
 
 def solution(mesh):

time: 41.6 us -> 41.6 us (level)
  waiting for transfers between devices: 7.87 us -> 7.2 us
  starting transfers between devices: 7.13 us -> 7.78 us
    ppermute x2, waiting for transfers between devices: 4.48 us -> 3.81 us  [on_device(): arrived.append(lax.ppermute(leaving[k][s - 1], 'cell', pairs))]
    ppermute x2, starting transfers between devices: 2.16 us -> 2.8 us  [on_device(): arrived.append(lax.ppermute(leaving[k][s - 1], 'cell', pairs))]
    ppermute x1, starting transfers between devices: 0.08 us -> 0.56 us  [on_device(): away = lax.ppermute(away, 'cell', swap)]
    ppermute x2, starting transfers between devices: 0.63 us -> 0.15 us  [on_device(): leaving.append(home + lax.ppermute(away, 'cell', swap))]
where the time goes in v7:
time: 41.6 us; the launch traced here: 41.3 us
  blocking collectives  16 us (38%)
  Pallas kernels  10.2 us (25%)
  starting transfers between devices  7.78 us (19%)
  waiting for transfers between devices  7.2 us (17%)
    all_to_all x1, blocking collectives, on_device(): lax.all_to_all(spectrum, 'freq', split_axis=0, concat_axis=0, tiled=True)  16 us
    ppermute x2, waiting for transfers between devices, on_device(): arrived.append(lax.ppermute(leaving[k][s - 1], 'cell', pairs))  3.81 us
    all_to_all x1, starting transfers between devices, on_device(): lax.all_to_all(spectrum, 'freq', split_axis=0, concat_axis=0, tiled=True)  3.6 us
    pallas_call x1, Pallas kernels, smooth(): pl.pallas_call(smooth_kernel, in_specs=[HBM_SPEC, VMEM_SPEC], out_specs=[...  3.55 us
    all_to_all x1, waiting for transfers between devices, on_device(): lax.all_to_all(spectrum, 'freq', split_axis=0, concat_axis=0, tiled=True)  3.38 us
    pallas_call x1, Pallas kernels, adjoint(): pl.pallas_call(adjoint_kernel, in_specs=[HBM_SPEC] * 5, out_specs=[VMEM_S...  2.85 us
    ppermute x2, starting transfers between devices, on_device(): arrived.append(lax.ppermute(leaving[k][s - 1], 'cell', pairs))  2.8 us
    pallas_call x3, Pallas kernels, forward(): pl.pallas_call(functools.partial(forward_kernel, steps, chips, wanted), i...  1.24 us
  transfers between devices with their start and end apart: 8, of which 3 were waited for; matrix products, arithmetic and copies ran while one was open for 0% of the time, Pallas kernels for 13%

profile of v7, /device:TPU:0, one launch (start us, length us, event | category | flops | bytes accessed | tf_op | source)
XLA Modules:
  0.0 41.3 jit_solution(16874689321741446613)
XLA Ops:
  0.0 2.8 %adjoint.1 = (f32[8,2,2,8,256]{4,3,2,1,0:T(8,128)S(1)}, f32[104,128]{1,0:T(8,128)S(1)}, f32[104,128]{1,0:T(8,128)S(1)}, s32[8,128]{1,0:T(8,128)S(1)}, f32[8,256]{1,0:T(8,128)S(1)}) custom-call(f32[2,2,64,600]{3,2,1,0:T(8,128)} %v_hbm.1, f32[2,2,600,256]{3,2,1,0:T(8,128)} %f_hbm.2, s32[1,256]{1,0:T(1,128)} %bitcast.17, f32[8]{0:T(128)} %rates_hbm.1, s32[64]{0:T(128)} %cut_hbm.1), custom_call_target="tpu_custom_call" | custom-call | flops 471859200 | bytes 2457600 | tf_op jit(solution)/shard_map/adjoint/pallas_call | solution.py:144
  2.9 16.0 %all_to_all.10.x_ref = f32[8,2,2,8,256]{4,3,2,1,0:T(8,128)S(1)} all-to-all(f32[8,2,2,8,256]{4,3,2,1,0:T(8,128)S(1)} %get-tuple-element.25), channel_id=1, replica_groups=mesh['freq'=8,'cell'=4] {'freq'}, dimensions={0} | all-to-all | bytes 524288 | tf_op jit(solution)/shard_map/all_to_all | solution.py:489
  18.9 0.9 %middle.1 = f32[8,2,2,8,256]{4,3,2,1,0:T(8,128)} custom-call(f32[8,2,2,8,256]{4,3,2,1,0:T(8,128)S(1)} %all_to_all.10.x_ref, s32[8,128]{1,0:T(8,128)S(1)} %get-tuple-element.26.cutoff_ref), custom_call_target="tpu_custom_call" | custom-call | flops 3932160 | bytes 524288 | tf_op jit(solution)/shard_map/middle/pallas_call | solution.py:229
  19.8 3.6 %all-to-all-start.1 = ((f32[8,2,2,8,256]{4,3,2,1,0:T(8,128)}), f32[8,2,2,8,256]{4,3,2,1,0:T(8,128)S(1)}, u32[]{:S(2)}, u32[]{:S(2)}) async-start(f32[8,2,2,8,256]{4,3,2,1,0:T(8,128)} %middle.1), calls=%async_computation.1 | async-start | bytes 524288 | tf_op jit(solution)/shard_map/all_to_all | solution.py:495
  23.4 0.0 collective-permute-start
  23.4 0.7 %collective-permute-start.1 = (f32[104,128]{1,0:T(8,128)S(1)}, f32[104,128]{1,0:T(8,128)S(1)}, u32[]{:S(2)}, u32[]{:S(2)}) collective-permute-start(f32[104,128]{1,0:T(8,128)S(1)} %get-tuple-element.36.own_outer_ref), channel_id=1, source_target_pairs={{1,2},{2,1},{5,6},{6,5},{9,10},{10,9},{13,14},{14,13},{17,18},{18,... | collective-permute-start | bytes 159752 | tf_op jit(solution)/shard_map/ppermute | solution.py:498
  24.1 3.6 %smooth.1 = (bf16[2,2,256,600]{3,2,1,0:T(8,128)(2,1)S(1)}, bf16[2,2,256,600]{3,2,1,0:T(8,128)(2,1)S(1)}, f32[2,2,32,600]{3,2,1,0:T(8,128)S(1)}) custom-call(f32[2,2,600,256]{3,2,1,0:T(8,128)} %f_hbm.2, f32[8,256]{1,0:T(8,128)S(1)} %get-tuple-element.31.rates_ref), custom_call_target="tpu_custom_call" | custom-call | flops 943718400 | bytes 4915200 | tf_op jit(solution)/shard_map/smooth/pallas_call | solution.py:302
  27.6 0.0 collective-permute-done.inner_ref
  27.6 0.0 collective-permute-done.1.outer_ref
  27.6 0.9 %near_edges.1 = (bf16[2,2,32,600]{3,2,1,0:T(8,128)(2,1)S(1)}, bf16[2,2,32,600]{3,2,1,0:T(8,128)(2,1)S(1)}) custom-call(f32[2,2,32,600]{3,2,1,0:T(8,128)S(1)} %get-tuple-element.34.near_ref, f32[104,128]{1,0:T(8,128)S(1)} %get-tuple-element.35.own_inner_ref, f32[104,128]{1,0:T(8,128)S(1)} %get-tuple-element.36.own_outer_ref, ...), custom_call_target="tpu_custom_call" | custom-call | flops 58982400 | bytes 614400 | tf_op jit(solution)/shard_map/near_edges/pallas_call | solution.py:401
  28.6 3.4 %all-to-all-done.1.x_ref = f32[8,2,2,8,256]{4,3,2,1,0:T(8,128)S(1)} async-done(((f32[8,2,2,8,256]{4,3,2,1,0:T(8,128)}), f32[8,2,2,8,256]{4,3,2,1,0:T(8,128)S(1)}, u32[]{:S(2)}, u32[]{:S(2)}) %all-to-all-start.1) | async-done | bytes 262176 | tf_op jit(solution)/shard_map/all_to_all | solution.py:495
  32.0 0.3 shard_map.56
  32.3 0.1 collective-permute-start.3
  32.4 0.6 %shard_map.55 = (f32[1,2,2,16,600]{4,3,2,1,0:T(8,128)S(1)}, f32[1,2,2,16,600]{4,3,2,1,0:T(8,128)S(1)}) custom-call(f32[8,2,2,8,256]{4,3,2,1,0:T(8,128)S(1)} %all-to-all-done.1.x_ref, bf16[2,2,256,600]{3,2,1,0:T(8,128)(2,1)S(1)} %get-tuple-element.32.high_ref, bf16[2,2,256,600]{3,2,1,0:T(8,128)(2,1)S(1)} %get-tuple-element.33.low_ref, ...), custom_call_target="tpu_custom_call" | custom-call | flops 235929600 | bytes 2457600 | tf_op jit(solution)/shard_map/pallas_call | solution.py:457
  32.9 0.6 %collective-permute-start.2 = (f32[1,2,2,16,600]{4,3,2,1,0:T(8,128)S(1)}, f32[1,2,2,16,600]{4,3,2,1,0:T(8,128)S(1)}, u32[]{:S(2)}, u32[]{:S(2)}) collective-permute-start(f32[1,2,2,16,600]{4,3,2,1,0:T(8,128)S(1)} %get-tuple-element.40), channel_id=1, source_target_pairs={{0,1},{1,0},{2,3},{3,2},{4,5},{5,4},{6,7},{7,6},{8,9},{9,8},{10,11... | collective-permute-start | bytes 460808 | tf_op jit(solution)/shard_map/ppermute | solution.py:514
  33.5 0.3 shard_map.57
  33.9 0.1 collective-permute-start.5
  33.9 0.0 collective-permute-done.3
  34.0 1.6 %collective-permute-start.4 = (f32[2,1,16,600]{3,2,1,0:T(8,128)S(1)}, f32[2,1,16,600]{3,2,1,0:T(8,128)S(1)}, u32[]{:S(2)}, u32[]{:S(2)}) collective-permute-start(f32[2,1,16,600]{3,2,1,0:T(8,128)S(1)} %fusion.1), channel_id=1, source_target_pairs={{0,2},{1,3},{2,0},{3,1},{4,6},{5,7},{6,4},{7,5},{8,10},{9,11},{10,... | collective-permute-start | bytes 230408 | tf_op jit(solution)/shard_map/ppermute | solution.py:512
  35.5 0.0 collective-permute-done.5
  35.5 1.2 %collective-permute-start.6 = (f32[2,1,16,600]{3,2,1,0:T(8,128)S(1)}, f32[2,1,16,600]{3,2,1,0:T(8,128)S(1)}, u32[]{:S(2)}, u32[]{:S(2)}) collective-permute-start(f32[2,1,16,600]{3,2,1,0:T(8,128)S(1)} %fusion), channel_id=1, source_target_pairs={{0,2},{1,3},{2,0},{3,1},{4,6},{5,7},{6,4},{7,5},{8,10},{9,11},{10,... | collective-permute-start | bytes 230408 | tf_op jit(solution)/shard_map/ppermute | solution.py:512
  36.8 2.5 %collective-permute-done.4.refs_0_ = f32[2,1,16,600]{3,2,1,0:T(8,128)S(1)} collective-permute-done((f32[2,1,16,600]{3,2,1,0:T(8,128)S(1)}, f32[2,1,16,600]{3,2,1,0:T(8,128)S(1)}, u32[]{:S(2)}, u32[]{:S(2)}) %collective-permute-start.4) | collective-permute-done | bytes 76832 | tf_op jit(solution)/shard_map/ppermute | solution.py:512
  39.3 1.3 %collective-permute-done.6.refs_1_ = f32[2,1,16,600]{3,2,1,0:T(8,128)S(1)} collective-permute-done((f32[2,1,16,600]{3,2,1,0:T(8,128)S(1)}, f32[2,1,16,600]{3,2,1,0:T(8,128)S(1)}, u32[]{:S(2)}, u32[]{:S(2)}) %collective-permute-start.6) | collective-permute-done | bytes 76832 | tf_op jit(solution)/shard_map/ppermute | solution.py:512
  40.6 0.7 %total.1 = f32[2,2,16,600]{3,2,1,0:T(8,128)} custom-call(f32[1,2,2,16,600]{4,3,2,1,0:T(8,128)S(1)} %add.9.stay_ref, f32[2,1,16,600]{3,2,1,0:T(8,128)S(1)} %collective-permute-done.4.refs_0_, f32[2,1,16,600]{3,2,1,0:T(8,128)S(1)} %collective-permute-done.6.refs_1_), custom_call_target="tpu_custom_call" | custom-call | tf_op jit(solution)/shard_map/total/pallas_call | solution.py:516
  (4 shorter events, 0.0 us)
Async XLA Ops:
  19.8 12.2 %all-to-all-start.1 = ((f32[8,2,2,8,256]{4,3,2,1,0:T(8,128)}), f32[8,2,2,8,256]{4,3,2,1,0:T(8,128)S(1)}, u32[]{:S(2)}, u32[]{:S(2)}) async-start(f32[8,2,2,8,256]{4,3,2,1,0:T(8,128)} %middle.1), calls=%async_computation.1 | async-start | bytes 524288 | tf_op jit(solution)/shard_map/all_to_all | solution.py:495
  23.4 4.2 %collective-permute-start = (f32[104,128]{1,0:T(8,128)S(1)}, f32[104,128]{1,0:T(8,128)S(1)}, u32[]{:S(2)}, u32[]{:S(2)}) collective-permute-start(f32[104,128]{1,0:T(8,128)S(1)} %get-tuple-element.35.own_inner_ref), channel_id=1, source_target_pairs={{0,1},{1,0},{2,3},{3,2},{4,5},{5,4},{6,7},{7,6},{8,9},{9,8},{10,11... | collective-permute-start | bytes 159752 | tf_op jit(solution)/shard_map/ppermute | solution.py:499
  23.4 4.2 %collective-permute-start.1 = (f32[104,128]{1,0:T(8,128)S(1)}, f32[104,128]{1,0:T(8,128)S(1)}, u32[]{:S(2)}, u32[]{:S(2)}) collective-permute-start(f32[104,128]{1,0:T(8,128)S(1)} %get-tuple-element.36.own_outer_ref), channel_id=1, source_target_pairs={{1,2},{2,1},{5,6},{6,5},{9,10},{10,9},{13,14},{14,13},{17,18},{18,... | collective-permute-start | bytes 159752 | tf_op jit(solution)/shard_map/ppermute | solution.py:498
  32.3 1.6 %collective-permute-start.3 = (f32[1,2,1,16,600]{4,3,1,2,0:T(8,128)S(1)}, f32[1,2,1,16,600]{4,3,1,2,0:T(8,128)S(1)}, u32[]{:S(2)}, u32[]{:S(2)}) collective-permute-start(f32[1,2,1,16,600]{4,3,1,2,0:T(8,128)S(1)} %bitcast.15), channel_id=1, source_target_pairs={{0,1},{1,0},{2,3},{3,2},{4,5},{5,4},{6,7},{7,6},{8,9},{9,8},{10,11... | collective-permute-start | bytes 230408 | tf_op jit(solution)/shard_map/ppermute | solution.py:507
  32.9 3.8 %collective-permute-start.2 = (f32[1,2,2,16,600]{4,3,2,1,0:T(8,128)S(1)}, f32[1,2,2,16,600]{4,3,2,1,0:T(8,128)S(1)}, u32[]{:S(2)}, u32[]{:S(2)}) collective-permute-start(f32[1,2,2,16,600]{4,3,2,1,0:T(8,128)S(1)} %get-tuple-element.40), channel_id=1, source_target_pairs={{0,1},{1,0},{2,3},{3,2},{4,5},{5,4},{6,7},{7,6},{8,9},{9,8},{10,11... | collective-permute-start | bytes 460808 | tf_op jit(solution)/shard_map/ppermute | solution.py:514
  33.9 1.7 %collective-permute-start.5 = (f32[1,2,1,16,600]{4,3,1,2,0:T(8,128)S(1)}, f32[1,2,1,16,600]{4,3,1,2,0:T(8,128)S(1)}, u32[]{:S(2)}, u32[]{:S(2)}) collective-permute-start(f32[1,2,1,16,600]{4,3,1,2,0:T(8,128)S(1)} %bitcast.16), channel_id=1, source_target_pairs={{0,1},{1,0},{2,3},{3,2},{4,5},{5,4},{6,7},{7,6},{8,9},{9,8},{10,11... | collective-permute-start | bytes 230408 | tf_op jit(solution)/shard_map/ppermute | solution.py:507
  34.0 5.3 %collective-permute-start.4 = (f32[2,1,16,600]{3,2,1,0:T(8,128)S(1)}, f32[2,1,16,600]{3,2,1,0:T(8,128)S(1)}, u32[]{:S(2)}, u32[]{:S(2)}) collective-permute-start(f32[2,1,16,600]{3,2,1,0:T(8,128)S(1)} %fusion.1), channel_id=1, source_target_pairs={{0,2},{1,3},{2,0},{3,1},{4,6},{5,7},{6,4},{7,5},{8,10},{9,11},{10,... | collective-permute-start | bytes 230408 | tf_op jit(solution)/shard_map/ppermute | solution.py:512
  35.5 5.1 %collective-permute-start.6 = (f32[2,1,16,600]{3,2,1,0:T(8,128)S(1)}, f32[2,1,16,600]{3,2,1,0:T(8,128)S(1)}, u32[]{:S(2)}, u32[]{:S(2)}) collective-permute-start(f32[2,1,16,600]{3,2,1,0:T(8,128)S(1)} %fusion), channel_id=1, source_target_pairs={{0,2},{1,3},{2,0},{3,1},{4,6},{5,7},{6,4},{7,5},{8,10},{9,11},{10,... | collective-permute-start | bytes 230408 | tf_op jit(solution)/shard_map/ppermute | solution.py:512
